TPU v7x, 32 devices: a whole 2x2x4 slice. The times are simulated.
32 devices in a mesh: row: 16 (over z, y, x), col: 2 (over core).
Axes of the slice: x: 2, y: 2, z: 4, core: 2. Of those that a mesh axis runs over, the one named last changes fastest.
Arguments:
- sources: bfloat16 [32768, 640], P(('row', 'col')), may hold values from -6 to 6
- tree_perm: int32 [32768], P(('row', 'col')), may hold values from 0 to 32767, as said below
- leaf_blocks: bfloat16 [32768, 512], P(('row', 'col')), may hold values from -0.25 to 0.25
- u_factors: bfloat16 [6, 32, 32768], P(None, None, ('row', 'col')), may hold values from -0.4375 to 0.4375
- v_factors: bfloat16 [6, 32, 32768], P(None, None, ('row', 'col')), as said below
- level_ranks: int32 [6], replicated, may hold values from 16 to 32
Outputs:
- products: bfloat16 [32768, 640], P(('row', 'col'))
Inputs may be any that keep to these rules, and one draw needn't show every extreme that they name: tree_perm is a permutation that maps each aligned block of 1024 positions onto the same block of initial indices. `v_factors`: entries of level l are of the order of the inverse square root of 32768 / 2^l.
All inputs are finite; a program needn't handle non-finite values.
Results may differ from a plain program's by a relative error of at most 0.0037.
Values sent between devices are 32-bit elements; how exact they have to be, the bound alone decides.
No kernel may reach another device: no remote copies, remote signals or barrier semaphores. Data moves between devices by JAX's collectives and lax.ppermute only.
A program may use at most 64 MiB of HBM per device.

v0:
```python
import jax
import jax.numpy as jnp
from jax import lax
from jax.sharding import PartitionSpec as P


def partner(x, axis, distance):
    return lax.ppermute(x, axis, [(i, i ^ 1 << distance) for i in range(lax.axis_size(axis))])


def per_device(sources, tree_perm, leaf_blocks, u_factors, v_factors, level_ranks):
    row_count, rhs_count = sources.shape
    leaf_size = leaf_blocks.shape[1]
    level_count, rank_cap, _ = u_factors.shape
    col_size = lax.axis_size("col")
    col_bits = col_size.bit_length() - 1
    row_bits = lax.axis_size("row").bit_length() - 1
    dev_bits = row_bits + col_bits
    first_row = (lax.axis_index("row") * col_size + lax.axis_index("col")) * row_count
    local_index = tree_perm - first_row
    ordered = sources[local_index]
    rank_mask = (lax.iota(jnp.int32, rank_cap)[None, :] < level_ranks[:, None]).astype(jnp.float32)
    partial_coef = jnp.einsum(
        "lkn,nr->lkr", v_factors[:dev_bits], ordered, preferred_element_type=jnp.float32
    )
    siblings = [None] * dev_bits
    running = partial_coef
    for bit_pos in range(col_bits):
        finish = dev_bits - 1 - bit_pos
        received = partner(running, "col", bit_pos)
        siblings[finish] = received[finish]
        running = running[:finish] + received[:finish]
    share_width = rhs_count // col_size
    running = lax.dynamic_slice_in_dim(running, lax.axis_index("col") * share_width, share_width, 2)
    coarse = [None] * row_bits
    for level in range(row_bits):
        level_sum = running[level]
        for bit_pos in range(row_bits - 1 - level):
            level_sum = level_sum + partner(level_sum, "row", bit_pos)
        coarse[level] = partner(level_sum, "row", row_bits - 1 - level)
    coarse_stack = jnp.stack(coarse)
    coarse_stack = lax.all_gather(coarse_stack, "col", axis=2, tiled=True)
    far_coef = (
        jnp.concatenate([coarse_stack, jnp.stack(siblings[row_bits:])], axis=0)
        * rank_mask[:dev_bits, :, None]
    ).astype(jnp.bfloat16)
    leaf_count = row_count // leaf_size
    result = jnp.einsum(
        "gij,gjr->gir",
        leaf_blocks.reshape(leaf_count, leaf_size, leaf_size),
        ordered.reshape(leaf_count, leaf_size, rhs_count),
        preferred_element_type=jnp.float32,
    ).reshape(row_count, rhs_count)
    result = result + jnp.einsum(
        "lkn,lkr->nr", u_factors[:dev_bits], far_coef, preferred_element_type=jnp.float32
    )
    for level in range(dev_bits, level_count):
        cluster_rows = row_count >> level - dev_bits + 1
        groups = row_count // cluster_rows
        near_coef = jnp.einsum(
            "kgs,gsr->gkr",
            v_factors[level].reshape(rank_cap, groups, cluster_rows),
            ordered.reshape(groups, cluster_rows, rhs_count),
            preferred_element_type=jnp.float32,
        )
        near_coef = near_coef.reshape(groups // 2, 2, rank_cap, rhs_count)[:, ::-1].reshape(
            groups, rank_cap, rhs_count
        )
        near_coef = (near_coef * rank_mask[level][None, :, None]).astype(jnp.bfloat16)
        result = result + jnp.einsum(
            "kgs,gkr->gsr",
            u_factors[level].reshape(rank_cap, groups, cluster_rows),
            near_coef,
            preferred_element_type=jnp.float32,
        ).reshape(row_count, rhs_count)
    return jnp.zeros_like(sources).at[local_index].set(result.astype(jnp.bfloat16))


def solution(mesh):
    placed = (
        P(("row", "col"), None),
        P(("row", "col")),
        P(("row", "col"), None),
        P(None, None, ("row", "col")),
        P(None, None, ("row", "col")),
        P(),
    )
    return jax.shard_map(
        per_device, mesh=mesh, in_specs=placed, out_specs=P(("row", "col"), None), check_vma=False
    )
```

profile of v0, /device:TPU:0, one launch (start us, length us, event | category | flops | bytes accessed | tf_op | source)
XLA Modules:
  0.0 56.9 jit_solution(1084728093172403832)
XLA Ops:
  0.0 0.8 %broadcast_clamp_fusion = (s32[1024]{0:T(1024)S(1)}, s32[1024]{0:T(1024)S(1)}) fusion(s32[1024]{0:T(1024)} %param.7, s32[]{:T(128)S(6)} %mul.28), kind=kLoop, calls=%fused_computation.29 | loop fusion | flops 5120 | bytes 12292 | tf_op jit(solution)/shard_map/gather | solution.py:21
  0.8 0.5 copy-done
  1.3 4.0 %gather_fusion = bf16[1024,640]{1,0:T(8,128)(2,1)S(1)} fusion(bf16[1024,640]{1,0:T(8,128)(2,1)S(1)} %copy-done, s32[1024]{0:T(1024)S(1)} %get-tuple-element.5), kind=kCustom, calls=%fused_computation | custom fusion | bytes 2625536 | tf_op jit(solution)/shard_map/gather | solution.py:21
  5.4 1.2 %fusion.4 = f32[5,32,640]{2,1,0:T(8,128)} fusion(bf16[1024,640]{1,0:T(8,128)(2,1)S(1)} %gather_fusion, bf16[6,32,1024]{2,1,0:T(8,128)(2,1)S(1)} %copy-done.3), kind=kOutput, calls=%fused_computation.7 | convolution fusion | flops 209715200 | bytes 2048000 | tf_op jit(solution)/shard_map/lkn,nr->lkr/dot_general | solution.py:23
  7.1 0.8 %slice.49 = bf16[1,32,1024]{2,1,0:T(8,128)(2,1)S(1)} slice(bf16[6,32,1024]{2,1,0:T(8,128)(2,1)} %param.10), slice={[5:6], [0:32], [0:1024]} | slice | bytes 131072 | tf_op jit(solution)/shard_map/slice | solution.py:62
  8.3 1.0 %slice.54 = f32[4,32,640]{2,1,0:T(8,128)S(1)} slice(f32[5,32,640]{2,1,0:T(8,128)} %fusion.4), slice={[0:4], [0:32], [0:640]} | slice | bytes 655360 | tf_op jit(solution)/shard_map/slice | solution.py:32
  9.3 3.7 %fusion.22 = f32[2,640,512]{1,2,0:T(8,128)} fusion(bf16[2,512,512]{2,1,0:T(8,128)(2,1)} %bitcast.55, bf16[2,512,640]{2,1,0:T(8,128)(2,1)S(1)} %bitcast.52), kind=kOutput, calls=%fused_computation.35 | convolution fusion | flops 671088640 | bytes 4980736 | tf_op jit(solution)/shard_map/gij,gjr->gir/dot_general | solution.py:48
  13.2 2.5 %collective-permute-start.1 = (f32[32,320]{1,0:T(8,128)S(1)}, f32[32,320]{1,0:T(8,128)S(1)}, u32[]{:S(2)}, u32[]{:S(2)}) collective-permute-start(f32[32,320]{1,0:T(8,128)S(1)} %get-tuple-element.10), channel_id=1, source_target_pairs={{0,2},{2,0},{4,6},{6,4},{8,10},{10,8},{12,14},{14,12},{16,18},{18,... | collective-permute-start | bytes 122888 | tf_op jit(solution)/shard_map/ppermute | solution.py:8
  15.9 1.9 %collective-permute-start.5 = (f32[32,320]{1,0:T(8,128)S(1)}, f32[32,320]{1,0:T(8,128)S(1)}, u32[]{:S(2)}, u32[]{:S(2)}) collective-permute-start(f32[32,320]{1,0:T(8,128)S(1)} %get-tuple-element.12), channel_id=1, source_target_pairs={{0,2},{2,0},{4,6},{6,4},{8,10},{10,8},{12,14},{14,12},{16,18},{18,... | collective-permute-start | bytes 122888 | tf_op jit(solution)/shard_map/ppermute | solution.py:8
  18.2 2.0 %collective-permute-done.8 = f32[32,320]{1,0:T(8,128)S(1)} collective-permute-done((f32[32,320]{1,0:T(8,128)S(1)}, f32[32,320]{1,0:T(8,128)S(1)}, u32[]{:S(2)}, u32[]{:S(2)}) %collective-permute-start.8) | collective-permute-done | bytes 40992 | tf_op jit(solution)/shard_map/ppermute | solution.py:8
  20.2 0.5 collective-permute-done.5
  20.7 1.6 %collective-permute-start.2 = (f32[32,320]{1,0:T(8,128)S(1)}, f32[32,320]{1,0:T(8,128)S(1)}, u32[]{:S(2)}, u32[]{:S(2)}) collective-permute-start(f32[32,320]{1,0:T(8,128)S(1)} %get-tuple-element.7), channel_id=1, source_target_pairs={{0,4},{2,6},{4,0},{6,2},{8,12},{10,14},{12,8},{14,10},{16,20},{18,... | collective-permute-start | bytes 122888 | tf_op jit(solution)/shard_map/ppermute | solution.py:8
  22.8 2.2 %collective-permute-done.2 = f32[32,320]{1,0:T(8,128)S(1)} collective-permute-done((f32[32,320]{1,0:T(8,128)S(1)}, f32[32,320]{1,0:T(8,128)S(1)}, u32[]{:S(2)}, u32[]{:S(2)}) %collective-permute-start.2) | collective-permute-done | bytes 40992 | tf_op jit(solution)/shard_map/ppermute | solution.py:8
  25.1 1.6 %collective-permute-start.3 = (f32[32,320]{1,0:T(8,128)S(1)}, f32[32,320]{1,0:T(8,128)S(1)}, u32[]{:S(2)}, u32[]{:S(2)}) collective-permute-start(f32[32,320]{1,0:T(8,128)S(1)} %add.42), channel_id=1, source_target_pairs={{0,8},{2,10},{4,12},{6,14},{8,0},{10,2},{12,4},{14,6},{16,24},{18,... | collective-permute-start | bytes 122888 | tf_op jit(solution)/shard_map/ppermute | solution.py:8
  26.9 1.7 %collective-permute-start.10 = (f32[32,320]{1,0:T(8,128)S(1)}, f32[32,320]{1,0:T(8,128)S(1)}, u32[]{:S(2)}, u32[]{:S(2)}) collective-permute-start(f32[32,320]{1,0:T(8,128)S(1)} %get-tuple-element.13), channel_id=1, source_target_pairs={{0,2},{2,0},{4,6},{6,4},{8,10},{10,8},{12,14},{14,12},{16,18},{18,... | collective-permute-start | bytes 122888 | tf_op jit(solution)/shard_map/ppermute | solution.py:8
  28.5 1.1 %collective-permute-start.9 = (f32[32,320]{1,0:T(8,128)S(1)}, f32[32,320]{1,0:T(8,128)S(1)}, u32[]{:S(2)}, u32[]{:S(2)}) collective-permute-start(f32[32,320]{1,0:T(8,128)S(1)} %get-tuple-element.8), channel_id=1, source_target_pairs={{0,4},{2,6},{4,0},{6,2},{8,12},{10,14},{12,8},{14,10},{16,20},{18,... | collective-permute-start | bytes 122888 | tf_op jit(solution)/shard_map/ppermute | solution.py:8
  30.1 2.7 %collective-permute-start.4 = (f32[32,320]{1,0:T(8,128)S(1)}, f32[32,320]{1,0:T(8,128)S(1)}, u32[]{:S(2)}, u32[]{:S(2)}) collective-permute-start(f32[32,320]{1,0:T(8,128)S(1)} %add.43), channel_id=1, source_target_pairs={{0,16},{2,18},{4,20},{6,22},{8,24},{10,26},{12,28},{14,30},{16,0},... | collective-permute-start | bytes 122888 | tf_op jit(solution)/shard_map/ppermute | solution.py:8
  32.8 2.0 %fusion.14 = f32[2,640,512]{1,2,0:T(8,128)} fusion(bf16[2,32,640]{2,1,0:T(8,128)(2,1)S(1)} %multiply_convert_fusion, bf16[32,2,512]{2,1,0:T(2,128)(2,1)S(1)} %reshape_squeeze.7), kind=kOutput, calls=%fused_computation.19 | convolution fusion | flops 41943040 | bytes 2768896 | tf_op jit(solution)/shard_map/kgs,gkr->gsr/dot_general | solution.py:70
  34.8 3.3 %copy.35 = f32[1024,640]{0,1:T(8,128)} copy(f32[1024,640]{1,0:T(8,128)} %bitcast.54) | data formatting | bytes 5242880 | tf_op jit(solution)/shard_map/reshape | solution.py:75
  38.1 3.3 %copy.30 = f32[1024,640]{0,1:T(8,128)} copy(f32[1024,640]{1,0:T(8,128)} %bitcast.53) | data formatting | bytes 5242880 | tf_op jit(solution)/shard_map/reshape | solution.py:53
  41.7 2.7 %all_gather.3 = f32[4,32,640]{1,0,2:T(4,128)S(1)} all-gather(f32[4,32,320]{1,0,2:T(4,128)S(1)} %copy.28), channel_id=1, replica_groups=mesh['row'=16,'col'=2] {'col'}, dimensions={2}, use_global_device_ids=true | all-gather | bytes 491520 | tf_op jit(solution)/shard_map/all_gather | solution.py:42
  45.5 3.1 %fusion.1 = bf16[1024,640]{0,1:T(8,128)(2,1)S(1)} fusion(f32[1024,640]{0,1:T(8,128)} %copy.35, f32[1024,640]{0,1:T(8,128)} %copy.30, bf16[6,32,1024]{2,1,0:T(8,128)(2,1)S(1)} %copy-done.2, f32[1,32,640]{2,1,0:T(8,128)S(1)} %slice-done, f32[4,32,640]{2,1,0:T(8,128)S(1)} %copy.29, f32[5,32]{1,0:T(8,128)S(1)} %bitcast.60), kind=kOutput, calls=%fused_computation.4 | convolution fusion | flops 211988480 | bytes 7294976 | tf_op jit(solution)/shard_map/lkn,lkr->nr/dot_general | solution.py:54
  48.6 1.5 %copy.34 = bf16[1024,640]{1,0:T(8,128)(2,1)} copy(bf16[1024,640]{0,1:T(8,128)(2,1)S(1)} %fusion.1) | data formatting | bytes 2621440 | tf_op jit(solution)/shard_map/convert_element_type | solution.py:76
  50.1 6.8 %scatter_custom_fusion = bf16[1024,640]{1,0:T(8,128)(2,1)} fusion(s32[1024]{0:T(1024)S(1)} %get-tuple-element.6, bf16[1024,640]{1,0:T(8,128)(2,1)} %copy.34, bf16[]{:T(256)} %constant.8.clone.1), kind=kCustom, calls=%fused_computation.9 | custom fusion | bytes 1311232 | tf_op jit(solution)/shard_map/scatter | solution.py:76
  (41 shorter events, 4.1 us)
Async XLA Ops:
  0.0 1.3 %copy-start = (bf16[1024,640]{1,0:T(8,128)(2,1)S(1)}, bf16[1024,640]{1,0:T(8,128)(2,1)}, u32[]{:S(2)}) copy-start(bf16[1024,640]{1,0:T(8,128)(2,1)} %param.6) | copy-start | bytes 3932164
  1.3 4.0 %copy-start.3 = (bf16[6,32,1024]{2,1,0:T(8,128)(2,1)S(1)}, bf16[6,32,1024]{2,1,0:T(8,128)(2,1)}, u32[]{:S(2)}) copy-start(bf16[6,32,1024]{2,1,0:T(8,128)(2,1)} %param.10) | copy-start | bytes 1179652
  6.6 6.4 %collective-permute-start = (f32[5,32,640]{2,1,0:T(8,128)}, f32[5,32,640]{2,1,0:T(8,128)S(1)}, u32[]{:S(2)}, u32[]{:S(2)}) collective-permute-start(f32[5,32,640]{2,1,0:T(8,128)} %fusion.4), channel_id=1, source_target_pairs={{0,1},{1,0},{2,3},{3,2},{4,5},{5,4},{6,7},{7,6},{8,9},{9,8},{10,11... | collective-permute-start | bytes 1228808 | tf_op jit(solution)/shard_map/ppermute | solution.py:8
  13.0 4.8 %copy-start.4 = (s32[6]{0:T(128)S(1)}, s32[6]{0:T(128)}, u32[]{:S(2)}) copy-start(s32[6]{0:T(128)} %param.11) | copy-start | bytes 76
  13.0 13.8 %slice-start.1 = ((bf16[6,32,1024]{2,1,0:T(8,128)(2,1)}), bf16[1,32,1024]{2,1,0:T(8,128)(2,1)S(1)}, s32[]{:S(2)}) async-start(bf16[6,32,1024]{2,1,0:T(8,128)(2,1)} %param.9), calls=%async_computation.1 | async-start | bytes 131072 | tf_op jit(solution)/shard_map/slice | solution.py:72
  13.0 28.4 %copy-start.1 = (f32[5,32,640]{2,1,0:T(8,128)}, f32[5,32,640]{2,1,0:T(8,128)S(1)}, u32[]{:S(2)}) copy-start(f32[5,32,640]{2,1,0:T(8,128)S(1)} %collective-permute-done) | copy-start | bytes 1228804
  13.2 5.0 %collective-permute-start.1 = (f32[32,320]{1,0:T(8,128)S(1)}, f32[32,320]{1,0:T(8,128)S(1)}, u32[]{:S(2)}, u32[]{:S(2)}) collective-permute-start(f32[32,320]{1,0:T(8,128)S(1)} %get-tuple-element.10), channel_id=1, source_target_pairs={{0,2},{2,0},{4,6},{6,4},{8,10},{10,8},{12,14},{14,12},{16,18},{18,... | collective-permute-start | bytes 122888 | tf_op jit(solution)/shard_map/ppermute | solution.py:8
  15.8 4.4 %collective-permute-start.8 = (f32[32,320]{1,0:T(8,128)S(1)}, f32[32,320]{1,0:T(8,128)S(1)}, u32[]{:S(2)}, u32[]{:S(2)}) collective-permute-start(f32[32,320]{1,0:T(8,128)S(1)} %get-tuple-element.11), channel_id=1, source_target_pairs={{0,2},{2,0},{4,6},{6,4},{8,10},{10,8},{12,14},{14,12},{16,18},{18,... | collective-permute-start | bytes 122888 | tf_op jit(solution)/shard_map/ppermute | solution.py:8
  15.9 4.8 %collective-permute-start.5 = (f32[32,320]{1,0:T(8,128)S(1)}, f32[32,320]{1,0:T(8,128)S(1)}, u32[]{:S(2)}, u32[]{:S(2)}) collective-permute-start(f32[32,320]{1,0:T(8,128)S(1)} %get-tuple-element.12), channel_id=1, source_target_pairs={{0,2},{2,0},{4,6},{6,4},{8,10},{10,8},{12,14},{14,12},{16,18},{18,... | collective-permute-start | bytes 122888 | tf_op jit(solution)/shard_map/ppermute | solution.py:8
  20.7 4.3 %collective-permute-start.2 = (f32[32,320]{1,0:T(8,128)S(1)}, f32[32,320]{1,0:T(8,128)S(1)}, u32[]{:S(2)}, u32[]{:S(2)}) collective-permute-start(f32[32,320]{1,0:T(8,128)S(1)} %get-tuple-element.7), channel_id=1, source_target_pairs={{0,4},{2,6},{4,0},{6,2},{8,12},{10,14},{12,8},{14,10},{16,20},{18,... | collective-permute-start | bytes 122888 | tf_op jit(solution)/shard_map/ppermute | solution.py:8
  22.3 7.3 %collective-permute-start.6 = (f32[32,320]{1,0:T(8,128)S(1)}, f32[32,320]{1,0:T(8,128)S(1)}, u32[]{:S(2)}, u32[]{:S(2)}) collective-permute-start(f32[32,320]{1,0:T(8,128)S(1)} %get-tuple-element.9), channel_id=1, source_target_pairs={{0,4},{2,6},{4,0},{6,2},{8,12},{10,14},{12,8},{14,10},{16,20},{18,... | collective-permute-start | bytes 122888 | tf_op jit(solution)/shard_map/ppermute | solution.py:8
  25.1 5.1 %collective-permute-start.3 = (f32[32,320]{1,0:T(8,128)S(1)}, f32[32,320]{1,0:T(8,128)S(1)}, u32[]{:S(2)}, u32[]{:S(2)}) collective-permute-start(f32[32,320]{1,0:T(8,128)S(1)} %add.42), channel_id=1, source_target_pairs={{0,8},{2,10},{4,12},{6,14},{8,0},{10,2},{12,4},{14,6},{16,24},{18,... | collective-permute-start | bytes 122888 | tf_op jit(solution)/shard_map/ppermute | solution.py:8
  26.9 14.5 %collective-permute-start.10 = (f32[32,320]{1,0:T(8,128)S(1)}, f32[32,320]{1,0:T(8,128)S(1)}, u32[]{:S(2)}, u32[]{:S(2)}) collective-permute-start(f32[32,320]{1,0:T(8,128)S(1)} %get-tuple-element.13), channel_id=1, source_target_pairs={{0,2},{2,0},{4,6},{6,4},{8,10},{10,8},{12,14},{14,12},{16,18},{18,... | collective-permute-start | bytes 122888 | tf_op jit(solution)/shard_map/ppermute | solution.py:8
  28.5 12.8 %collective-permute-start.9 = (f32[32,320]{1,0:T(8,128)S(1)}, f32[32,320]{1,0:T(8,128)S(1)}, u32[]{:S(2)}, u32[]{:S(2)}) collective-permute-start(f32[32,320]{1,0:T(8,128)S(1)} %get-tuple-element.8), channel_id=1, source_target_pairs={{0,4},{2,6},{4,0},{6,2},{8,12},{10,14},{12,8},{14,10},{16,20},{18,... | collective-permute-start | bytes 122888 | tf_op jit(solution)/shard_map/ppermute | solution.py:8
  29.6 11.8 %collective-permute-start.7 = (f32[32,320]{1,0:T(8,128)S(1)}, f32[32,320]{1,0:T(8,128)S(1)}, u32[]{:S(2)}, u32[]{:S(2)}) collective-permute-start(f32[32,320]{1,0:T(8,128)S(1)} %add.45), channel_id=1, source_target_pairs={{0,8},{2,10},{4,12},{6,14},{8,0},{10,2},{12,4},{14,6},{16,24},{18,... | collective-permute-start | bytes 122888 | tf_op jit(solution)/shard_map/ppermute | solution.py:8
  30.1 11.2 %collective-permute-start.4 = (f32[32,320]{1,0:T(8,128)S(1)}, f32[32,320]{1,0:T(8,128)S(1)}, u32[]{:S(2)}, u32[]{:S(2)}) collective-permute-start(f32[32,320]{1,0:T(8,128)S(1)} %add.43), channel_id=1, source_target_pairs={{0,16},{2,18},{4,20},{6,22},{8,24},{10,26},{12,28},{14,30},{16,0},... | collective-permute-start | bytes 122888 | tf_op jit(solution)/shard_map/ppermute | solution.py:8
  44.4 0.9 %slice-start = ((f32[5,32,640]{2,1,0:T(8,128)}), f32[1,32,640]{2,1,0:T(8,128)S(1)}, s32[]{:S(2)}) async-start(f32[5,32,640]{2,1,0:T(8,128)} %copy-done.1), calls=%async_computation | async-start | bytes 163840 | tf_op jit(solution)/shard_map/slice | solution.py:31
  44.4 1.0 %copy-start.2 = (bf16[6,32,1024]{2,1,0:T(8,128)(2,1)S(1)}, bf16[6,32,1024]{2,1,0:T(8,128)(2,1)}, u32[]{:S(2)}) copy-start(bf16[6,32,1024]{2,1,0:T(8,128)(2,1)} %param.9) | copy-start | bytes 1179652
where the time goes:
time: 57.3 us; the launch traced here: 56.9 us
  local copies, waits for them, and re-layouts  22.6 us (39%)
  starting transfers between devices  14.7 us (26%)
  matrix products  10.4 us (18%)
  waiting for transfers between devices  5.07 us (9%)
  blocking collectives  2.74 us (5%)
  other arithmetic  1.2 us (2%)
    ppermute x11, starting transfers between devices, partner(): lax.ppermute(x, axis, [(i, i ^ 1 << distance) for i in range(lax.axis_siz...  14.7 us
    scatter x1, local copies, waits for them, and re-layouts, per_device(): jnp.zeros_like(sources).at[local_index].set(result.astype(jnp.bfloat16))  6.79 us
    ppermute x11, waiting for transfers between devices, partner(): lax.ppermute(x, axis, [(i, i ^ 1 << distance) for i in range(lax.axis_siz...  5.07 us
    gather x1, local copies, waits for them, and re-layouts, per_device(): ordered = sources[local_index]  4.02 us
    dot_general x1, matrix products, per_device(): jnp.einsum('gij,gjr->gir', leaf_blocks.reshape(leaf_count, leaf_size, lea...  3.71 us
    reshape x1, local copies, waits for them, and re-layouts, per_device(): result = result + jnp.einsum('kgs,gkr->gsr', u_factors[level].reshape(ran...  3.28 us
    reshape x1, local copies, waits for them, and re-layouts, per_device(): result = jnp.einsum('gij,gjr->gir', leaf_blocks.reshape(leaf_count, leaf_...  3.25 us
    dot_general x1, matrix products, per_device(): jnp.einsum('lkn,lkr->nr', u_factors[:dev_bits], far_coef, preferred_eleme...  3.14 us
  transfers between devices with their start and end apart: 11, of which 4 were waited for; matrix products, arithmetic and copies ran while one was open for 26% of the time, Pallas kernels for 0%

commit v1 on v0

v1 whole, which is shorter than its diff:
```python
import functools

import jax
import jax.numpy as jnp
from jax import lax
from jax.experimental import pallas as pl
from jax.experimental.pallas import tpu as pltpu
from jax.sharding import PartitionSpec as P

AXES = ("row", "col")
BF16, F32 = jnp.bfloat16, jnp.float32


def partner(x, bit):
    count = lax.axis_size("row") * lax.axis_size("col")
    return lax.ppermute(x, AXES, [(i, i ^ 1 << bit) for i in range(count)])


def local_positions(perm_ref, row_count):
    return lax.rem(perm_ref[...], row_count)


def fill_select(select_ref, index):
    blocks, width = index.shape
    columns = index.T
    lane = lax.broadcasted_iota(jnp.int32, (width, blocks * width), 1)
    for block in range(blocks):
        hit = lane == columns[:, block : block + 1]
        select_ref[block * width : (block + 1) * width, :] = jnp.where(hit, 1.0, 0.0).astype(BF16)


def fill_select_t(select_ref, index):
    blocks, width = index.shape
    sublane = lax.broadcasted_iota(jnp.int32, (blocks * width, width), 0)
    for block in range(blocks):
        hit = sublane == index[block : block + 1, :]
        select_ref[:, block * width : (block + 1) * width] = jnp.where(hit, 1.0, 0.0).astype(BF16)


def dot(a, b):
    return jnp.dot(a, b, preferred_element_type=F32)


def dot_t(a, b):
    return lax.dot_general(a, b, (((1,), (1,)), ((), ())), preferred_element_type=F32)


def coef_kernel(dev_bits, ranks_ref, perm_ref, v_ref, sources_ref, send_ref, keep_ref,
                select, v_rows, sources, sem):
    copy = pltpu.make_async_copy(sources_ref, sources, sem)
    copy.start()
    rank_cap, row_count = v_ref.shape[1:]
    half = rank_cap // 2
    coarse = (dev_bits - 1) * half
    core = lax.rem(lax.axis_index("col"), 2)
    fill_select(select, local_positions(perm_ref, row_count))
    iota = lax.broadcasted_iota(jnp.int32, (half, 1), 0)

    def masked(level, start):
        rows = v_ref[level, pl.ds(pl.multiple_of(start, half), half), :]
        keep = iota + start < ranks_ref[level]
        return jnp.where(keep, rows.astype(F32), 0.0).astype(BF16)

    for level in range(dev_bits - 1):
        v_rows[level * half : (level + 1) * half, :] = masked(level, (1 - core) * half)
        at = coarse + rank_cap + level * half
        v_rows[at : at + half, :] = masked(level, core * half)
    for part in range(2):
        at = coarse + part * half
        v_rows[at : at + half, :] = masked(dev_bits - 1, jnp.int32(part * half))
    v_local = dot(v_rows[...], select[...]).astype(BF16)
    copy.wait()
    coef = dot(v_local, sources[...])
    send_ref[...] = coef[: coarse + rank_cap]
    keep_ref[...] = coef[coarse + rank_cap :]


def order_kernel(perm_ref, sources_ref, ordered_ref, select):
    row_count = sources_ref.shape[0]
    fill_select(select, local_positions(perm_ref, row_count))
    ordered_ref[...] = dot(select[...], sources_ref[...]).astype(BF16)


def near_kernel(dev_bits, ranks_ref, perm_ref, leaf_ref, u_ref, v_ref, ordered_ref,
                near_ref, u_far_ref, select_t, left, right):
    level_count, rank_cap, row_count = u_ref.shape
    half = rank_cap // 2
    leaf_size = leaf_ref.shape[1]
    core = lax.rem(lax.axis_index("col"), 2)
    fill_select_t(select_t, local_positions(perm_ref, row_count))
    for leaf in range(row_count // leaf_size):
        at = slice(leaf * leaf_size, (leaf + 1) * leaf_size)
        left[:, at] = dot(select_t[:, at], leaf_ref[at, :]).astype(BF16)
    right[:row_count, :] = ordered_ref[...]
    column = row_count
    iota = lax.broadcasted_iota(jnp.int32, (rank_cap, 1), 0)
    for level in range(dev_bits, level_count):
        cluster = row_count >> level - dev_bits + 1
        keep = iota < ranks_ref[level]
        for group in range(row_count // cluster):
            at = slice(group * cluster, (group + 1) * cluster)
            coef = dot(v_ref[level, :, at], ordered_ref[at, :])
            other = column + (group ^ 1) * rank_cap
            right[other : other + rank_cap, :] = jnp.where(keep, coef, 0.0).astype(BF16)
            mine = column + group * rank_cap
            left[:, mine : mine + rank_cap] = dot_t(select_t[:, at], u_ref[level, :, at]).astype(BF16)
        column += row_count // cluster * rank_cap
    near_ref[...] = dot(left[...], right[...])
    coarse = (dev_bits - 1) * half
    rows = []
    for start in (core * half, (1 - core) * half):
        for level in range(dev_bits - 1):
            rows.append(u_ref[level, pl.ds(pl.multiple_of(start, half), half), :])
    rows.append(u_ref[dev_bits - 1])
    u_rows = jnp.concatenate(rows, axis=0)
    u_far_ref[...] = dot_t(select_t[...], u_rows).astype(BF16)


def far_kernel(block, near_ref, u_far_ref, mine_ref, other_ref, sibling_ref, out_ref, far, out, sems):
    coarse, rank_cap = mine_ref.shape[0], sibling_ref.shape[0]
    far[:coarse, :] = mine_ref[...].astype(BF16)
    far[coarse : 2 * coarse, :] = other_ref[...].astype(BF16)
    far[2 * coarse :, :] = sibling_ref[...].astype(BF16)
    copies = []
    for step in range(near_ref.shape[0] // block):
        at = slice(step * block, (step + 1) * block)
        out[at, :] = (near_ref[at, :] + dot(u_far_ref[at, :], far[...])).astype(BF16)
        copy = pltpu.make_async_copy(out.at[at, :], out_ref.at[at, :], sems.at[step])
        copy.start()
        copies.append(copy)
    for copy in copies:
        copy.wait()


VMEM = pl.BlockSpec(memory_space=pltpu.VMEM)
SMEM = pl.BlockSpec(memory_space=pltpu.SMEM)
ANY = pl.BlockSpec(memory_space=pl.ANY)


def params(mib):
    return pltpu.CompilerParams(vmem_limit_bytes=mib << 20)


def cost(flops, size):
    return pl.CostEstimate(flops=flops, bytes_accessed=size, transcendentals=0)


def per_device(sources, tree_perm, leaf_blocks, u_factors, v_factors, level_ranks):
    row_count, rhs_count = sources.shape
    leaf_size = leaf_blocks.shape[1]
    level_count, rank_cap, _ = u_factors.shape
    dev_bits = (lax.axis_size("row") * lax.axis_size("col")).bit_length() - 1
    half = rank_cap // 2
    coarse = (dev_bits - 1) * half
    total = 2 * coarse + rank_cap
    lanes = 128
    perm = tree_perm.reshape(row_count // lanes, lanes)
    near_rows = sum(rank_cap << level - dev_bits + 1 for level in range(dev_bits, level_count))

    send, keep = pl.pallas_call(
        functools.partial(coef_kernel, dev_bits),
        out_shape=(
            jax.ShapeDtypeStruct((coarse + rank_cap, rhs_count), F32),
            jax.ShapeDtypeStruct((coarse, rhs_count), F32),
        ),
        in_specs=[SMEM, VMEM, VMEM, ANY],
        out_specs=(VMEM, VMEM),
        scratch_shapes=[
            pltpu.VMEM((row_count, row_count), BF16),
            pltpu.VMEM((total, row_count), BF16),
            pltpu.VMEM((row_count, rhs_count), BF16),
            pltpu.SemaphoreType.DMA,
        ],
        compiler_params=params(16),
        cost_estimate=cost(2 * total * row_count * (row_count + rhs_count), 2 << 20),
        name="coef",
    )(level_ranks, perm, v_factors, sources)

    ordered = pl.pallas_call(
        order_kernel,
        out_shape=jax.ShapeDtypeStruct((row_count, rhs_count), BF16),
        in_specs=[VMEM, VMEM],
        out_specs=VMEM,
        scratch_shapes=[pltpu.VMEM((row_count, row_count), BF16)],
        compiler_params=params(16),
        cost_estimate=cost(2 * row_count * row_count * rhs_count, 2 << 20),
        name="order",
    )(perm, sources)

    near, u_far = pl.pallas_call(
        functools.partial(near_kernel, dev_bits),
        out_shape=(
            jax.ShapeDtypeStruct((row_count, rhs_count), F32),
            jax.ShapeDtypeStruct((row_count, total), BF16),
        ),
        in_specs=[SMEM, VMEM, VMEM, VMEM, VMEM, VMEM],
        out_specs=(VMEM, VMEM),
        scratch_shapes=[
            pltpu.VMEM((row_count, row_count), BF16),
            pltpu.VMEM((row_count, row_count + near_rows), BF16),
            pltpu.VMEM((row_count + near_rows, rhs_count), BF16),
        ],
        compiler_params=params(28),
        cost_estimate=cost(2 * row_count * row_count * (leaf_size + rhs_count + total), 6 << 20),
        name="near",
    )(level_ranks, perm, leaf_blocks, u_factors, v_factors, ordered)

    received = partner(send, 0)
    running = keep + received[:coarse]
    sibling = received[coarse:]
    far = []
    for bit in range(1, dev_bits):
        received = partner(running, bit)
        far.insert(0, received[-half:])
        running = running[:-half] + received[:-half]
    mine = jnp.concatenate(far, axis=0)
    other = partner(mine, 0)

    block = row_count // 4
    return pl.pallas_call(
        functools.partial(far_kernel, block),
        out_shape=jax.ShapeDtypeStruct((row_count, rhs_count), BF16),
        in_specs=[VMEM] * 5,
        out_specs=ANY,
        scratch_shapes=[
            pltpu.VMEM((total, rhs_count), BF16),
            pltpu.VMEM((row_count, rhs_count), BF16),
            pltpu.SemaphoreType.DMA((row_count // block,)),
        ],
        compiler_params=params(16),
        cost_estimate=cost(2 * row_count * total * rhs_count, 5 << 20),
        name="far",
    )(near, u_far, mine, other, sibling)


def solution(mesh):
    placed = (
        P(("row", "col"), None),
        P(("row", "col")),
        P(("row", "col"), None),
        P(None, None, ("row", "col")),
        P(None, None, ("row", "col")),
        P(),
    )
    return jax.shard_map(
        per_device, mesh=mesh, in_specs=placed, out_specs=P(("row", "col"), None), check_vma=False
    )
```

time: 57.3 us -> 36.3 us (0.63)
  local copies, waits for them, and re-layouts: 22.6 us -> 3.7 us
  matrix products: 10.4 us -> 0 us
  Pallas kernels: 0 us -> 10.2 us
  waiting for transfers between devices: 5.07 us -> 11.4 us
  starting transfers between devices: 14.7 us -> 10.6 us
  blocking collectives: 2.74 us -> 0 us
  other arithmetic: 1.2 us -> 0.07 us
    dot_general x5 -> x0, matrix products: 10.4 us -> none  [the longest x1 3.71 us: per_device(): jnp.einsum('gij,gjr->gir', leaf_blocks.reshape(leaf_count, leaf_size, lea...]
    pallas_call x0 -> x4, Pallas kernels: none -> 10.2 us  [the longest x1 5.12 us: per_device(): pl.pallas_call(functools.partial(near_kernel, dev_bits), out_shape=(jax.S...]
    scatter x1 -> x0, local copies, waits for them, and re-layouts: 6.79 us -> none  [per_device(): jnp.zeros_like(sources).at[local_index].set(result.astype(jnp.bfloat16))]
    reshape x2 -> x0, local copies, waits for them, and re-layouts: 6.53 us -> none  [the longest x1 3.28 us: per_device(): result = result + jnp.einsum('kgs,gkr->gsr', u_factors[level].reshape(ran...]
    ppermute x11 -> x6, waiting for transfers between devices: 5.07 us -> 11.4 us  [partner(): return lax.ppermute(x, AXES, [(i, i ^ 1 << bit) for i in range(count)])]
    ppermute x11 -> x6, starting transfers between devices: 14.7 us -> 10.6 us  [partner(): return lax.ppermute(x, AXES, [(i, i ^ 1 << bit) for i in range(count)])]
    gather x1 -> x0, local copies, waits for them, and re-layouts: 4.02 us -> none  [per_device(): ordered = sources[local_index]]
    unnamed x10 -> x18, local copies, waits for them, and re-layouts: 0.7 us -> 3.68 us
  transfers between devices with their start and end apart: 11 -> 6, of which waited for: 4 -> 4; matrix products, arithmetic and copies ran while one was open for 26% -> 0% of each run, Pallas kernels for 0% -> 20%
where the time goes in v1:
time: 36.3 us; the launch traced here: 36.1 us
  waiting for transfers between devices  11.4 us (31%)
  starting transfers between devices  10.6 us (29%)
  Pallas kernels  10.2 us (28%)
  local copies, waits for them, and re-layouts  3.7 us (10%)
    ppermute x6, waiting for transfers between devices, partner(): return lax.ppermute(x, AXES, [(i, i ^ 1 << bit) for i in range(count)])  11.4 us
    ppermute x6, starting transfers between devices, partner(): return lax.ppermute(x, AXES, [(i, i ^ 1 << bit) for i in range(count)])  10.6 us
    pallas_call x1, Pallas kernels, per_device(): pl.pallas_call(functools.partial(near_kernel, dev_bits), out_shape=(jax.S...  5.12 us
    unnamed x18, local copies, waits for them, and re-layouts  3.68 us
    pallas_call x1, Pallas kernels, per_device(): pl.pallas_call(order_kernel, out_shape=jax.ShapeDtypeStruct((row_count, r...  1.92 us
    pallas_call x1, Pallas kernels, per_device(): pl.pallas_call(functools.partial(coef_kernel, dev_bits), out_shape=(jax.S...  1.77 us
    pallas_call x1, Pallas kernels, per_device(): pl.pallas_call(functools.partial(far_kernel, block), out_shape=jax.ShapeD...  1.4 us
  transfers between devices with their start and end apart: 6, of which 4 were waited for; matrix products, arithmetic and copies ran while one was open for 0% of the time, Pallas kernels for 20%

profile of v1, /device:TPU:0, one launch (start us, length us, event | category | flops | bytes accessed | tf_op | source)
XLA Modules:
  0.0 36.1 jit_solution(8246616811855799682)
XLA Ops:
  0.0 1.3 %copy-done = bf16[1024,640]{1,0:T(8,128)(2,1)S(1)} copy-done((bf16[1024,640]{1,0:T(8,128)(2,1)S(1)}, bf16[1024,640]{1,0:T(8,128)(2,1)}, u32[]{:S(2)}) %copy-start) | copy-done | bytes 1310744
  1.3 1.0 %copy-done.3 = bf16[6,32,1024]{2,1,0:T(8,128)(2,1)S(1)} copy-done((bf16[6,32,1024]{2,1,0:T(8,128)(2,1)S(1)}, bf16[6,32,1024]{2,1,0:T(8,128)(2,1)}, u32[]{:S(2)}) %copy-start.3) | copy-done | bytes 393240
  2.3 0.7 %copy-done.5 = s32[1024]{0:T(1024)S(1)} copy-done((s32[1024]{0:T(1024)S(1)}, s32[1024]{0:T(1024)}, u32[]{:S(2)}) %copy-start.5) | copy-done | bytes 4120
  3.0 0.7 %copy-done.7 = s32[6]{0:T(128)S(1)} copy-done((s32[6]{0:T(128)S(1)}, s32[6]{0:T(128)}, u32[]{:S(2)}) %copy-start.7) | copy-done | bytes 48
  3.7 1.8 %coef.1 = (f32[96,640]{1,0:T(8,128)S(1)}, f32[64,640]{1,0:T(8,128)S(1)}) custom-call(s32[6]{0:T(128)S(1)} %copy-done.7, s32[8,128]{1,0:T(8,128)S(1)} %bitcast.1, bf16[6,32,1024]{2,1,0:T(8,128)(2,1)S(1)} %copy-done.3, bf16[1024,640]{1,0:T(8,128)(2,1)S(1)} %copy-done), custom_call_target="tpu_custom_call" | custom-call | flops 545259520 | bytes 2097152 | tf_op jit(solution)/shard_map/coef/pallas_call | solution.py:160
  5.4 0.5 %collective-permute-start = (f32[96,640]{1,0:T(8,128)S(1)}, f32[96,640]{1,0:T(8,128)S(1)}, u32[]{:S(2)}, u32[]{:S(2)}) collective-permute-start(f32[96,640]{1,0:T(8,128)S(1)} %get-tuple-element.12), channel_id=1, source_target_pairs={{0,1},{1,0},{2,3},{3,2},{4,5},{5,4},{6,7},{7,6},{8,9},{9,8},{10,11... | collective-permute-start | bytes 737288 | tf_op jit(solution)/shard_map/ppermute | solution.py:16
  6.0 1.1 %collective-permute-done = f32[96,640]{1,0:T(8,128)S(1)} collective-permute-done((f32[96,640]{1,0:T(8,128)S(1)}, f32[96,640]{1,0:T(8,128)S(1)}, u32[]{:S(2)}, u32[]{:S(2)}) %collective-permute-start) | collective-permute-done | bytes 245792 | tf_op jit(solution)/shard_map/ppermute | solution.py:16
  7.1 2.9 %collective-permute-start.1 = (f32[64,640]{1,0:T(8,128)S(1)}, f32[64,640]{1,0:T(8,128)S(1)}, u32[]{:S(2)}, u32[]{:S(2)}) collective-permute-start(f32[64,640]{1,0:T(8,128)S(1)} %slice_add_fusion), channel_id=1, source_target_pairs={{0,2},{1,3},{2,0},{3,1},{4,6},{5,7},{6,4},{7,5},{8,10},{9,11},{10,... | collective-permute-start | bytes 491528 | tf_op jit(solution)/shard_map/ppermute | solution.py:16
  10.1 4.5 %collective-permute-done.1 = f32[64,640]{1,0:T(8,128)S(1)} collective-permute-done((f32[64,640]{1,0:T(8,128)S(1)}, f32[64,640]{1,0:T(8,128)S(1)}, u32[]{:S(2)}, u32[]{:S(2)}) %collective-permute-start.1) | collective-permute-done | bytes 163872 | tf_op jit(solution)/shard_map/ppermute | solution.py:16
  14.6 1.8 %collective-permute-start.2 = (f32[48,640]{1,0:T(8,128)S(1)}, f32[48,640]{1,0:T(8,128)S(1)}, u32[]{:S(2)}, u32[]{:S(2)}) collective-permute-start(f32[48,640]{1,0:T(8,128)S(1)} %slice_add_fusion.1), channel_id=1, source_target_pairs={{0,4},{1,5},{2,6},{3,7},{4,0},{5,1},{6,2},{7,3},{8,12},{9,13},{10,... | collective-permute-start | bytes 368648 | tf_op jit(solution)/shard_map/ppermute | solution.py:16
  16.4 3.1 %collective-permute-done.2 = f32[48,640]{1,0:T(8,128)S(1)} collective-permute-done((f32[48,640]{1,0:T(8,128)S(1)}, f32[48,640]{1,0:T(8,128)S(1)}, u32[]{:S(2)}, u32[]{:S(2)}) %collective-permute-start.2) | collective-permute-done | bytes 122912 | tf_op jit(solution)/shard_map/ppermute | solution.py:16
  19.5 1.9 %collective-permute-start.3 = (f32[32,640]{1,0:T(8,128)S(1)}, f32[32,640]{1,0:T(8,128)S(1)}, u32[]{:S(2)}, u32[]{:S(2)}) collective-permute-start(f32[32,640]{1,0:T(8,128)S(1)} %slice_add_fusion.2), channel_id=1, source_target_pairs={{0,8},{1,9},{2,10},{3,11},{4,12},{5,13},{6,14},{7,15},{8,0},{9,1},... | collective-permute-start | bytes 245768 | tf_op jit(solution)/shard_map/ppermute | solution.py:16
  21.4 2.6 %collective-permute-done.3 = f32[32,640]{1,0:T(8,128)S(1)} collective-permute-done((f32[32,640]{1,0:T(8,128)S(1)}, f32[32,640]{1,0:T(8,128)S(1)}, u32[]{:S(2)}, u32[]{:S(2)}) %collective-permute-start.3) | collective-permute-done | bytes 81952 | tf_op jit(solution)/shard_map/ppermute | solution.py:16
  24.1 0.0 copy-start.1
  24.1 0.0 copy-start.2
  24.1 0.0 copy-start.4
  24.1 0.0 copy-start.6
  24.1 0.0 copy-start.8
  24.1 3.3 %collective-permute-start.4 = (f32[16,640]{1,0:T(8,128)S(1)}, f32[16,640]{1,0:T(8,128)S(1)}, u32[]{:S(2)}, u32[]{:S(2)}) collective-permute-start(f32[16,640]{1,0:T(8,128)S(1)} %get-tuple-element.13), channel_id=1, source_target_pairs={{0,16},{1,17},{2,18},{3,19},{4,20},{5,21},{6,22},{7,23},{8,24},{9,... | collective-permute-start | bytes 122888 | tf_op jit(solution)/shard_map/ppermute | solution.py:16
  27.4 1.9 %order.1.ordered_ref = bf16[1024,640]{1,0:T(8,128)(2,1)S(1)} custom-call(s32[8,128]{1,0:T(8,128)S(1)} %bitcast.2, bf16[1024,640]{1,0:T(8,128)(2,1)S(1)} %copy-done), custom_call_target="tpu_custom_call" | custom-call | flops 1342177280 | bytes 2097152 | tf_op jit(solution)/shard_map/order/pallas_call | solution.py:179
  29.4 0.0 collective-permute-done.4
  29.4 0.1 collective-permute-start.5
  29.6 5.1 %near.1 = (f32[1024,640]{1,0:T(8,128)S(1)}, bf16[1024,160]{1,0:T(8,128)(2,1)S(1)}) custom-call(s32[6]{0:T(128)S(1)} %copy-done.8, s32[8,128]{1,0:T(8,128)S(1)} %bitcast.3, bf16[1024,512]{1,0:T(8,128)(2,1)S(1)} %copy-done.1, bf16[6,32,1024]{2,1,0:T(8,128)(2,1)S(1)} %copy-done.2, bf16[6,32,1024]{2,1,0:T(8,128)(2,1)S(1)} %copy-done.4, ...), custom_call_target="tpu_custom_call" | custom-call | flops 2751463424 | bytes 6291456 | tf_op jit(solution)/shard_map/near/pallas_call | solution.py:190
  34.7 1.4 %far.1 = bf16[1024,640]{1,0:T(8,128)(2,1)} custom-call(f32[1024,640]{1,0:T(8,128)S(1)} %get-tuple-element.9.near_ref, bf16[1024,160]{1,0:T(8,128)(2,1)S(1)} %get-tuple-element.10.u_far_ref, f32[64,640]{1,0:T(8,128)S(1)} %pad_maximum_fusion.mine_ref, f32[64,640]{1,0:T(8,128)S(1)} %collective-permute-done.5.other_ref, f32[32,640]{1,0:T(8,128)S(1)} %slice.54.sibling_ref), custom_call_target="tpu_custom_call" | custom-call | flops 209715200 | bytes 5242880 | tf_op jit(solution)/shard_map/far/pallas_call | solution.py:220
  (18 shorter events, 0.1 us)
Async XLA Ops:
  0.0 1.3 %copy-start = (bf16[1024,640]{1,0:T(8,128)(2,1)S(1)}, bf16[1024,640]{1,0:T(8,128)(2,1)}, u32[]{:S(2)}) copy-start(bf16[1024,640]{1,0:T(8,128)(2,1)} %sources_ref.3) | copy-start | bytes 3932164
  1.3 1.0 %copy-start.3 = (bf16[6,32,1024]{2,1,0:T(8,128)(2,1)S(1)}, bf16[6,32,1024]{2,1,0:T(8,128)(2,1)}, u32[]{:S(2)}) copy-start(bf16[6,32,1024]{2,1,0:T(8,128)(2,1)} %v_ref.3) | copy-start | bytes 1179652
  2.3 0.7 %copy-start.5 = (s32[1024]{0:T(1024)S(1)}, s32[1024]{0:T(1024)}, u32[]{:S(2)}) copy-start(s32[1024]{0:T(1024)} %param.7) | copy-start | bytes 12292
  3.0 0.7 %copy-start.7 = (s32[6]{0:T(128)S(1)}, s32[6]{0:T(128)}, u32[]{:S(2)}) copy-start(s32[6]{0:T(128)} %ranks_ref.3) | copy-start | bytes 76
  5.4 1.7 %collective-permute-start = (f32[96,640]{1,0:T(8,128)S(1)}, f32[96,640]{1,0:T(8,128)S(1)}, u32[]{:S(2)}, u32[]{:S(2)}) collective-permute-start(f32[96,640]{1,0:T(8,128)S(1)} %get-tuple-element.12), channel_id=1, source_target_pairs={{0,1},{1,0},{2,3},{3,2},{4,5},{5,4},{6,7},{7,6},{8,9},{9,8},{10,11... | collective-permute-start | bytes 737288 | tf_op jit(solution)/shard_map/ppermute | solution.py:16
  7.1 7.4 %collective-permute-start.1 = (f32[64,640]{1,0:T(8,128)S(1)}, f32[64,640]{1,0:T(8,128)S(1)}, u32[]{:S(2)}, u32[]{:S(2)}) collective-permute-start(f32[64,640]{1,0:T(8,128)S(1)} %slice_add_fusion), channel_id=1, source_target_pairs={{0,2},{1,3},{2,0},{3,1},{4,6},{5,7},{6,4},{7,5},{8,10},{9,11},{10,... | collective-permute-start | bytes 491528 | tf_op jit(solution)/shard_map/ppermute | solution.py:16
  14.6 4.9 %collective-permute-start.2 = (f32[48,640]{1,0:T(8,128)S(1)}, f32[48,640]{1,0:T(8,128)S(1)}, u32[]{:S(2)}, u32[]{:S(2)}) collective-permute-start(f32[48,640]{1,0:T(8,128)S(1)} %slice_add_fusion.1), channel_id=1, source_target_pairs={{0,4},{1,5},{2,6},{3,7},{4,0},{5,1},{6,2},{7,3},{8,12},{9,13},{10,... | collective-permute-start | bytes 368648 | tf_op jit(solution)/shard_map/ppermute | solution.py:16
  19.5 4.5 %collective-permute-start.3 = (f32[32,640]{1,0:T(8,128)S(1)}, f32[32,640]{1,0:T(8,128)S(1)}, u32[]{:S(2)}, u32[]{:S(2)}) collective-permute-start(f32[32,640]{1,0:T(8,128)S(1)} %slice_add_fusion.2), channel_id=1, source_target_pairs={{0,8},{1,9},{2,10},{3,11},{4,12},{5,13},{6,14},{7,15},{8,0},{9,1},... | collective-permute-start | bytes 245768 | tf_op jit(solution)/shard_map/ppermute | solution.py:16
  24.1 5.5 %copy-start.1 = (bf16[1024,512]{1,0:T(8,128)(2,1)S(1)}, bf16[1024,512]{1,0:T(8,128)(2,1)}, u32[]{:S(2)}) copy-start(bf16[1024,512]{1,0:T(8,128)(2,1)} %leaf_ref.1) | copy-start | bytes 3145732
  24.1 5.5 %copy-start.2 = (bf16[6,32,1024]{2,1,0:T(8,128)(2,1)S(1)}, bf16[6,32,1024]{2,1,0:T(8,128)(2,1)}, u32[]{:S(2)}) copy-start(bf16[6,32,1024]{2,1,0:T(8,128)(2,1)} %u_ref.1) | copy-start | bytes 1179652
  24.1 5.5 %copy-start.4 = (bf16[6,32,1024]{2,1,0:T(8,128)(2,1)S(1)}, bf16[6,32,1024]{2,1,0:T(8,128)(2,1)}, u32[]{:S(2)}) copy-start(bf16[6,32,1024]{2,1,0:T(8,128)(2,1)} %v_ref.3) | copy-start | bytes 1179652
  24.1 5.4 %copy-start.6 = (s32[1024]{0:T(1024)S(1)}, s32[1024]{0:T(1024)}, u32[]{:S(2)}) copy-start(s32[1024]{0:T(1024)} %param.7) | copy-start | bytes 12292
  24.1 5.4 %copy-start.8 = (s32[6]{0:T(128)S(1)}, s32[6]{0:T(128)}, u32[]{:S(2)}) copy-start(s32[6]{0:T(128)} %ranks_ref.3) | copy-start | bytes 76
  24.1 5.3 %collective-permute-start.4 = (f32[16,640]{1,0:T(8,128)S(1)}, f32[16,640]{1,0:T(8,128)S(1)}, u32[]{:S(2)}, u32[]{:S(2)}) collective-permute-start(f32[16,640]{1,0:T(8,128)S(1)} %get-tuple-element.13), channel_id=1, source_target_pairs={{0,16},{1,17},{2,18},{3,19},{4,20},{5,21},{6,22},{7,23},{8,24},{9,... | collective-permute-start | bytes 122888 | tf_op jit(solution)/shard_map/ppermute | solution.py:16
  29.4 5.3 %collective-permute-start.5 = (f32[64,640]{1,0:T(8,128)S(1)}, f32[64,640]{1,0:T(8,128)S(1)}, u32[]{:S(2)}, u32[]{:S(2)}) collective-permute-start(f32[64,640]{1,0:T(8,128)S(1)} %pad_maximum_fusion.mine_ref), channel_id=1, source_target_pairs={{0,1},{1,0},{2,3},{3,2},{4,5},{5,4},{6,7},{7,6},{8,9},{9,8},{10,11... | collective-permute-start | bytes 491528 | tf_op jit(solution)/shard_map/ppermute | solution.py:16

commit v2 on v1

v2 whole, which is shorter than its diff:
```python
import functools

import jax
import jax.numpy as jnp
from jax import lax
from jax.experimental import pallas as pl
from jax.experimental.pallas import tpu as pltpu
from jax.sharding import PartitionSpec as P


AXES = ("row", "col")
BF16, F32 = jnp.bfloat16, jnp.float32


def partner(x, bit):
    count = lax.axis_size("row") * lax.axis_size("col")
    return lax.ppermute(x, AXES, [(i, i ^ 1 << bit) for i in range(count)])


def local_positions(perm_ref, row_count):
    return lax.rem(perm_ref[...], row_count)


def fill_select(select_ref, index):
    blocks, width = index.shape
    columns = index.T
    lane = lax.broadcasted_iota(jnp.int32, (width, blocks * width), 1)
    for block in range(blocks):
        hit = lane == columns[:, block : block + 1]
        select_ref[block * width : (block + 1) * width, :] = jnp.where(hit, 1.0, 0.0).astype(BF16)


def fill_select_t(select_ref, index):
    blocks, width = index.shape
    sublane = lax.broadcasted_iota(jnp.int32, (blocks * width, width), 0)
    for block in range(blocks):
        hit = sublane == index[block : block + 1, :]
        select_ref[:, block * width : (block + 1) * width] = jnp.where(hit, 1.0, 0.0).astype(BF16)


def dot(a, b):
    return jnp.dot(a, b, preferred_element_type=F32)


def dot_t(a, b):
    return lax.dot_general(a, b, (((1,), (1,)), ((), ())), preferred_element_type=F32)


def coef_kernel(dev_bits, ranks_hbm, perm_hbm, v_hbm, sources_hbm, send_ref, keep_ref,
                select, sources, v, perm, ranks, v_rows, sems):
    copies = [
        pltpu.make_async_copy(source, target, sems.at[at])
        for at, (source, target) in enumerate(
            ((perm_hbm, perm), (ranks_hbm, ranks), (v_hbm, v), (sources_hbm, sources))
        )
    ]
    for copy in copies:
        copy.start()
    rank_cap, row_count = v.shape[1:]
    half = rank_cap // 2
    coarse = (dev_bits - 1) * half
    core = lax.rem(lax.axis_index("col"), 2)
    iota = lax.broadcasted_iota(jnp.int32, (half, 1), 0)

    def masked(level, start):
        rows = v[level, pl.ds(pl.multiple_of(start, half), half), :]
        return jnp.where(iota + start < ranks[level], rows.astype(F32), 0.0).astype(BF16)

    copies[0].wait()
    fill_select(select, local_positions(perm, row_count))
    copies[1].wait()
    copies[2].wait()
    for level in range(dev_bits - 1):
        v_rows[level * half : (level + 1) * half, :] = masked(level, (1 - core) * half)
        at = coarse + rank_cap + level * half
        v_rows[at : at + half, :] = masked(level, core * half)
    for part in range(2):
        at = coarse + part * half
        v_rows[at : at + half, :] = masked(dev_bits - 1, jnp.int32(part * half))
    v_local = dot(v_rows[...], select[...]).astype(BF16)
    copies[3].wait()
    coef = dot(v_local, sources[...])
    send_ref[...] = coef[: coarse + rank_cap]
    keep_ref[...] = coef[coarse + rank_cap :]


def order_kernel(dev_bits, ranks_ref, perm_ref, sources_ref, v_ref, ordered_ref, near_far_ref, select):
    level_count, rank_cap, row_count = v_ref.shape
    fill_select(select, local_positions(perm_ref, row_count))
    ordered_ref[...] = dot(select[...], sources_ref[...]).astype(BF16)
    iota = lax.broadcasted_iota(jnp.int32, (rank_cap, 1), 0)
    row = 0
    for level in range(dev_bits, level_count):
        cluster = row_count >> level - dev_bits + 1
        keep = iota < ranks_ref[level]
        for group in range(row_count // cluster):
            at = slice(group * cluster, (group + 1) * cluster)
            coef = dot(v_ref[level, :, at], ordered_ref[at, :])
            other = row + (group ^ 1) * rank_cap
            near_far_ref[other : other + rank_cap, :] = jnp.where(keep, coef, 0.0).astype(BF16)
        row += row_count // cluster * rank_cap


def leaf_kernel(dev_bits, perm_ref, leaf_ref, u_ref, left_ref, u_far_ref, select_t):
    level_count, rank_cap, row_count = u_ref.shape
    half = rank_cap // 2
    coarse = (dev_bits - 1) * half
    leaf_size = leaf_ref.shape[1]
    core = lax.rem(lax.axis_index("col"), 2)
    fill_select_t(select_t, local_positions(perm_ref, row_count))
    for leaf in range(row_count // leaf_size):
        at = slice(leaf * leaf_size, (leaf + 1) * leaf_size)
        left_ref[:, at] = dot(select_t[:, at], leaf_ref[at, :]).astype(BF16)
    rows = []
    for start in (core * half, (1 - core) * half):
        for level in range(dev_bits - 1):
            rows.append(u_ref[level, pl.ds(pl.multiple_of(start, half), half), :])
    rows.append(u_ref[dev_bits - 1])
    column = 2 * coarse + rank_cap
    u_far_ref[:, :column] = dot_t(select_t[...], jnp.concatenate(rows, axis=0)).astype(BF16)
    for level in range(dev_bits, level_count):
        cluster = row_count >> level - dev_bits + 1
        for group in range(row_count // cluster):
            at = slice(group * cluster, (group + 1) * cluster)
            part = dot_t(select_t[:, at], u_ref[level, :, at])
            u_far_ref[:, column : column + rank_cap] = part.astype(BF16)
            column += rank_cap


def near_kernel(left_ref, ordered_ref, near_ref):
    near_ref[...] = dot(left_ref[...], ordered_ref[...])


def far_kernel(block, near_ref, u_far_ref, mine_ref, other_ref, first_ref, near_far_ref, out_ref, far, out, sems):
    coarse = mine_ref.shape[0]
    rank_cap = first_ref.shape[0] - coarse
    far[:coarse, :] = mine_ref[...].astype(BF16)
    far[coarse : 2 * coarse, :] = other_ref[...].astype(BF16)
    far[2 * coarse : 2 * coarse + rank_cap, :] = first_ref[coarse:, :].astype(BF16)
    far[2 * coarse + rank_cap :, :] = near_far_ref[...]
    copies = []
    for step in range(near_ref.shape[0] // block):
        at = slice(step * block, (step + 1) * block)
        out[at, :] = (near_ref[at, :] + dot(u_far_ref[at, :], far[...])).astype(BF16)
        copy = pltpu.make_async_copy(out.at[at, :], out_ref.at[at, :], sems.at[step])
        copy.start()
        copies.append(copy)
    for copy in copies:
        copy.wait()


VMEM = pl.BlockSpec(memory_space=pltpu.VMEM)
SMEM = pl.BlockSpec(memory_space=pltpu.SMEM)
HBM = pl.BlockSpec(memory_space=pltpu.HBM)


def params(mib):
    return pltpu.CompilerParams(vmem_limit_bytes=mib << 20)


def cost(flops, size):
    return pl.CostEstimate(flops=flops, bytes_accessed=size, transcendentals=0)


def like(shape, dtype):
    return jax.ShapeDtypeStruct(shape, dtype)


def exchange(send, keep, half, dev_bits):
    count = 1 << dev_bits
    coarse = keep.shape[0]
    first = lax.rem(lax.axis_index("col"), 2) == 1

    def crossed(x, bits):
        return lax.ppermute(x, AXES, [(i, i ^ 1 << bits[i & 1]) for i in range(count)])

    received = partner(send, 0)
    running = keep + received[:coarse]
    first_received = received
    received = crossed(running, (2, 1))
    met = received[-2 * half : -half]
    summed = running[:-half] + received[:-half]
    one = received[-half:]
    again = jnp.where(first, summed[-half:], met)
    running = jnp.concatenate([summed[:-half], again, running[-half:]], axis=0)
    received = crossed(running, (1, 2))
    far = [
        received[-2 * half : -half] + jnp.where(first, 0.0, met),
        jnp.where(first, one, received[-half:]),
    ]
    running = running[: -2 * half] + received[: -2 * half]
    for bit in range(3, dev_bits):
        received = partner(running, bit)
        far.insert(0, received[-half:])
        running = running[:-half] + received[:-half]
    mine = jnp.concatenate(far, axis=0)
    return mine, partner(mine, 0), first_received


def per_device(sources, tree_perm, leaf_blocks, u_factors, v_factors, level_ranks):
    row_count, rhs_count = sources.shape
    leaf_size = leaf_blocks.shape[1]
    level_count, rank_cap, _ = u_factors.shape
    dev_bits = (lax.axis_size("row") * lax.axis_size("col")).bit_length() - 1
    half = rank_cap // 2
    coarse = (dev_bits - 1) * half
    total = 2 * coarse + rank_cap
    lanes = 128
    perm_shape = (row_count // lanes, lanes)
    near_rows = sum(rank_cap << level - dev_bits + 1 for level in range(dev_bits, level_count))

    def in_hbm(x):
        return pltpu.with_memory_space_constraint(x, pltpu.HBM)

    perm = tree_perm.reshape(perm_shape)
    send, keep = pl.pallas_call(
        functools.partial(coef_kernel, dev_bits),
        out_shape=(like((coarse + rank_cap, rhs_count), F32), like((coarse, rhs_count), F32)),
        in_specs=[HBM] * 4,
        out_specs=(VMEM,) * 2,
        scratch_shapes=[
            pltpu.VMEM((row_count, row_count), BF16),
            pltpu.VMEM(sources.shape, BF16),
            pltpu.VMEM(v_factors.shape, BF16),
            pltpu.VMEM(perm_shape, jnp.int32),
            pltpu.SMEM((level_count,), jnp.int32),
            pltpu.VMEM((total, row_count), BF16),
            pltpu.SemaphoreType.DMA((4,)),
        ],
        compiler_params=params(16),
        cost_estimate=cost(2 * total * row_count * (row_count + rhs_count), 2 << 20),
        name="coef",
    )(in_hbm(level_ranks), in_hbm(perm), in_hbm(v_factors), in_hbm(sources))

    ordered, near_far = pl.pallas_call(
        functools.partial(order_kernel, dev_bits),
        out_shape=(like(sources.shape, BF16), like((near_rows, rhs_count), BF16)),
        in_specs=[SMEM] + [VMEM] * 3,
        out_specs=(VMEM,) * 2,
        scratch_shapes=[pltpu.VMEM((row_count, row_count), BF16)],
        compiler_params=params(16),
        cost_estimate=cost(2 * row_count * row_count * rhs_count, 2 << 20),
        name="order",
    )(level_ranks, perm, sources, v_factors)

    left, u_far = pl.pallas_call(
        functools.partial(leaf_kernel, dev_bits),
        out_shape=(like((row_count, row_count), BF16), like((row_count, total + near_rows), BF16)),
        in_specs=[VMEM] * 3,
        out_specs=(VMEM,) * 2,
        scratch_shapes=[pltpu.VMEM((row_count, row_count), BF16)],
        compiler_params=params(16),
        cost_estimate=cost(2 * row_count * row_count * (leaf_size + total), 4 << 20),
        name="leaf",
    )(perm, leaf_blocks, u_factors)

    near = pl.pallas_call(
        near_kernel,
        out_shape=like((row_count, rhs_count), F32),
        in_specs=[VMEM] * 2,
        out_specs=VMEM,
        compiler_params=params(16),
        cost_estimate=cost(2 * row_count * row_count * rhs_count, 6 << 20),
        name="near",
    )(left, ordered)

    mine, other, received = exchange(send, keep, half, dev_bits)

    block = row_count // 4
    return pl.pallas_call(
        functools.partial(far_kernel, block),
        out_shape=like((row_count, rhs_count), BF16),
        in_specs=[VMEM] * 6,
        out_specs=HBM,
        scratch_shapes=[
            pltpu.VMEM((total + near_rows, rhs_count), BF16),
            pltpu.VMEM((row_count, rhs_count), BF16),
            pltpu.SemaphoreType.DMA((row_count // block,)),
        ],
        compiler_params=params(16),
        cost_estimate=cost(2 * row_count * total * rhs_count, 5 << 20),
        name="far",
    )(near, u_far, mine, other, received, near_far)


def solution(mesh):
    placed = (
        P(("row", "col"), None),
        P(("row", "col")),
        P(("row", "col"), None),
        P(None, None, ("row", "col")),
        P(None, None, ("row", "col")),
        P(),
    )

    return jax.shard_map(
        per_device, mesh=mesh, in_specs=placed, out_specs=P(("row", "col"), None), check_vma=False
    )
```

time: 36.3 us -> 31.9 us (0.88)
  local copies, waits for them, and re-layouts: 3.7 us -> 0.05 us
  waiting for transfers between devices: 11.4 us -> 9.73 us
  Pallas kernels: 10.2 us -> 10.7 us
  starting transfers between devices: 10.6 us -> 11 us
    ppermute x6 -> x4, waiting for transfers between devices: 11.4 us -> 3.11 us  [partner(): return lax.ppermute(x, AXES, [(i, i ^ 1 << bit) for i in range(count)])]
    ppermute x0 -> x2, waiting for transfers between devices: none -> 6.62 us  [crossed(): lax.ppermute(x, AXES, [(i, i ^ 1 << bits[i & 1]) for i in range(count)])]
    ppermute x0 -> x2, starting transfers between devices: none -> 5 us  [crossed(): lax.ppermute(x, AXES, [(i, i ^ 1 << bits[i & 1]) for i in range(count)])]
    ppermute x6 -> x4, starting transfers between devices: 10.6 us -> 6.01 us  [partner(): return lax.ppermute(x, AXES, [(i, i ^ 1 << bit) for i in range(count)])]
    unnamed x18 -> x12, local copies, waits for them, and re-layouts: 3.68 us -> 0.04 us
    pallas_call x4 -> x5, Pallas kernels: 10.2 us -> 10.7 us  [the longest x1 2.79 us: per_device(): pl.pallas_call(functools.partial(order_kernel, dev_bits), out_shape=(like...]
  transfers between devices with their start and end apart: 6 -> 6, of which waited for: 4 -> 4; matrix products, arithmetic and copies ran while one was open for 0% -> 0% of each run, Pallas kernels for 20% -> 22%
where the time goes in v2:
time: 31.9 us; the launch traced here: 31.8 us
  starting transfers between devices  11 us (34%)
  Pallas kernels  10.7 us (34%)
  waiting for transfers between devices  9.73 us (31%)
    ppermute x2, waiting for transfers between devices, crossed(): lax.ppermute(x, AXES, [(i, i ^ 1 << bits[i & 1]) for i in range(count)])  6.62 us
    ppermute x4, starting transfers between devices, partner(): return lax.ppermute(x, AXES, [(i, i ^ 1 << bit) for i in range(count)])  6.01 us
    ppermute x2, starting transfers between devices, crossed(): lax.ppermute(x, AXES, [(i, i ^ 1 << bits[i & 1]) for i in range(count)])  5 us
    ppermute x4, waiting for transfers between devices, partner(): return lax.ppermute(x, AXES, [(i, i ^ 1 << bit) for i in range(count)])  3.11 us
    pallas_call x1, Pallas kernels, per_device(): pl.pallas_call(functools.partial(order_kernel, dev_bits), out_shape=(like...  2.79 us
    pallas_call x1, Pallas kernels, per_device(): pl.pallas_call(functools.partial(leaf_kernel, dev_bits), out_shape=(like(...  2.43 us
    pallas_call x1, Pallas kernels, per_device(): pl.pallas_call(functools.partial(coef_kernel, dev_bits), out_shape=(like(...  2.3 us
    pallas_call x1, Pallas kernels, per_device(): pl.pallas_call(near_kernel, out_shape=like((row_count, rhs_count), F32),...  1.8 us
  transfers between devices with their start and end apart: 6, of which 4 were waited for; matrix products, arithmetic and copies ran while one was open for 0% of the time, Pallas kernels for 22%

profile of v2, /device:TPU:0, one launch (start us, length us, event | category | flops | bytes accessed | tf_op | source)
XLA Modules:
  0.0 31.8 jit_solution(367457587056549400)
XLA Ops:
  0.0 2.3 %coef.1 = (f32[96,640]{1,0:T(8,128)S(1)}, f32[64,640]{1,0:T(8,128)S(1)}) custom-call(s32[6]{0:T(128)} %ranks_hbm.1, s32[8,128]{1,0:T(8,128)} %bitcast.1, bf16[6,32,1024]{2,1,0:T(8,128)(2,1)} %v_hbm.1, bf16[1024,640]{1,0:T(8,128)(2,1)} %sources_hbm.1), custom_call_target="tpu_custom_call" | custom-call | flops 545259520 | bytes 2097152 | tf_op jit(solution)/shard_map/coef/pallas_call | solution.py:216
  2.3 0.0 copy-start.1
  2.3 0.0 copy-start.2
  2.3 0.0 copy-start.4
  2.3 0.6 %collective-permute-start = (f32[96,640]{1,0:T(8,128)S(1)}, f32[96,640]{1,0:T(8,128)S(1)}, u32[]{:S(2)}, u32[]{:S(2)}) collective-permute-start(f32[96,640]{1,0:T(8,128)S(1)} %get-tuple-element.15), channel_id=1, source_target_pairs={{0,1},{1,0},{2,3},{3,2},{4,5},{5,4},{6,7},{7,6},{8,9},{9,8},{10,11... | collective-permute-start | bytes 737288 | tf_op jit(solution)/shard_map/ppermute | solution.py:17
  2.9 1.1 %collective-permute-done.first_ref = f32[96,640]{1,0:T(8,128)S(1)} collective-permute-done((f32[96,640]{1,0:T(8,128)S(1)}, f32[96,640]{1,0:T(8,128)S(1)}, u32[]{:S(2)}, u32[]{:S(2)}) %collective-permute-start) | collective-permute-done | bytes 245792 | tf_op jit(solution)/shard_map/ppermute | solution.py:17
  4.1 2.9 %collective-permute-start.1 = (f32[64,640]{1,0:T(8,128)S(1)}, f32[64,640]{1,0:T(8,128)S(1)}, u32[]{:S(2)}, u32[]{:S(2)}) collective-permute-start(f32[64,640]{1,0:T(8,128)S(1)} %slice_add_fusion), channel_id=1, source_target_pairs={{0,4},{1,3},{2,6},{3,1},{4,0},{5,7},{6,2},{7,5},{8,12},{9,11},{10,... | collective-permute-start | bytes 491528 | tf_op jit(solution)/shard_map/ppermute | solution.py:175
  7.0 3.3 %collective-permute-done.1 = f32[64,640]{1,0:T(8,128)S(1)} collective-permute-done((f32[64,640]{1,0:T(8,128)S(1)}, f32[64,640]{1,0:T(8,128)S(1)}, u32[]{:S(2)}, u32[]{:S(2)}) %collective-permute-start.1) | collective-permute-done | bytes 163872 | tf_op jit(solution)/shard_map/ppermute | solution.py:175
  10.4 2.1 %collective-permute-start.2 = (f32[64,640]{1,0:T(8,128)S(1)}, f32[64,640]{1,0:T(8,128)S(1)}, u32[]{:S(2)}, u32[]{:S(2)}) collective-permute-start(f32[64,640]{1,0:T(8,128)S(1)} %pad_maximum_fusion), channel_id=1, source_target_pairs={{0,2},{1,5},{2,0},{3,7},{4,6},{5,1},{6,4},{7,3},{8,10},{9,13},{10,... | collective-permute-start | bytes 491528 | tf_op jit(solution)/shard_map/ppermute | solution.py:175
  12.4 3.3 %collective-permute-done.2 = f32[64,640]{1,0:T(8,128)S(1)} collective-permute-done((f32[64,640]{1,0:T(8,128)S(1)}, f32[64,640]{1,0:T(8,128)S(1)}, u32[]{:S(2)}, u32[]{:S(2)}) %collective-permute-start.2) | collective-permute-done | bytes 163872 | tf_op jit(solution)/shard_map/ppermute | solution.py:175
  15.8 0.0 copy-start
  15.8 0.0 copy-start.3
  15.8 0.0 copy-start.5
  15.8 2.1 %collective-permute-start.3 = (f32[32,640]{1,0:T(8,128)S(1)}, f32[32,640]{1,0:T(8,128)S(1)}, u32[]{:S(2)}, u32[]{:S(2)}) collective-permute-start(f32[32,640]{1,0:T(8,128)S(1)} %slice_add_fusion.2), channel_id=1, source_target_pairs={{0,8},{1,9},{2,10},{3,11},{4,12},{5,13},{6,14},{7,15},{8,0},{9,1},... | collective-permute-start | bytes 245768 | tf_op jit(solution)/shard_map/ppermute | solution.py:17
  17.9 0.0 copy-done.1
  18.0 2.4 %leaf.1 = (bf16[1024,1024]{1,0:T(8,128)(2,1)S(1)}, bf16[1024,224]{1,0:T(8,128)(2,1)S(1)}) custom-call(s32[8,128]{1,0:T(8,128)S(1)} %bitcast.2, bf16[1024,512]{1,0:T(8,128)(2,1)S(1)} %copy-done.1, bf16[6,32,1024]{2,1,0:T(8,128)(2,1)S(1)} %copy-done.2), custom_call_target="tpu_custom_call" | custom-call | flops 1409286144 | bytes 4194304 | tf_op jit(solution)/shard_map/leaf/pallas_call | solution.py:246
  20.4 0.0 collective-permute-done.3
  20.4 3.2 %collective-permute-start.4 = (f32[16,640]{1,0:T(8,128)S(1)}, f32[16,640]{1,0:T(8,128)S(1)}, u32[]{:S(2)}, u32[]{:S(2)}) collective-permute-start(f32[16,640]{1,0:T(8,128)S(1)} %get-tuple-element.19), channel_id=1, source_target_pairs={{0,16},{1,17},{2,18},{3,19},{4,20},{5,21},{6,22},{7,23},{8,24},{9,... | collective-permute-start | bytes 122888 | tf_op jit(solution)/shard_map/ppermute | solution.py:17
  23.7 2.0 %collective-permute-done.4 = f32[16,640]{1,0:T(8,128)S(1)} collective-permute-done((f32[16,640]{1,0:T(8,128)S(1)}, f32[16,640]{1,0:T(8,128)S(1)}, u32[]{:S(2)}, u32[]{:S(2)}) %collective-permute-start.4) | collective-permute-done | bytes 40992 | tf_op jit(solution)/shard_map/ppermute | solution.py:17
  25.6 0.1 collective-permute-start.5
  25.7 2.8 %order.1 = (bf16[1024,640]{1,0:T(8,128)(2,1)S(1)}, bf16[64,640]{1,0:T(8,128)(2,1)S(1)}) custom-call(s32[6]{0:T(128)S(1)} %copy-done.5, s32[8,128]{1,0:T(8,128)S(1)} %bitcast.3, bf16[1024,640]{1,0:T(8,128)(2,1)S(1)} %copy-done, bf16[6,32,1024]{2,1,0:T(8,128)(2,1)S(1)} %copy-done.3), custom_call_target="tpu_custom_call" | custom-call | flops 1342177280 | bytes 2097152 | tf_op jit(solution)/shard_map/order/pallas_call | solution.py:235
  28.6 1.8 %near.1.near_ref = f32[1024,640]{1,0:T(8,128)S(1)} custom-call(bf16[1024,1024]{1,0:T(8,128)(2,1)S(1)} %get-tuple-element.11.left_ref, bf16[1024,640]{1,0:T(8,128)(2,1)S(1)} %get-tuple-element.12.ordered_ref), custom_call_target="tpu_custom_call" | custom-call | flops 1342177280 | bytes 6291456 | tf_op jit(solution)/shard_map/near/pallas_call | solution.py:257
  30.4 0.0 collective-permute-done.5.other_ref
  30.4 1.4 %far.1 = bf16[1024,640]{1,0:T(8,128)(2,1)} custom-call(f32[1024,640]{1,0:T(8,128)S(1)} %near.1.near_ref, bf16[1024,224]{1,0:T(8,128)(2,1)S(1)} %get-tuple-element.13.u_far_ref, f32[64,640]{1,0:T(8,128)S(1)} %pad_maximum_fusion.1.mine_ref, f32[64,640]{1,0:T(8,128)S(1)} %collective-permute-done.5.other_ref, f32[96,640]{1,0:T(8,128)S(1)} %collective-permute-done.first_ref, ...), custom_call_target="tpu_custom_call" | custom-call | flops 209715200 | bytes 5242880 | tf_op jit(solution)/shard_map/far/pallas_call | solution.py:270
  (15 shorter events, 0.1 us)
Async XLA Ops:
  2.3 15.6 %copy-start.1 = (bf16[1024,512]{1,0:T(8,128)(2,1)S(1)}, bf16[1024,512]{1,0:T(8,128)(2,1)}, u32[]{:S(2)}) copy-start(bf16[1024,512]{1,0:T(8,128)(2,1)} %leaf_ref.1) | copy-start | bytes 3145732
  2.3 15.6 %copy-start.2 = (bf16[6,32,1024]{2,1,0:T(8,128)(2,1)S(1)}, bf16[6,32,1024]{2,1,0:T(8,128)(2,1)}, u32[]{:S(2)}) copy-start(bf16[6,32,1024]{2,1,0:T(8,128)(2,1)} %u_ref.1) | copy-start | bytes 1179652
  2.3 15.6 %copy-start.4 = (s32[1024]{0:T(1024)S(1)}, s32[1024]{0:T(1024)}, u32[]{:S(2)}) copy-start(s32[1024]{0:T(1024)} %param.7) | copy-start | bytes 12292
  2.3 1.7 %collective-permute-start = (f32[96,640]{1,0:T(8,128)S(1)}, f32[96,640]{1,0:T(8,128)S(1)}, u32[]{:S(2)}, u32[]{:S(2)}) collective-permute-start(f32[96,640]{1,0:T(8,128)S(1)} %get-tuple-element.15), channel_id=1, source_target_pairs={{0,1},{1,0},{2,3},{3,2},{4,5},{5,4},{6,7},{7,6},{8,9},{9,8},{10,11... | collective-permute-start | bytes 737288 | tf_op jit(solution)/shard_map/ppermute | solution.py:17
  4.1 6.2 %collective-permute-start.1 = (f32[64,640]{1,0:T(8,128)S(1)}, f32[64,640]{1,0:T(8,128)S(1)}, u32[]{:S(2)}, u32[]{:S(2)}) collective-permute-start(f32[64,640]{1,0:T(8,128)S(1)} %slice_add_fusion), channel_id=1, source_target_pairs={{0,4},{1,3},{2,6},{3,1},{4,0},{5,7},{6,2},{7,5},{8,12},{9,11},{10,... | collective-permute-start | bytes 491528 | tf_op jit(solution)/shard_map/ppermute | solution.py:175
  10.4 5.4 %collective-permute-start.2 = (f32[64,640]{1,0:T(8,128)S(1)}, f32[64,640]{1,0:T(8,128)S(1)}, u32[]{:S(2)}, u32[]{:S(2)}) collective-permute-start(f32[64,640]{1,0:T(8,128)S(1)} %pad_maximum_fusion), channel_id=1, source_target_pairs={{0,2},{1,5},{2,0},{3,7},{4,6},{5,1},{6,4},{7,3},{8,10},{9,13},{10,... | collective-permute-start | bytes 491528 | tf_op jit(solution)/shard_map/ppermute | solution.py:175
  15.8 10.0 %copy-start = (bf16[1024,640]{1,0:T(8,128)(2,1)S(1)}, bf16[1024,640]{1,0:T(8,128)(2,1)}, u32[]{:S(2)}) copy-start(bf16[1024,640]{1,0:T(8,128)(2,1)} %sources_hbm.1) | copy-start | bytes 3932164
  15.8 10.0 %copy-start.3 = (bf16[6,32,1024]{2,1,0:T(8,128)(2,1)S(1)}, bf16[6,32,1024]{2,1,0:T(8,128)(2,1)}, u32[]{:S(2)}) copy-start(bf16[6,32,1024]{2,1,0:T(8,128)(2,1)} %v_hbm.1) | copy-start | bytes 1179652
  15.8 10.0 %copy-start.5 = (s32[6]{0:T(128)S(1)}, s32[6]{0:T(128)}, u32[]{:S(2)}) copy-start(s32[6]{0:T(128)} %ranks_hbm.1) | copy-start | bytes 76
  15.8 4.6 %collective-permute-start.3 = (f32[32,640]{1,0:T(8,128)S(1)}, f32[32,640]{1,0:T(8,128)S(1)}, u32[]{:S(2)}, u32[]{:S(2)}) collective-permute-start(f32[32,640]{1,0:T(8,128)S(1)} %slice_add_fusion.2), channel_id=1, source_target_pairs={{0,8},{1,9},{2,10},{3,11},{4,12},{5,13},{6,14},{7,15},{8,0},{9,1},... | collective-permute-start | bytes 245768 | tf_op jit(solution)/shard_map/ppermute | solution.py:17
  20.4 5.2 %collective-permute-start.4 = (f32[16,640]{1,0:T(8,128)S(1)}, f32[16,640]{1,0:T(8,128)S(1)}, u32[]{:S(2)}, u32[]{:S(2)}) collective-permute-start(f32[16,640]{1,0:T(8,128)S(1)} %get-tuple-element.19), channel_id=1, source_target_pairs={{0,16},{1,17},{2,18},{3,19},{4,20},{5,21},{6,22},{7,23},{8,24},{9,... | collective-permute-start | bytes 122888 | tf_op jit(solution)/shard_map/ppermute | solution.py:17
  25.6 4.7 %collective-permute-start.5 = (f32[64,640]{1,0:T(8,128)S(1)}, f32[64,640]{1,0:T(8,128)S(1)}, u32[]{:S(2)}, u32[]{:S(2)}) collective-permute-start(f32[64,640]{1,0:T(8,128)S(1)} %pad_maximum_fusion.1.mine_ref), channel_id=1, source_target_pairs={{0,1},{1,0},{2,3},{3,2},{4,5},{5,4},{6,7},{7,6},{8,9},{9,8},{10,11... | collective-permute-start | bytes 491528 | tf_op jit(solution)/shard_map/ppermute | solution.py:17

commit v3 on v2

--- a/solution.py
+++ b/solution.py
@@ -12,9 +12,24 @@
 BF16, F32 = jnp.bfloat16, jnp.float32
 
 
-def partner(x, bit):
-    count = lax.axis_size("row") * lax.axis_size("col")
-    return lax.ppermute(x, AXES, [(i, i ^ 1 << bit) for i in range(count)])
+def parity(index, bits):
+    folded = index
+    for bit in range(1, bits):
+        folded = folded ^ index >> bit
+    return folded & 1
+
+
+def half_index(dev_bits):
+    return parity(lax.axis_index("row") * lax.axis_size("col") + lax.axis_index("col"), dev_bits)
+
+
+def core_swap(x, dev_bits):
+    return lax.ppermute(x, AXES, [(i, i ^ 1) for i in range(1 << dev_bits)])
+
+
+def chip_swap(x, dev_bits, bits):
+    pairs = [(i, i ^ 1 << bits[parity(i, dev_bits)] ^ 1) for i in range(1 << dev_bits)]
+    return lax.ppermute(x, AXES, pairs)
 
 
 def local_positions(perm_ref, row_count):
@@ -46,20 +61,21 @@
     return lax.dot_general(a, b, (((1,), (1,)), ((), ())), preferred_element_type=F32)
 
 
-def coef_kernel(dev_bits, ranks_hbm, perm_hbm, v_hbm, sources_hbm, send_ref, keep_ref,
-                select, sources, v, perm, ranks, v_rows, sems):
+def coef_kernel(dev_bits, ranks_hbm, perm_hbm, v_hbm, sources_hbm, u_hbm,
+                send_ref, keep_ref, near_far_ref, perm, u,
+                select, sources, v, ranks, v_rows, sems):
     copies = [
         pltpu.make_async_copy(source, target, sems.at[at])
         for at, (source, target) in enumerate(
-            ((perm_hbm, perm), (ranks_hbm, ranks), (v_hbm, v), (sources_hbm, sources))
+            ((perm_hbm, perm), (ranks_hbm, ranks), (v_hbm, v), (sources_hbm, sources), (u_hbm, u))
         )
     ]
     for copy in copies:
         copy.start()
-    rank_cap, row_count = v.shape[1:]
+    level_count, rank_cap, row_count = v.shape
     half = rank_cap // 2
     coarse = (dev_bits - 1) * half
-    core = lax.rem(lax.axis_index("col"), 2)
+    core = half_index(dev_bits)
     iota = lax.broadcasted_iota(jnp.int32, (half, 1), 0)
 
     def masked(level, start):
@@ -77,40 +93,34 @@
     for part in range(2):
         at = coarse + part * half
         v_rows[at : at + half, :] = masked(dev_bits - 1, jnp.int32(part * half))
+    row = 2 * coarse + rank_cap
+    column = lax.broadcasted_iota(jnp.int32, (1, row_count), 1)
+    rank = lax.broadcasted_iota(jnp.int32, (rank_cap, 1), 0)
+    for level in range(dev_bits, level_count):
+        cluster = row_count >> level - dev_bits + 1
+        groups = row_count // cluster
+        rows = jnp.where(rank < ranks[level], v[level].astype(F32), 0.0)
+        for group in range(groups):
+            other = group ^ 1
+            inside = (column >= other * cluster) & (column < (other + 1) * cluster)
+            v_rows[row : row + rank_cap, :] = jnp.where(inside, rows, 0.0).astype(BF16)
+            row += rank_cap
     v_local = dot(v_rows[...], select[...]).astype(BF16)
     copies[3].wait()
     coef = dot(v_local, sources[...])
-    send_ref[...] = coef[: coarse + rank_cap]
-    keep_ref[...] = coef[coarse + rank_cap :]
-
-
-def order_kernel(dev_bits, ranks_ref, perm_ref, sources_ref, v_ref, ordered_ref, near_far_ref, select):
-    level_count, rank_cap, row_count = v_ref.shape
-    fill_select(select, local_positions(perm_ref, row_count))
-    ordered_ref[...] = dot(select[...], sources_ref[...]).astype(BF16)
-    iota = lax.broadcasted_iota(jnp.int32, (rank_cap, 1), 0)
-    row = 0
-    for level in range(dev_bits, level_count):
-        cluster = row_count >> level - dev_bits + 1
-        keep = iota < ranks_ref[level]
-        for group in range(row_count // cluster):
-            at = slice(group * cluster, (group + 1) * cluster)
-            coef = dot(v_ref[level, :, at], ordered_ref[at, :])
-            other = row + (group ^ 1) * rank_cap
-            near_far_ref[other : other + rank_cap, :] = jnp.where(keep, coef, 0.0).astype(BF16)
-        row += row_count // cluster * rank_cap
-
-
-def leaf_kernel(dev_bits, perm_ref, leaf_ref, u_ref, left_ref, u_far_ref, select_t):
+    split = coarse + rank_cap
+    send_ref[...] = coef[:split]
+    keep_ref[...] = coef[split : split + coarse]
+    near_far_ref[...] = coef[split + coarse :].astype(BF16)
+    copies[4].wait()
+
+
+def basis_kernel(dev_bits, perm_ref, u_ref, select_t, u_far_ref):
     level_count, rank_cap, row_count = u_ref.shape
     half = rank_cap // 2
     coarse = (dev_bits - 1) * half
-    leaf_size = leaf_ref.shape[1]
-    core = lax.rem(lax.axis_index("col"), 2)
+    core = half_index(dev_bits)
     fill_select_t(select_t, local_positions(perm_ref, row_count))
-    for leaf in range(row_count // leaf_size):
-        at = slice(leaf * leaf_size, (leaf + 1) * leaf_size)
-        left_ref[:, at] = dot(select_t[:, at], leaf_ref[at, :]).astype(BF16)
     rows = []
     for start in (core * half, (1 - core) * half):
         for level in range(dev_bits - 1):
@@ -125,6 +135,18 @@
             part = dot_t(select_t[:, at], u_ref[level, :, at])
             u_far_ref[:, column : column + rank_cap] = part.astype(BF16)
             column += rank_cap
+
+
+def leaf_kernel(perm_ref, select_t, leaf_ref, left_ref, select):
+    row_count, leaf_size = leaf_ref.shape
+    for leaf in range(row_count // leaf_size):
+        at = slice(leaf * leaf_size, (leaf + 1) * leaf_size)
+        left_ref[:, at] = dot(select_t[:, at], leaf_ref[at, :]).astype(BF16)
+    fill_select(select, local_positions(perm_ref, row_count))
+
+
+def order_kernel(select_ref, sources_ref, ordered_ref):
+    ordered_ref[...] = dot(select_ref[...], sources_ref[...]).astype(BF16)
 
 
 def near_kernel(left_ref, ordered_ref, near_ref):
@@ -167,34 +189,52 @@
 
 
 def exchange(send, keep, half, dev_bits):
-    count = 1 << dev_bits
+    top = dev_bits - 1
     coarse = keep.shape[0]
-    first = lax.rem(lax.axis_index("col"), 2) == 1
-
-    def crossed(x, bits):
-        return lax.ppermute(x, AXES, [(i, i ^ 1 << bits[i & 1]) for i in range(count)])
-
-    received = partner(send, 0)
-    running = keep + received[:coarse]
-    first_received = received
-    received = crossed(running, (2, 1))
-    met = received[-2 * half : -half]
-    summed = running[:-half] + received[:-half]
-    one = received[-half:]
-    again = jnp.where(first, summed[-half:], met)
-    running = jnp.concatenate([summed[:-half], again, running[-half:]], axis=0)
-    received = crossed(running, (1, 2))
-    far = [
-        received[-2 * half : -half] + jnp.where(first, 0.0, met),
-        jnp.where(first, one, received[-half:]),
-    ]
-    running = running[: -2 * half] + received[: -2 * half]
-    for bit in range(3, dev_bits):
-        received = partner(running, bit)
-        far.insert(0, received[-half:])
-        running = running[:-half] + received[:-half]
+    second = half_index(dev_bits) == 1
+
+    first = core_swap(send, dev_bits)
+    running = keep + first[:coarse]
+
+    def add_unless(drop, own, received):
+        if drop == (False, False):
+            return own + received
+        if drop == (True, True):
+            return received
+        return received + jnp.where(second if drop[1] else jnp.logical_not(second), 0.0, own)
+
+    def settle(own, arrived, step):
+        if step == 1:
+            met.append(arrived[-half:])
+            last = add_unless((True, False), own[-2 * half : -half], arrived[-2 * half : -half])
+            return jnp.concatenate([own[: -2 * half] + arrived[: -2 * half], last, own[-half:]], axis=0)
+        if step == 2:
+            far[top - 1] = jnp.where(second, met[0], arrived[-half:])
+            far[top - 2] = add_unless((False, True), own[-2 * half : -half], arrived[-2 * half : -half])
+            return own[: -2 * half] + arrived[: -2 * half]
+        far[top - step] = arrived[-half:]
+        return own[:-half] + arrived[:-half]
+
+    met = []
+    head, rest = running[:half], running[half:]
+    far = [None] * top
+    straight = list(range(3, top - 1))
+    head_bits = list(zip([2, 1] + straight + [top, top - 1], [1, 2] + straight + [top - 1, top]))
+    rest_bits = [(2, 1), (1, 2)] + [(bit, bit) for bit in range(3, top)]
+    arriving = None
+    for step in range(top):
+        bits = head_bits[step]
+        received = chip_swap(head, dev_bits, bits)
+        if arriving is not None:
+            rest = settle(rest, arriving, step)
+        if step < top - 1:
+            arriving = chip_swap(rest, dev_bits, rest_bits[step])
+        head = add_unless((bits[0] == top, bits[1] == top), head, received)
+        if step < top - 1:
+            _, arriving = lax.optimization_barrier((head, arriving))
+    far[0] = head
     mine = jnp.concatenate(far, axis=0)
-    return mine, partner(mine, 0), first_received
+    return mine, core_swap(mine, dev_bits), first
 
 
 def per_device(sources, tree_perm, leaf_blocks, u_factors, v_factors, level_ranks):
@@ -212,47 +252,59 @@
     def in_hbm(x):
         return pltpu.with_memory_space_constraint(x, pltpu.HBM)
 
-    perm = tree_perm.reshape(perm_shape)
-    send, keep = pl.pallas_call(
+    send, keep, near_far, perm, u_in = pl.pallas_call(
         functools.partial(coef_kernel, dev_bits),
-        out_shape=(like((coarse + rank_cap, rhs_count), F32), like((coarse, rhs_count), F32)),
-        in_specs=[HBM] * 4,
-        out_specs=(VMEM,) * 2,
+        out_shape=(
+            like((coarse + rank_cap, rhs_count), F32),
+            like((coarse, rhs_count), F32),
+            like((near_rows, rhs_count), BF16),
+            like(perm_shape, jnp.int32),
+            like(u_factors.shape, BF16),
+        ),
+        in_specs=[HBM] * 5,
+        out_specs=(VMEM,) * 5,
         scratch_shapes=[
             pltpu.VMEM((row_count, row_count), BF16),
             pltpu.VMEM(sources.shape, BF16),
             pltpu.VMEM(v_factors.shape, BF16),
-            pltpu.VMEM(perm_shape, jnp.int32),
             pltpu.SMEM((level_count,), jnp.int32),
-            pltpu.VMEM((total, row_count), BF16),
-            pltpu.SemaphoreType.DMA((4,)),
+            pltpu.VMEM((total + near_rows, row_count), BF16),
+            pltpu.SemaphoreType.DMA((5,)),
         ],
         compiler_params=params(16),
         cost_estimate=cost(2 * total * row_count * (row_count + rhs_count), 2 << 20),
         name="coef",
-    )(in_hbm(level_ranks), in_hbm(perm), in_hbm(v_factors), in_hbm(sources))
-
-    ordered, near_far = pl.pallas_call(
-        functools.partial(order_kernel, dev_bits),
-        out_shape=(like(sources.shape, BF16), like((near_rows, rhs_count), BF16)),
-        in_specs=[SMEM] + [VMEM] * 3,
+    )(*map(in_hbm, (level_ranks, tree_perm.reshape(perm_shape), v_factors, sources, u_factors)))
+
+    select_t, u_far = pl.pallas_call(
+        functools.partial(basis_kernel, dev_bits),
+        out_shape=(like((row_count, row_count), BF16), like((row_count, total + near_rows), BF16)),
+        in_specs=[VMEM] * 2,
         out_specs=(VMEM,) * 2,
-        scratch_shapes=[pltpu.VMEM((row_count, row_count), BF16)],
+        compiler_params=params(16),
+        cost_estimate=cost(2 * row_count * row_count * total, 3 << 20),
+        name="basis",
+    )(perm, u_in)
+
+    left, select = pl.pallas_call(
+        leaf_kernel,
+        out_shape=(like((row_count, row_count), BF16),) * 2,
+        in_specs=[VMEM] * 3,
+        out_specs=(VMEM,) * 2,
+        compiler_params=params(16),
+        cost_estimate=cost(2 * row_count * row_count * leaf_size, 4 << 20),
+        name="leaf",
+    )(perm, select_t, leaf_blocks)
+
+    ordered = pl.pallas_call(
+        order_kernel,
+        out_shape=like(sources.shape, BF16),
+        in_specs=[VMEM] * 2,
+        out_specs=VMEM,
         compiler_params=params(16),
         cost_estimate=cost(2 * row_count * row_count * rhs_count, 2 << 20),
         name="order",
-    )(level_ranks, perm, sources, v_factors)
-
-    left, u_far = pl.pallas_call(
-        functools.partial(leaf_kernel, dev_bits),
-        out_shape=(like((row_count, row_count), BF16), like((row_count, total + near_rows), BF16)),
-        in_specs=[VMEM] * 3,
-        out_specs=(VMEM,) * 2,
-        scratch_shapes=[pltpu.VMEM((row_count, row_count), BF16)],
-        compiler_params=params(16),
-        cost_estimate=cost(2 * row_count * row_count * (leaf_size + total), 4 << 20),
-        name="leaf",
-    )(perm, leaf_blocks, u_factors)
+    )(select, sources)
 
     near = pl.pallas_call(
         near_kernel,

time: 31.9 us -> 35.1 us (1.10)
  local copies, waits for them, and re-layouts: 0.05 us -> 5.06 us
  waiting for transfers between devices: 9.73 us -> 4.88 us
  other arithmetic: 0.1 us -> 2.52 us
  starting transfers between devices: 11 us -> 11.8 us
    ppermute x6 -> x9, waiting for transfers between devices: 9.73 us -> 4.88 us  [the longest x7 3.74 us: chip_swap(): return lax.ppermute(x, AXES, pairs)]
    unnamed x12 -> x18, local copies, waits for them, and re-layouts: 0.04 us -> 4.4 us
    add x5 -> x7, other arithmetic: 0.07 us -> 2.5 us  [the longest x1 0.87 us: settle(): own[:-2 * half] + arrived[:-2 * half]]
    ppermute x6 -> x9, starting transfers between devices: 11 us -> 11.8 us  [the longest x7 11.1 us: chip_swap(): return lax.ppermute(x, AXES, pairs)]
    slice x2, local copies, waits for them, and re-layouts: 0.01 us -> 0.66 us  [exchange(): head, rest = (running[:half], running[half:])]
    pallas_call x2 -> x3, Pallas kernels: 5.22 us -> 4.61 us  [the longest x1 1.78 us: per_device(): pl.pallas_call(order_kernel, out_shape=like(sources.shape, BF16), in_spec...]
  transfers between devices with their start and end apart: 6 -> 9, of which waited for: 4 -> 3; matrix products, arithmetic and copies ran while one was open for 0% -> 9% of each run, Pallas kernels for 22% -> 18%
where the time goes in v3:
time: 35.1 us; the launch traced here: 34.8 us
  starting transfers between devices  11.8 us (34%)
  Pallas kernels  10.4 us (30%)
  local copies, waits for them, and re-layouts  5.06 us (14%)
  waiting for transfers between devices  4.88 us (14%)
  other arithmetic  2.52 us (7%)
    ppermute x7, starting transfers between devices, chip_swap(): return lax.ppermute(x, AXES, pairs)  11.1 us
    unnamed x18, local copies, waits for them, and re-layouts  4.4 us
    ppermute x7, waiting for transfers between devices, chip_swap(): return lax.ppermute(x, AXES, pairs)  3.74 us
    pallas_call x1, Pallas kernels, per_device(): pl.pallas_call(functools.partial(coef_kernel, dev_bits), out_shape=(like(...  2.62 us
    pallas_call x1, Pallas kernels, per_device(): pl.pallas_call(near_kernel, out_shape=like((row_count, rhs_count), F32),...  1.79 us
    pallas_call x1, Pallas kernels, per_device(): pl.pallas_call(order_kernel, out_shape=like(sources.shape, BF16), in_spec...  1.78 us
    pallas_call x1, Pallas kernels, per_device(): pl.pallas_call(leaf_kernel, out_shape=(like((row_count, row_count), BF16)...  1.53 us
    pallas_call x1, Pallas kernels, per_device(): pl.pallas_call(functools.partial(far_kernel, block), out_shape=like((row_...  1.39 us
  transfers between devices with their start and end apart: 9, of which 3 were waited for; matrix products, arithmetic and copies ran while one was open for 9% of the time, Pallas kernels for 18%

profile of v3, /device:TPU:0, one launch (start us, length us, event | category | flops | bytes accessed | tf_op | source)
XLA Modules:
  0.0 34.8 jit_solution(840413872075804473)
XLA Ops:
  0.0 2.6 %coef.1 = (f32[96,640]{1,0:T(8,128)S(1)}, f32[64,640]{1,0:T(8,128)S(1)}, bf16[64,640]{1,0:T(8,128)(2,1)S(1)}, s32[8,128]{1,0:T(8,128)S(1)}, bf16[6,32,1024]{2,1,0:T(8,128)(2,1)S(1)}) custom-call(s32[6]{0:T(128)} %ranks_hbm.1, s32[8,128]{1,0:T(8,128)} %bitcast.1, bf16[6,32,1024]{2,1,0:T(8,128)(2,1)} %v_hbm.1, bf16[1024,640]{1,0:T(8,128)(2,1)} %sources_ref.1, ...), custom_call_target="tpu_custom_call" | custom-call | flops 545259520 | bytes 2097152 | tf_op jit(solution)/shard_map/coef/pallas_call | solution.py:255
  2.6 0.6 %collective-permute-start = (f32[96,640]{1,0:T(8,128)S(1)}, f32[96,640]{1,0:T(8,128)S(1)}, u32[]{:S(2)}, u32[]{:S(2)}) collective-permute-start(f32[96,640]{1,0:T(8,128)S(1)} %get-tuple-element.24), channel_id=1, source_target_pairs={{0,1},{1,0},{2,3},{3,2},{4,5},{5,4},{6,7},{7,6},{8,9},{9,8},{10,11... | collective-permute-start | bytes 737288 | tf_op jit(solution)/shard_map/ppermute | solution.py:27
  3.2 1.1 %collective-permute-done.first_ref = f32[96,640]{1,0:T(8,128)S(1)} collective-permute-done((f32[96,640]{1,0:T(8,128)S(1)}, f32[96,640]{1,0:T(8,128)S(1)}, u32[]{:S(2)}, u32[]{:S(2)}) %collective-permute-start) | collective-permute-done | bytes 245792 | tf_op jit(solution)/shard_map/ppermute | solution.py:27
  4.4 0.7 %copy-done.1 = f32[96,640]{1,0:T(8,128)} copy-done((f32[96,640]{1,0:T(8,128)}, f32[96,640]{1,0:T(8,128)S(1)}, u32[]{:S(2)}) %copy-start.1) | copy-done | bytes 245784
  5.0 2.6 %collective-permute-start.1 = (f32[16,640]{1,0:T(8,128)S(1)}, f32[16,640]{1,0:T(8,128)S(1)}, u32[]{:S(2)}, u32[]{:S(2)}) collective-permute-start(f32[16,640]{1,0:T(8,128)S(1)} %slice.52), channel_id=1, source_target_pairs={{0,5},{1,2},{2,1},{3,6},{4,7},{5,0},{6,3},{7,4},{8,11},{9,12},{10,... | collective-permute-start | bytes 122888 | tf_op jit(solution)/shard_map/ppermute | solution.py:32
  7.7 1.3 %basis.1 = (bf16[1024,1024]{1,0:T(8,128)(2,1)S(1)}, bf16[1024,224]{1,0:T(8,128)(2,1)S(1)}) custom-call(s32[8,128]{1,0:T(8,128)S(1)} %get-tuple-element.17.perm_ref, bf16[6,32,1024]{2,1,0:T(8,128)(2,1)S(1)} %get-tuple-element.18.u_ref), custom_call_target="tpu_custom_call" | custom-call | flops 335544320 | bytes 3145728 | tf_op jit(solution)/shard_map/basis/pallas_call | solution.py:279
  9.0 0.8 %copy-done.3 = bf16[1024,224]{1,0:T(8,128)(2,1)} copy-done((bf16[1024,224]{1,0:T(8,128)(2,1)}, bf16[1024,224]{1,0:T(8,128)(2,1)S(1)}, u32[]{:S(2)}) %copy-start.3) | copy-done | bytes 458776
  9.8 0.7 %slice.54 = f32[48,640]{1,0:T(8,128)} slice(f32[64,640]{1,0:T(8,128)S(1)} %slice_add_fusion), slice={[16:64], [0:640]} | slice | bytes 245760 | tf_op jit(solution)/shard_map/slice | solution.py:219
  10.4 1.8 %collective-permute-start.2 = (f32[16,640]{1,0:T(8,128)S(1)}, f32[16,640]{1,0:T(8,128)}, u32[]{:S(2)}, u32[]{:S(2)}) collective-permute-start(f32[16,640]{1,0:T(8,128)S(1)} %slice_add_fusion.3), channel_id=1, source_target_pairs={{0,3},{1,4},{2,7},{3,0},{4,1},{5,6},{6,5},{7,2},{8,13},{9,10},{10,... | collective-permute-start | bytes 122888 | tf_op jit(solution)/shard_map/ppermute | solution.py:32
  12.2 1.5 %leaf.1 = (bf16[1024,1024]{1,0:T(8,128)(2,1)S(1)}, bf16[1024,1024]{1,0:T(8,128)(2,1)S(1)}) custom-call(s32[8,128]{1,0:T(8,128)S(1)} %get-tuple-element.17.perm_ref, bf16[1024,1024]{1,0:T(8,128)(2,1)S(1)} %get-tuple-element.19.select_t, bf16[1024,512]{1,0:T(8,128)(2,1)S(1)} %copy-done.5), custom_call_target="tpu_custom_call" | custom-call | flops 1073741824 | bytes 4194304 | tf_op jit(solution)/shard_map/leaf/pallas_call | solution.py:289
  13.8 1.3 %copy-done.6 = bf16[1024,1024]{1,0:T(8,128)(2,1)} copy-done((bf16[1024,1024]{1,0:T(8,128)(2,1)}, bf16[1024,1024]{1,0:T(8,128)(2,1)S(1)}, u32[]{:S(2)}) %copy-start.6) | copy-done | bytes 2097176
  15.1 0.8 %add.32 = f32[16,640]{1,0:T(8,128)S(1)} add(f32[16,640]{1,0:T(8,128)S(1)} %slice_add_fusion.3, f32[16,640]{1,0:T(8,128)} %collective-permute-done.2) | non-fusion elementwise | flops 10240 | bytes 122880 | tf_op jit(solution)/shard_map/add | solution.py:201
  15.9 2.6 %collective-permute-start.3 = (f32[16,640]{1,0:T(8,128)S(1)}, f32[16,640]{1,0:T(8,128)S(1)}, u32[]{:S(2)}, u32[]{:S(2)}) collective-permute-start(f32[16,640]{1,0:T(8,128)S(1)} %add.32), channel_id=1, source_target_pairs={{0,17},{1,8},{2,11},{3,18},{4,13},{5,20},{6,23},{7,14},{8,1},{9,24... | collective-permute-start | bytes 122888 | tf_op jit(solution)/shard_map/ppermute | solution.py:32
  18.5 0.9 %slice_add_fusion.1 = (f32[16,640]{1,0:T(8,128)S(1)}, f32[16,640]{1,0:T(8,128)S(1)}, f32[16,640]{1,0:T(8,128)S(1)}) fusion(f32[64,640]{1,0:T(8,128)} %copy-done.8, f32[48,640]{1,0:T(8,128)} %collective-permute-done.5, pred[]{:T(512)S(6)} %not.4), kind=kLoop, calls=%fused_computation.5 | loop fusion | flops 30720 | bytes 327681 | tf_op jit(solution)/shard_map/add | solution.py:210
  19.4 1.1 %collective-permute-start.6 = (f32[48,640]{1,0:T(8,128)S(1)}, f32[48,640]{1,0:T(8,128)S(1)}, u32[]{:S(2)}, u32[]{:S(2)}) collective-permute-start(f32[48,640]{1,0:T(8,128)S(1)} %pad_maximum_fusion.1), channel_id=1, source_target_pairs={{0,3},{1,4},{2,7},{3,0},{4,1},{5,6},{6,5},{7,2},{8,13},{9,10},{10,... | collective-permute-start | bytes 368648 | tf_op jit(solution)/shard_map/ppermute | solution.py:32
  20.5 1.4 %collective-permute-start.4 = (f32[16,640]{1,0:T(8,128)S(1)}, f32[16,640]{1,0:T(8,128)S(1)}, u32[]{:S(2)}, u32[]{:S(2)}) collective-permute-start(f32[16,640]{1,0:T(8,128)S(1)} %select_add_fusion.2), channel_id=1, source_target_pairs={{0,9},{1,16},{2,19},{3,10},{4,21},{5,12},{6,15},{7,22},{8,25},{9,0... | collective-permute-start | bytes 122888 | tf_op jit(solution)/shard_map/ppermute | solution.py:32
  21.9 1.9 %collective-permute-done.6 = f32[48,640]{1,0:T(8,128)S(1)} collective-permute-done((f32[48,640]{1,0:T(8,128)S(1)}, f32[48,640]{1,0:T(8,128)S(1)}, u32[]{:S(2)}, u32[]{:S(2)}) %collective-permute-start.6) | collective-permute-done | bytes 122912 | tf_op jit(solution)/shard_map/ppermute | solution.py:32
  23.7 0.8 %slice_add_fusion.2 = (f32[16,640]{1,0:T(8,128)S(1)}, f32[16,640]{1,0:T(8,128)S(1)}, f32[16,640]{1,0:T(8,128)S(1)}) fusion(f32[16,640]{1,0:T(8,128)S(1)} %get-tuple-element.29, f32[48,640]{1,0:T(8,128)S(1)} %collective-permute-done.6, f32[48,640]{1,0:T(8,128)} %collective-permute-done.5, pred[]{:T(512)S(6)} %eq.3, f32[16,640]{1,0:T(8,128)S(1)} %get-tuple-element.30), kind=kLoop, calls=%fused_computation.8 | loop fusion | flops 40960 | bytes 368641 | tf_op jit(solution)/shard_map/add | solution.py:214
  24.5 1.7 %collective-permute-start.7 = (f32[16,640]{1,0:T(8,128)S(1)}, f32[16,640]{1,0:T(8,128)S(1)}, u32[]{:S(2)}, u32[]{:S(2)}) collective-permute-start(f32[16,640]{1,0:T(8,128)S(1)} %get-tuple-element.32), channel_id=1, source_target_pairs={{0,9},{1,8},{2,11},{3,10},{4,13},{5,12},{6,15},{7,14},{8,1},{9,0},... | collective-permute-start | bytes 122888 | tf_op jit(solution)/shard_map/ppermute | solution.py:32
  26.2 1.9 %collective-permute-done.7 = f32[16,640]{1,0:T(8,128)S(1)} collective-permute-done((f32[16,640]{1,0:T(8,128)S(1)}, f32[16,640]{1,0:T(8,128)S(1)}, u32[]{:S(2)}, u32[]{:S(2)}) %collective-permute-start.7) | collective-permute-done | bytes 40992 | tf_op jit(solution)/shard_map/ppermute | solution.py:32
  28.2 1.6 %copy-done.7 = bf16[1024,1024]{1,0:T(8,128)(2,1)S(1)} copy-done((bf16[1024,1024]{1,0:T(8,128)(2,1)S(1)}, bf16[1024,1024]{1,0:T(8,128)(2,1)}, u32[]{:S(2)}) %copy-start.7) | copy-done | bytes 2097176
  29.8 1.8 %order.1.ordered_ref = bf16[1024,640]{1,0:T(8,128)(2,1)S(1)} custom-call(bf16[1024,1024]{1,0:T(8,128)(2,1)S(1)} %copy-done.7, bf16[1024,640]{1,0:T(8,128)(2,1)S(1)} %copy-done), custom_call_target="tpu_custom_call" | custom-call | flops 1342177280 | bytes 2097152 | tf_op jit(solution)/shard_map/order/pallas_call | solution.py:299
  31.6 1.8 %near.1.near_ref = f32[1024,640]{1,0:T(8,128)S(1)} custom-call(bf16[1024,1024]{1,0:T(8,128)(2,1)S(1)} %get-tuple-element.20.left_ref, bf16[1024,640]{1,0:T(8,128)(2,1)S(1)} %order.1.ordered_ref), custom_call_target="tpu_custom_call" | custom-call | flops 1342177280 | bytes 6291456 | tf_op jit(solution)/shard_map/near/pallas_call | solution.py:309
  33.4 1.4 %far.1 = bf16[1024,640]{1,0:T(8,128)(2,1)} custom-call(f32[1024,640]{1,0:T(8,128)S(1)} %near.1.near_ref, bf16[1024,224]{1,0:T(8,128)(2,1)S(1)} %copy-done.4, f32[64,640]{1,0:T(8,128)S(1)} %pad_maximum_fusion.mine_ref, f32[64,640]{1,0:T(8,128)S(1)} %collective-permute-done.8.other_ref, f32[96,640]{1,0:T(8,128)S(1)} %copy-done.2, ...), custom_call_target="tpu_custom_call" | custom-call | flops 209715200 | bytes 5242880 | tf_op jit(solution)/shard_map/far/pallas_call | solution.py:322
  (29 shorter events, 0.2 us)
Async XLA Ops:
  0.0 12.2 %copy-start.5 = (bf16[1024,512]{1,0:T(8,128)(2,1)S(1)}, bf16[1024,512]{1,0:T(8,128)(2,1)}, u32[]{:S(2)}) copy-start(bf16[1024,512]{1,0:T(8,128)(2,1)} %leaf_ref.1) | copy-start | bytes 3145732
  2.6 1.7 %collective-permute-start = (f32[96,640]{1,0:T(8,128)S(1)}, f32[96,640]{1,0:T(8,128)S(1)}, u32[]{:S(2)}, u32[]{:S(2)}) collective-permute-start(f32[96,640]{1,0:T(8,128)S(1)} %get-tuple-element.24), channel_id=1, source_target_pairs={{0,1},{1,0},{2,3},{3,2},{4,5},{5,4},{6,7},{7,6},{8,9},{9,8},{10,11... | collective-permute-start | bytes 737288 | tf_op jit(solution)/shard_map/ppermute | solution.py:27
  4.3 0.7 %copy-start.1 = (f32[96,640]{1,0:T(8,128)}, f32[96,640]{1,0:T(8,128)S(1)}, u32[]{:S(2)}) copy-start(f32[96,640]{1,0:T(8,128)S(1)} %collective-permute-done.first_ref) | copy-start | bytes 737284
  5.0 7.2 %copy-start.8 = (f32[64,640]{1,0:T(8,128)}, f32[64,640]{1,0:T(8,128)S(1)}, u32[]{:S(2)}) copy-start(f32[64,640]{1,0:T(8,128)S(1)} %slice_add_fusion) | copy-start | bytes 491524
  5.0 5.4 %collective-permute-start.1 = (f32[16,640]{1,0:T(8,128)S(1)}, f32[16,640]{1,0:T(8,128)S(1)}, u32[]{:S(2)}, u32[]{:S(2)}) collective-permute-start(f32[16,640]{1,0:T(8,128)S(1)} %slice.52), channel_id=1, source_target_pairs={{0,5},{1,2},{2,1},{3,6},{4,7},{5,0},{6,3},{7,4},{8,11},{9,12},{10,... | collective-permute-start | bytes 122888 | tf_op jit(solution)/shard_map/ppermute | solution.py:32
  9.0 0.8 %copy-start.3 = (bf16[1024,224]{1,0:T(8,128)(2,1)}, bf16[1024,224]{1,0:T(8,128)(2,1)S(1)}, u32[]{:S(2)}) copy-start(bf16[1024,224]{1,0:T(8,128)(2,1)S(1)} %get-tuple-element.22.u_far_ref) | copy-start | bytes 1376260
  10.4 8.0 %collective-permute-start.5 = (f32[48,640]{1,0:T(8,128)}, f32[48,640]{1,0:T(8,128)}, u32[]{:S(2)}, u32[]{:S(2)}) collective-permute-start(f32[48,640]{1,0:T(8,128)} %slice.54), channel_id=1, source_target_pairs={{0,5},{1,2},{2,1},{3,6},{4,7},{5,0},{6,3},{7,4},{8,11},{9,12},{10,... | collective-permute-start | bytes 368648 | tf_op jit(solution)/shard_map/ppermute | solution.py:32
  10.4 4.7 %collective-permute-start.2 = (f32[16,640]{1,0:T(8,128)S(1)}, f32[16,640]{1,0:T(8,128)}, u32[]{:S(2)}, u32[]{:S(2)}) collective-permute-start(f32[16,640]{1,0:T(8,128)S(1)} %slice_add_fusion.3), channel_id=1, source_target_pairs={{0,3},{1,4},{2,7},{3,0},{4,1},{5,6},{6,5},{7,2},{8,13},{9,10},{10,... | collective-permute-start | bytes 122888 | tf_op jit(solution)/shard_map/ppermute | solution.py:32
  12.2 15.9 %copy-start = (bf16[1024,640]{1,0:T(8,128)(2,1)S(1)}, bf16[1024,640]{1,0:T(8,128)(2,1)}, u32[]{:S(2)}) copy-start(bf16[1024,640]{1,0:T(8,128)(2,1)} %sources_ref.1) | copy-start | bytes 3932164
  13.8 1.3 %copy-start.6 = (bf16[1024,1024]{1,0:T(8,128)(2,1)}, bf16[1024,1024]{1,0:T(8,128)(2,1)S(1)}, u32[]{:S(2)}) copy-start(bf16[1024,1024]{1,0:T(8,128)(2,1)S(1)} %get-tuple-element.21.select_ref) | copy-start | bytes 6291460
  15.9 4.6 %collective-permute-start.3 = (f32[16,640]{1,0:T(8,128)S(1)}, f32[16,640]{1,0:T(8,128)S(1)}, u32[]{:S(2)}, u32[]{:S(2)}) collective-permute-start(f32[16,640]{1,0:T(8,128)S(1)} %add.32), channel_id=1, source_target_pairs={{0,17},{1,8},{2,11},{3,18},{4,13},{5,20},{6,23},{7,14},{8,1},{9,24... | collective-permute-start | bytes 122888 | tf_op jit(solution)/shard_map/ppermute | solution.py:32
  19.4 4.4 %collective-permute-start.6 = (f32[48,640]{1,0:T(8,128)S(1)}, f32[48,640]{1,0:T(8,128)S(1)}, u32[]{:S(2)}, u32[]{:S(2)}) collective-permute-start(f32[48,640]{1,0:T(8,128)S(1)} %pad_maximum_fusion.1), channel_id=1, source_target_pairs={{0,3},{1,4},{2,7},{3,0},{4,1},{5,6},{6,5},{7,2},{8,13},{9,10},{10,... | collective-permute-start | bytes 368648 | tf_op jit(solution)/shard_map/ppermute | solution.py:32
  20.5 5.7 %collective-permute-start.4 = (f32[16,640]{1,0:T(8,128)S(1)}, f32[16,640]{1,0:T(8,128)S(1)}, u32[]{:S(2)}, u32[]{:S(2)}) collective-permute-start(f32[16,640]{1,0:T(8,128)S(1)} %select_add_fusion.2), channel_id=1, source_target_pairs={{0,9},{1,16},{2,19},{3,10},{4,21},{5,12},{6,15},{7,22},{8,25},{9,0... | collective-permute-start | bytes 122888 | tf_op jit(solution)/shard_map/ppermute | solution.py:32
  24.5 3.5 %collective-permute-start.7 = (f32[16,640]{1,0:T(8,128)S(1)}, f32[16,640]{1,0:T(8,128)S(1)}, u32[]{:S(2)}, u32[]{:S(2)}) collective-permute-start(f32[16,640]{1,0:T(8,128)S(1)} %get-tuple-element.32), channel_id=1, source_target_pairs={{0,9},{1,8},{2,11},{3,10},{4,13},{5,12},{6,15},{7,14},{8,1},{9,0},... | collective-permute-start | bytes 122888 | tf_op jit(solution)/shard_map/ppermute | solution.py:32
  28.1 5.3 %collective-permute-start.8 = (f32[64,640]{1,0:T(8,128)S(1)}, f32[64,640]{1,0:T(8,128)S(1)}, u32[]{:S(2)}, u32[]{:S(2)}) collective-permute-start(f32[64,640]{1,0:T(8,128)S(1)} %pad_maximum_fusion.mine_ref), channel_id=1, source_target_pairs={{0,1},{1,0},{2,3},{3,2},{4,5},{5,4},{6,7},{7,6},{8,9},{9,8},{10,11... | collective-permute-start | bytes 491528 | tf_op jit(solution)/shard_map/ppermute | solution.py:27
  28.2 1.6 %copy-start.7 = (bf16[1024,1024]{1,0:T(8,128)(2,1)S(1)}, bf16[1024,1024]{1,0:T(8,128)(2,1)}, u32[]{:S(2)}) copy-start(bf16[1024,1024]{1,0:T(8,128)(2,1)} %copy-done.6) | copy-start | bytes 6291460
  31.6 1.8 %copy-start.2 = (f32[96,640]{1,0:T(8,128)S(1)}, f32[96,640]{1,0:T(8,128)}, u32[]{:S(2)}) copy-start(f32[96,640]{1,0:T(8,128)} %copy-done.1) | copy-start | bytes 737284
  31.6 1.8 %copy-start.4 = (bf16[1024,224]{1,0:T(8,128)(2,1)S(1)}, bf16[1024,224]{1,0:T(8,128)(2,1)}, u32[]{:S(2)}) copy-start(bf16[1024,224]{1,0:T(8,128)(2,1)} %copy-done.3) | copy-start | bytes 1376260

commit v4 on v3

--- a/solution.py
+++ b/solution.py
@@ -32,25 +32,35 @@
     return lax.ppermute(x, AXES, pairs)
 
 
-def local_positions(perm_ref, row_count):
-    return lax.rem(perm_ref[...], row_count)
-
-
-def fill_select(select_ref, index):
+def local_positions(perm_ref, row_count, start=0, stop=None):
+    blocks, width = perm_ref.shape
+    stop = blocks * width if stop is None else stop
+    return lax.rem(perm_ref[start // width : stop // width, :], row_count)
+
+
+def fill_select(select_ref, index, row_count):
     blocks, width = index.shape
     columns = index.T
-    lane = lax.broadcasted_iota(jnp.int32, (width, blocks * width), 1)
+    lane = lax.broadcasted_iota(jnp.int32, (width, row_count), 1)
     for block in range(blocks):
         hit = lane == columns[:, block : block + 1]
         select_ref[block * width : (block + 1) * width, :] = jnp.where(hit, 1.0, 0.0).astype(BF16)
 
 
-def fill_select_t(select_ref, index):
+def fill_select_t(select_ref, index, row_count):
     blocks, width = index.shape
-    sublane = lax.broadcasted_iota(jnp.int32, (blocks * width, width), 0)
+    sublane = lax.broadcasted_iota(jnp.int32, (row_count, width), 0)
     for block in range(blocks):
         hit = sublane == index[block : block + 1, :]
         select_ref[:, block * width : (block + 1) * width] = jnp.where(hit, 1.0, 0.0).astype(BF16)
+
+
+def cluster_columns(row_count, depth):
+    cluster = row_count >> depth
+    column = lax.broadcasted_iota(jnp.int32, (1, row_count), 1)
+    return [
+        (column >= start) & (column < start + cluster) for start in range(0, row_count, cluster)
+    ]
 
 
 def dot(a, b):
@@ -83,7 +93,7 @@
         return jnp.where(iota + start < ranks[level], rows.astype(F32), 0.0).astype(BF16)
 
     copies[0].wait()
-    fill_select(select, local_positions(perm, row_count))
+    fill_select(select, local_positions(perm, row_count), row_count)
     copies[1].wait()
     copies[2].wait()
     for level in range(dev_bits - 1):
@@ -94,16 +104,12 @@
         at = coarse + part * half
         v_rows[at : at + half, :] = masked(dev_bits - 1, jnp.int32(part * half))
     row = 2 * coarse + rank_cap
-    column = lax.broadcasted_iota(jnp.int32, (1, row_count), 1)
     rank = lax.broadcasted_iota(jnp.int32, (rank_cap, 1), 0)
     for level in range(dev_bits, level_count):
-        cluster = row_count >> level - dev_bits + 1
-        groups = row_count // cluster
         rows = jnp.where(rank < ranks[level], v[level].astype(F32), 0.0)
-        for group in range(groups):
-            other = group ^ 1
-            inside = (column >= other * cluster) & (column < (other + 1) * cluster)
-            v_rows[row : row + rank_cap, :] = jnp.where(inside, rows, 0.0).astype(BF16)
+        clusters = cluster_columns(row_count, level - dev_bits + 1)
+        for group in range(len(clusters)):
+            v_rows[row : row + rank_cap, :] = jnp.where(clusters[group ^ 1], rows, 0.0).astype(BF16)
             row += rank_cap
     v_local = dot(v_rows[...], select[...]).astype(BF16)
     copies[3].wait()
@@ -115,42 +121,43 @@
     copies[4].wait()
 
 
-def basis_kernel(dev_bits, perm_ref, u_ref, select_t, u_far_ref):
+def basis_kernel(dev_bits, perm_ref, u_ref, u_far_ref, select_t):
     level_count, rank_cap, row_count = u_ref.shape
     half = rank_cap // 2
-    coarse = (dev_bits - 1) * half
     core = half_index(dev_bits)
-    fill_select_t(select_t, local_positions(perm_ref, row_count))
+    fill_select_t(select_t, local_positions(perm_ref, row_count), row_count)
     rows = []
     for start in (core * half, (1 - core) * half):
         for level in range(dev_bits - 1):
             rows.append(u_ref[level, pl.ds(pl.multiple_of(start, half), half), :])
     rows.append(u_ref[dev_bits - 1])
-    column = 2 * coarse + rank_cap
-    u_far_ref[:, :column] = dot_t(select_t[...], jnp.concatenate(rows, axis=0)).astype(BF16)
     for level in range(dev_bits, level_count):
-        cluster = row_count >> level - dev_bits + 1
-        for group in range(row_count // cluster):
-            at = slice(group * cluster, (group + 1) * cluster)
-            part = dot_t(select_t[:, at], u_ref[level, :, at])
-            u_far_ref[:, column : column + rank_cap] = part.astype(BF16)
-            column += rank_cap
-
-
-def leaf_kernel(perm_ref, select_t, leaf_ref, left_ref, select):
-    row_count, leaf_size = leaf_ref.shape
-    for leaf in range(row_count // leaf_size):
-        at = slice(leaf * leaf_size, (leaf + 1) * leaf_size)
-        left_ref[:, at] = dot(select_t[:, at], leaf_ref[at, :]).astype(BF16)
-    fill_select(select, local_positions(perm_ref, row_count))
-
-
-def order_kernel(select_ref, sources_ref, ordered_ref):
-    ordered_ref[...] = dot(select_ref[...], sources_ref[...]).astype(BF16)
-
-
-def near_kernel(left_ref, ordered_ref, near_ref):
-    near_ref[...] = dot(left_ref[...], ordered_ref[...])
+        for inside in cluster_columns(row_count, level - dev_bits + 1):
+            rows.append(jnp.where(inside, u_ref[level].astype(F32), 0.0).astype(BF16))
+    u_far_ref[...] = dot_t(select_t[...], jnp.concatenate(rows, axis=0)).astype(BF16)
+
+
+def order_kernel(start, stop, perm_ref, sources_ref, ordered_ref, select):
+    row_count = sources_ref.shape[0]
+    fill_select(select, local_positions(perm_ref, row_count, start, stop), row_count)
+    ordered_ref[...] = dot(select[...], sources_ref[...]).astype(BF16)
+
+
+def leaf_kernel(leaf, perm_ref, block_ref, left_ref, select_t):
+    row_count, leaf_size = block_ref.shape
+    start, stop = leaf * leaf_size, (leaf + 1) * leaf_size
+    fill_select_t(select_t, local_positions(perm_ref, row_count, start, stop), row_count)
+    left_ref[...] = dot(select_t[...], block_ref[start:stop, :]).astype(BF16)
+
+
+def near_kernel(leaves, pieces, *refs):
+    lefts, ordered, near_ref = refs[:leaves], refs[leaves:-1], refs[-1]
+    leaf_size = lefts[0].shape[1]
+    parts = []
+    for (start, stop), piece in zip(pieces, ordered):
+        at = slice(start % leaf_size, start % leaf_size + stop - start)
+        parts.append(dot(lefts[start // leaf_size][:, at], piece[...]))
+    near_ref[...] = sum(parts)
 
 
 def far_kernel(block, near_ref, u_far_ref, mine_ref, other_ref, first_ref, near_far_ref, out_ref, far, out, sems):
@@ -276,49 +283,61 @@
         name="coef",
     )(*map(in_hbm, (level_ranks, tree_perm.reshape(perm_shape), v_factors, sources, u_factors)))
 
-    select_t, u_far = pl.pallas_call(
+    u_far = pl.pallas_call(
         functools.partial(basis_kernel, dev_bits),
-        out_shape=(like((row_count, row_count), BF16), like((row_count, total + near_rows), BF16)),
+        out_shape=like((row_count, total + near_rows), BF16),
         in_specs=[VMEM] * 2,
-        out_specs=(VMEM,) * 2,
+        out_specs=VMEM,
+        scratch_shapes=[pltpu.VMEM((row_count, row_count), BF16)],
         compiler_params=params(16),
         cost_estimate=cost(2 * row_count * row_count * total, 3 << 20),
         name="basis",
     )(perm, u_in)
 
-    left, select = pl.pallas_call(
-        leaf_kernel,
-        out_shape=(like((row_count, row_count), BF16),) * 2,
-        in_specs=[VMEM] * 3,
-        out_specs=(VMEM,) * 2,
-        compiler_params=params(16),
-        cost_estimate=cost(2 * row_count * row_count * leaf_size, 4 << 20),
-        name="leaf",
-    )(perm, select_t, leaf_blocks)
-
-    ordered = pl.pallas_call(
-        order_kernel,
-        out_shape=like(sources.shape, BF16),
-        in_specs=[VMEM] * 2,
-        out_specs=VMEM,
-        compiler_params=params(16),
-        cost_estimate=cost(2 * row_count * row_count * rhs_count, 2 << 20),
-        name="order",
-    )(select, sources)
+    leaves = row_count // leaf_size
+    middle = row_count // 2
+    pieces = [(0, middle), (middle, middle + middle // 2), (middle + middle // 2, row_count)]
+    ordered, left = [], []
+    for start, stop in pieces:
+        ordered.append(
+            pl.pallas_call(
+                functools.partial(order_kernel, start, stop),
+                out_shape=like((stop - start, rhs_count), BF16),
+                in_specs=[VMEM] * 2,
+                out_specs=VMEM,
+                scratch_shapes=[pltpu.VMEM((stop - start, row_count), BF16)],
+                compiler_params=params(16),
+                cost_estimate=cost(2 * (stop - start) * row_count * rhs_count, 2 << 20),
+                name="order",
+            )(perm, sources)
+        )
+    for leaf in range(leaves):
+        left.append(
+            pl.pallas_call(
+                functools.partial(leaf_kernel, leaf),
+                out_shape=like((row_count, leaf_size), BF16),
+                in_specs=[VMEM] * 2,
+                out_specs=VMEM,
+                scratch_shapes=[pltpu.VMEM((row_count, leaf_size), BF16)],
+                compiler_params=params(16),
+                cost_estimate=cost(2 * row_count * leaf_size * leaf_size, 2 << 20),
+                name="leaf",
+            )(perm, leaf_blocks)
+        )
 
     near = pl.pallas_call(
-        near_kernel,
+        functools.partial(near_kernel, leaves, pieces),
         out_shape=like((row_count, rhs_count), F32),
-        in_specs=[VMEM] * 2,
+        in_specs=[VMEM] * (leaves + len(pieces)),
         out_specs=VMEM,
         compiler_params=params(16),
         cost_estimate=cost(2 * row_count * row_count * rhs_count, 6 << 20),
         name="near",
-    )(left, ordered)
+    )(*left, *ordered)
 
     mine, other, received = exchange(send, keep, half, dev_bits)
 
-    block = row_count // 4
+    block = row_count // 8
     return pl.pallas_call(
         functools.partial(far_kernel, block),
         out_shape=like((row_count, rhs_count), BF16),

time: 35.1 us -> 31.5 us (0.90)
  local copies, waits for them, and re-layouts: 5.06 us -> 2.45 us
  other arithmetic: 2.52 us -> 0.88 us
    unnamed x18 -> x20, local copies, waits for them, and re-layouts: 4.4 us -> 2.44 us
    ppermute x7, waiting for transfers between devices: 3.74 us -> 5.19 us  [chip_swap(): return lax.ppermute(x, AXES, pairs)]
    ppermute x2, waiting for transfers between devices: 1.14 us -> 0.01 us  [core_swap(): return lax.ppermute(x, AXES, [(i, i ^ 1) for i in range(1 << dev_bits)])]
    add x1, other arithmetic: 0.87 us -> 0.02 us  [settle(): own[:-2 * half] + arrived[:-2 * half]]
    add x1, other arithmetic: 0.8 us -> 0.02 us  [settle(): return own[:-2 * half] + arrived[:-2 * half]]
    slice x2, local copies, waits for them, and re-layouts: 0.66 us -> 0.01 us  [exchange(): head, rest = (running[:half], running[half:])]
    pallas_call x4 -> x7, Pallas kernels: 6.4 us -> 6.73 us  [the longest x3 2.55 us: per_device(): pl.pallas_call(functools.partial(order_kernel, start, stop), out_shape=li...]
  transfers between devices with their start and end apart: 9 -> 9, of which waited for: 3 -> 4; matrix products, arithmetic and copies ran while one was open for 9% -> 3% of each run, Pallas kernels for 18% -> 22%
where the time goes in v4:
time: 31.5 us; the launch traced here: 31.3 us
  starting transfers between devices  11.9 us (38%)
  Pallas kernels  10.7 us (34%)
  waiting for transfers between devices  5.19 us (16%)
  local copies, waits for them, and re-layouts  2.45 us (8%)
  other arithmetic  0.88 us (3%)
    ppermute x7, starting transfers between devices, chip_swap(): return lax.ppermute(x, AXES, pairs)  11.3 us
    ppermute x7, waiting for transfers between devices, chip_swap(): return lax.ppermute(x, AXES, pairs)  5.19 us
    pallas_call x1, Pallas kernels, per_device(): pl.pallas_call(functools.partial(coef_kernel, dev_bits), out_shape=(like(...  2.64 us
    pallas_call x3, Pallas kernels, per_device(): pl.pallas_call(functools.partial(order_kernel, start, stop), out_shape=li...  2.55 us
    unnamed x20, local copies, waits for them, and re-layouts  2.44 us
    pallas_call x1, Pallas kernels, per_device(): pl.pallas_call(functools.partial(near_kernel, leaves, pieces), out_shape=...  1.81 us
    pallas_call x2, Pallas kernels, per_device(): pl.pallas_call(functools.partial(leaf_kernel, leaf), out_shape=like((row_...  1.45 us
    pallas_call x1, Pallas kernels, per_device(): pl.pallas_call(functools.partial(far_kernel, block), out_shape=like((row_...  1.36 us
  transfers between devices with their start and end apart: 9, of which 4 were waited for; matrix products, arithmetic and copies ran while one was open for 3% of the time, Pallas kernels for 22%

profile of v4, /device:TPU:0, one launch (start us, length us, event | category | flops | bytes accessed | tf_op | source)
XLA Modules:
  0.0 31.3 jit_solution(15536089787171301938)
XLA Ops:
  0.0 2.6 %coef.1 = (f32[96,640]{1,0:T(8,128)S(1)}, f32[64,640]{1,0:T(8,128)S(1)}, bf16[64,640]{1,0:T(8,128)(2,1)S(1)}, s32[8,128]{1,0:T(8,128)S(1)}, bf16[6,32,1024]{2,1,0:T(8,128)(2,1)S(1)}) custom-call(s32[6]{0:T(128)} %ranks_hbm.1, s32[8,128]{1,0:T(8,128)} %bitcast.1, bf16[6,32,1024]{2,1,0:T(8,128)(2,1)} %v_hbm.1, bf16[1024,640]{1,0:T(8,128)(2,1)} %sources_ref.5, ...), custom_call_target="tpu_custom_call" | custom-call | flops 545259520 | bytes 2097152 | tf_op jit(solution)/shard_map/coef/pallas_call | solution.py:262
  2.7 0.7 %copy-done.6 = bf16[6,32,1024]{2,1,0:T(8,128)(2,1)} copy-done((bf16[6,32,1024]{2,1,0:T(8,128)(2,1)}, bf16[6,32,1024]{2,1,0:T(8,128)(2,1)S(1)}, u32[]{:S(2)}) %copy-start.6) | copy-done | bytes 393240
  3.4 0.5 %collective-permute-start = (f32[96,640]{1,0:T(8,128)S(1)}, f32[96,640]{1,0:T(8,128)S(1)}, u32[]{:S(2)}, u32[]{:S(2)}) collective-permute-start(f32[96,640]{1,0:T(8,128)S(1)} %get-tuple-element.16), channel_id=1, source_target_pairs={{0,1},{1,0},{2,3},{3,2},{4,5},{5,4},{6,7},{7,6},{8,9},{9,8},{10,11... | collective-permute-start | bytes 737288 | tf_op jit(solution)/shard_map/ppermute | solution.py:27
  3.9 1.1 %order.3.refs_2_ = bf16[512,640]{1,0:T(8,128)(2,1)S(1)} custom-call(s32[8,128]{1,0:T(8,128)S(1)} %get-tuple-element.13.perm_ref, bf16[1024,640]{1,0:T(8,128)(2,1)S(1)} %copy-done), custom_call_target="tpu_custom_call" | custom-call | flops 671088640 | bytes 2097152 | tf_op jit(solution)/shard_map/order/pallas_call | solution.py:303
  5.0 0.8 %copy-done.4 = bf16[512,640]{1,0:T(8,128)(2,1)} copy-done((bf16[512,640]{1,0:T(8,128)(2,1)}, bf16[512,640]{1,0:T(8,128)(2,1)S(1)}, u32[]{:S(2)}) %copy-start.4) | copy-done | bytes 655384
  5.9 0.6 %copy-done.2 = f32[96,640]{1,0:T(8,128)} copy-done((f32[96,640]{1,0:T(8,128)}, f32[96,640]{1,0:T(8,128)S(1)}, u32[]{:S(2)}) %copy-start.2) | copy-done | bytes 245784
  6.6 2.6 %collective-permute-start.1 = (f32[16,640]{1,0:T(8,128)S(1)}, f32[16,640]{1,0:T(8,128)}, u32[]{:S(2)}, u32[]{:S(2)}) collective-permute-start(f32[16,640]{1,0:T(8,128)S(1)} %slice.52), channel_id=1, source_target_pairs={{0,5},{1,2},{2,1},{3,6},{4,7},{5,0},{6,3},{7,4},{8,11},{9,12},{10,... | collective-permute-start | bytes 122888 | tf_op jit(solution)/shard_map/ppermute | solution.py:32
  9.2 0.7 %leaf.2.refs_0_ = bf16[1024,512]{1,0:T(8,128)(2,1)S(1)} custom-call(s32[8,128]{1,0:T(8,128)S(1)} %get-tuple-element.13.perm_ref, bf16[1024,512]{1,0:T(8,128)(2,1)S(1)} %copy-done.1), custom_call_target="tpu_custom_call" | custom-call | flops 536870912 | bytes 2097152 | tf_op jit(solution)/shard_map/leaf/pallas_call | solution.py:316
  9.9 0.7 %order.4.refs_3_ = bf16[256,640]{1,0:T(8,128)(2,1)S(1)} custom-call(s32[8,128]{1,0:T(8,128)S(1)} %get-tuple-element.13.perm_ref, bf16[1024,640]{1,0:T(8,128)(2,1)S(1)} %copy-done), custom_call_target="tpu_custom_call" | custom-call | flops 335544320 | bytes 2097152 | tf_op jit(solution)/shard_map/order/pallas_call | solution.py:303
  11.0 0.8 %slice_add_fusion.3 = f32[16,640]{1,0:T(8,128)S(1)} fusion(f32[16,640]{1,0:T(8,128)} %collective-permute-done.1, f32[64,640]{1,0:T(8,128)S(1)} %copy-done.9), kind=kLoop, calls=%fused_computation.11 | loop fusion | flops 10240 | bytes 122880 | tf_op jit(solution)/shard_map/add | solution.py:208
  11.8 1.7 %collective-permute-start.2 = (f32[16,640]{1,0:T(8,128)S(1)}, f32[16,640]{1,0:T(8,128)S(1)}, u32[]{:S(2)}, u32[]{:S(2)}) collective-permute-start(f32[16,640]{1,0:T(8,128)S(1)} %slice_add_fusion.3), channel_id=1, source_target_pairs={{0,3},{1,4},{2,7},{3,0},{4,1},{5,6},{6,5},{7,2},{8,13},{9,10},{10,... | collective-permute-start | bytes 122888 | tf_op jit(solution)/shard_map/ppermute | solution.py:32
  13.5 0.7 %leaf.3.refs_1_ = bf16[1024,512]{1,0:T(8,128)(2,1)S(1)} custom-call(s32[8,128]{1,0:T(8,128)S(1)} %get-tuple-element.13.perm_ref, bf16[1024,512]{1,0:T(8,128)(2,1)S(1)} %copy-done.1), custom_call_target="tpu_custom_call" | custom-call | flops 536870912 | bytes 2097152 | tf_op jit(solution)/shard_map/leaf/pallas_call | solution.py:316
  14.2 1.4 %collective-permute-done.2 = f32[16,640]{1,0:T(8,128)S(1)} collective-permute-done((f32[16,640]{1,0:T(8,128)S(1)}, f32[16,640]{1,0:T(8,128)S(1)}, u32[]{:S(2)}, u32[]{:S(2)}) %collective-permute-start.2) | collective-permute-done | bytes 40992 | tf_op jit(solution)/shard_map/ppermute | solution.py:32
  15.7 2.4 %collective-permute-start.3 = (f32[16,640]{1,0:T(8,128)S(1)}, f32[16,640]{1,0:T(8,128)S(1)}, u32[]{:S(2)}, u32[]{:S(2)}) collective-permute-start(f32[16,640]{1,0:T(8,128)S(1)} %add.32), channel_id=1, source_target_pairs={{0,17},{1,8},{2,11},{3,18},{4,13},{5,20},{6,23},{7,14},{8,1},{9,24... | collective-permute-start | bytes 122888 | tf_op jit(solution)/shard_map/ppermute | solution.py:32
  18.1 1.1 %collective-permute-start.6 = (f32[48,640]{1,0:T(8,128)S(1)}, f32[48,640]{1,0:T(8,128)S(1)}, u32[]{:S(2)}, u32[]{:S(2)}) collective-permute-start(f32[48,640]{1,0:T(8,128)S(1)} %pad_maximum_fusion.1), channel_id=1, source_target_pairs={{0,3},{1,4},{2,7},{3,0},{4,1},{5,6},{6,5},{7,2},{8,13},{9,10},{10,... | collective-permute-start | bytes 368648 | tf_op jit(solution)/shard_map/ppermute | solution.py:32
  19.2 0.8 %collective-permute-done.3 = f32[16,640]{1,0:T(8,128)S(1)} collective-permute-done((f32[16,640]{1,0:T(8,128)S(1)}, f32[16,640]{1,0:T(8,128)S(1)}, u32[]{:S(2)}, u32[]{:S(2)}) %collective-permute-start.3) | collective-permute-done | bytes 40992 | tf_op jit(solution)/shard_map/ppermute | solution.py:32
  20.0 1.7 %collective-permute-start.4 = (f32[16,640]{1,0:T(8,128)S(1)}, f32[16,640]{1,0:T(8,128)S(1)}, u32[]{:S(2)}, u32[]{:S(2)}) collective-permute-start(f32[16,640]{1,0:T(8,128)S(1)} %select_add_fusion.2), channel_id=1, source_target_pairs={{0,9},{1,16},{2,19},{3,10},{4,21},{5,12},{6,15},{7,22},{8,25},{9,0... | collective-permute-start | bytes 122888 | tf_op jit(solution)/shard_map/ppermute | solution.py:32
  21.7 0.8 %collective-permute-done.6 = f32[48,640]{1,0:T(8,128)S(1)} collective-permute-done((f32[48,640]{1,0:T(8,128)S(1)}, f32[48,640]{1,0:T(8,128)S(1)}, u32[]{:S(2)}, u32[]{:S(2)}) %collective-permute-start.6) | collective-permute-done | bytes 122912 | tf_op jit(solution)/shard_map/ppermute | solution.py:32
  22.5 1.6 %collective-permute-start.7 = (f32[16,640]{1,0:T(8,128)S(1)}, f32[16,640]{1,0:T(8,128)S(1)}, u32[]{:S(2)}, u32[]{:S(2)}) collective-permute-start(f32[16,640]{1,0:T(8,128)S(1)} %get-tuple-element.24), channel_id=1, source_target_pairs={{0,9},{1,8},{2,11},{3,10},{4,13},{5,12},{6,15},{7,14},{8,1},{9,0},... | collective-permute-start | bytes 122888 | tf_op jit(solution)/shard_map/ppermute | solution.py:32
  24.1 2.2 %collective-permute-done.7 = f32[16,640]{1,0:T(8,128)S(1)} collective-permute-done((f32[16,640]{1,0:T(8,128)S(1)}, f32[16,640]{1,0:T(8,128)S(1)}, u32[]{:S(2)}, u32[]{:S(2)}) %collective-permute-start.7) | collective-permute-done | bytes 40992 | tf_op jit(solution)/shard_map/ppermute | solution.py:32
  26.4 0.7 %order.5.refs_4_ = bf16[256,640]{1,0:T(8,128)(2,1)S(1)} custom-call(s32[8,128]{1,0:T(8,128)S(1)} %get-tuple-element.13.perm_ref, bf16[1024,640]{1,0:T(8,128)(2,1)S(1)} %copy-done), custom_call_target="tpu_custom_call" | custom-call | flops 335544320 | bytes 2097152 | tf_op jit(solution)/shard_map/order/pallas_call | solution.py:303
  27.2 0.9 %basis.1.u_far_ref = bf16[1024,224]{1,0:T(8,128)(2,1)S(1)} custom-call(s32[8,128]{1,0:T(8,128)S(1)} %get-tuple-element.13.perm_ref, bf16[6,32,1024]{2,1,0:T(8,128)(2,1)S(1)} %copy-done.7), custom_call_target="tpu_custom_call" | custom-call | flops 335544320 | bytes 3145728 | tf_op jit(solution)/shard_map/basis/pallas_call | solution.py:286
  28.1 1.8 %near.1.near_ref = f32[1024,640]{1,0:T(8,128)S(1)} custom-call(bf16[1024,512]{1,0:T(8,128)(2,1)S(1)} %leaf.2.refs_0_, bf16[1024,512]{1,0:T(8,128)(2,1)S(1)} %leaf.3.refs_1_, bf16[512,640]{1,0:T(8,128)(2,1)S(1)} %copy-done.5, bf16[256,640]{1,0:T(8,128)(2,1)S(1)} %order.4.refs_3_, bf16[256,640]{1,0:T(8,128)(2,1)S(1)} %order.5.refs_4_), custom_call_target="tpu_custom_call" | custom-call | flops 1342177280 | bytes 6291456 | tf_op jit(solution)/shard_map/near/pallas_call | solution.py:328
  30.0 1.4 %far.1 = bf16[1024,640]{1,0:T(8,128)(2,1)} custom-call(f32[1024,640]{1,0:T(8,128)S(1)} %near.1.near_ref, bf16[1024,224]{1,0:T(8,128)(2,1)S(1)} %basis.1.u_far_ref, f32[64,640]{1,0:T(8,128)S(1)} %pad_maximum_fusion.mine_ref, f32[64,640]{1,0:T(8,128)S(1)} %collective-permute-done.8.other_ref, f32[96,640]{1,0:T(8,128)S(1)} %copy-done.3, ...), custom_call_target="tpu_custom_call" | custom-call | flops 209715200 | bytes 5242880 | tf_op jit(solution)/shard_map/far/pallas_call | solution.py:341
  (34 shorter events, 0.6 us)
Async XLA Ops:
  0.0 3.9 %copy-start = (bf16[1024,640]{1,0:T(8,128)(2,1)S(1)}, bf16[1024,640]{1,0:T(8,128)(2,1)}, u32[]{:S(2)}) copy-start(bf16[1024,640]{1,0:T(8,128)(2,1)} %sources_ref.5) | copy-start | bytes 3932164
  2.6 0.8 %copy-start.6 = (bf16[6,32,1024]{2,1,0:T(8,128)(2,1)}, bf16[6,32,1024]{2,1,0:T(8,128)(2,1)S(1)}, u32[]{:S(2)}) copy-start(bf16[6,32,1024]{2,1,0:T(8,128)(2,1)S(1)} %get-tuple-element.14.u_ref) | copy-start | bytes 1179652
  3.4 2.5 %collective-permute-start = (f32[96,640]{1,0:T(8,128)S(1)}, f32[96,640]{1,0:T(8,128)S(1)}, u32[]{:S(2)}, u32[]{:S(2)}) collective-permute-start(f32[96,640]{1,0:T(8,128)S(1)} %get-tuple-element.16), channel_id=1, source_target_pairs={{0,1},{1,0},{2,3},{3,2},{4,5},{5,4},{6,7},{7,6},{8,9},{9,8},{10,11... | collective-permute-start | bytes 737288 | tf_op jit(solution)/shard_map/ppermute | solution.py:27
  3.9 5.3 %copy-start.1 = (bf16[1024,512]{1,0:T(8,128)(2,1)S(1)}, bf16[1024,512]{1,0:T(8,128)(2,1)}, u32[]{:S(2)}) copy-start(bf16[1024,512]{1,0:T(8,128)(2,1)} %block_ref.3) | copy-start | bytes 3145732
  5.0 0.8 %copy-start.4 = (bf16[512,640]{1,0:T(8,128)(2,1)}, bf16[512,640]{1,0:T(8,128)(2,1)S(1)}, u32[]{:S(2)}) copy-start(bf16[512,640]{1,0:T(8,128)(2,1)S(1)} %order.3.refs_2_) | copy-start | bytes 1966084
  5.9 0.7 %copy-start.2 = (f32[96,640]{1,0:T(8,128)}, f32[96,640]{1,0:T(8,128)S(1)}, u32[]{:S(2)}) copy-start(f32[96,640]{1,0:T(8,128)S(1)} %collective-permute-done.first_ref) | copy-start | bytes 737284
  5.9 3.3 %copy-start.8 = (f32[64,640]{1,0:T(8,128)}, f32[64,640]{1,0:T(8,128)S(1)}, u32[]{:S(2)}) copy-start(f32[64,640]{1,0:T(8,128)S(1)} %slice_add_fusion) | copy-start | bytes 491524
  6.6 4.4 %collective-permute-start.1 = (f32[16,640]{1,0:T(8,128)S(1)}, f32[16,640]{1,0:T(8,128)}, u32[]{:S(2)}, u32[]{:S(2)}) collective-permute-start(f32[16,640]{1,0:T(8,128)S(1)} %slice.52), channel_id=1, source_target_pairs={{0,5},{1,2},{2,1},{3,6},{4,7},{5,0},{6,3},{7,4},{8,11},{9,12},{10,... | collective-permute-start | bytes 122888 | tf_op jit(solution)/shard_map/ppermute | solution.py:32
  9.9 0.9 %copy-start.9 = (f32[64,640]{1,0:T(8,128)S(1)}, f32[64,640]{1,0:T(8,128)}, u32[]{:S(2)}) copy-start(f32[64,640]{1,0:T(8,128)} %copy-done.8) | copy-start | bytes 491524
  10.9 7.2 %collective-permute-start.5 = (f32[48,640]{1,0:T(8,128)S(1)}, f32[48,640]{1,0:T(8,128)S(1)}, u32[]{:S(2)}, u32[]{:S(2)}) collective-permute-start(f32[48,640]{1,0:T(8,128)S(1)} %slice.54), channel_id=1, source_target_pairs={{0,5},{1,2},{2,1},{3,6},{4,7},{5,0},{6,3},{7,4},{8,11},{9,12},{10,... | collective-permute-start | bytes 368648 | tf_op jit(solution)/shard_map/ppermute | solution.py:32
  11.8 3.9 %collective-permute-start.2 = (f32[16,640]{1,0:T(8,128)S(1)}, f32[16,640]{1,0:T(8,128)S(1)}, u32[]{:S(2)}, u32[]{:S(2)}) collective-permute-start(f32[16,640]{1,0:T(8,128)S(1)} %slice_add_fusion.3), channel_id=1, source_target_pairs={{0,3},{1,4},{2,7},{3,0},{4,1},{5,6},{6,5},{7,2},{8,13},{9,10},{10,... | collective-permute-start | bytes 122888 | tf_op jit(solution)/shard_map/ppermute | solution.py:32
  15.7 4.3 %collective-permute-start.3 = (f32[16,640]{1,0:T(8,128)S(1)}, f32[16,640]{1,0:T(8,128)S(1)}, u32[]{:S(2)}, u32[]{:S(2)}) collective-permute-start(f32[16,640]{1,0:T(8,128)S(1)} %add.32), channel_id=1, source_target_pairs={{0,17},{1,8},{2,11},{3,18},{4,13},{5,20},{6,23},{7,14},{8,1},{9,24... | collective-permute-start | bytes 122888 | tf_op jit(solution)/shard_map/ppermute | solution.py:32
  18.1 9.1 %copy-start.7 = (bf16[6,32,1024]{2,1,0:T(8,128)(2,1)S(1)}, bf16[6,32,1024]{2,1,0:T(8,128)(2,1)}, u32[]{:S(2)}) copy-start(bf16[6,32,1024]{2,1,0:T(8,128)(2,1)} %copy-done.6) | copy-start | bytes 1179652
  18.1 4.4 %collective-permute-start.6 = (f32[48,640]{1,0:T(8,128)S(1)}, f32[48,640]{1,0:T(8,128)S(1)}, u32[]{:S(2)}, u32[]{:S(2)}) collective-permute-start(f32[48,640]{1,0:T(8,128)S(1)} %pad_maximum_fusion.1), channel_id=1, source_target_pairs={{0,3},{1,4},{2,7},{3,0},{4,1},{5,6},{6,5},{7,2},{8,13},{9,10},{10,... | collective-permute-start | bytes 368648 | tf_op jit(solution)/shard_map/ppermute | solution.py:32
  20.0 4.1 %collective-permute-start.4 = (f32[16,640]{1,0:T(8,128)S(1)}, f32[16,640]{1,0:T(8,128)S(1)}, u32[]{:S(2)}, u32[]{:S(2)}) collective-permute-start(f32[16,640]{1,0:T(8,128)S(1)} %select_add_fusion.2), channel_id=1, source_target_pairs={{0,9},{1,16},{2,19},{3,10},{4,21},{5,12},{6,15},{7,22},{8,25},{9,0... | collective-permute-start | bytes 122888 | tf_op jit(solution)/shard_map/ppermute | solution.py:32
  22.5 3.8 %collective-permute-start.7 = (f32[16,640]{1,0:T(8,128)S(1)}, f32[16,640]{1,0:T(8,128)S(1)}, u32[]{:S(2)}, u32[]{:S(2)}) collective-permute-start(f32[16,640]{1,0:T(8,128)S(1)} %get-tuple-element.24), channel_id=1, source_target_pairs={{0,9},{1,8},{2,11},{3,10},{4,13},{5,12},{6,15},{7,14},{8,1},{9,0},... | collective-permute-start | bytes 122888 | tf_op jit(solution)/shard_map/ppermute | solution.py:32
  26.4 1.8 %copy-start.5 = (bf16[512,640]{1,0:T(8,128)(2,1)S(1)}, bf16[512,640]{1,0:T(8,128)(2,1)}, u32[]{:S(2)}) copy-start(bf16[512,640]{1,0:T(8,128)(2,1)} %copy-done.4) | copy-start | bytes 1966084
  26.4 3.6 %collective-permute-start.8 = (f32[64,640]{1,0:T(8,128)S(1)}, f32[64,640]{1,0:T(8,128)S(1)}, u32[]{:S(2)}, u32[]{:S(2)}) collective-permute-start(f32[64,640]{1,0:T(8,128)S(1)} %pad_maximum_fusion.mine_ref), channel_id=1, source_target_pairs={{0,1},{1,0},{2,3},{3,2},{4,5},{5,4},{6,7},{7,6},{8,9},{9,8},{10,11... | collective-permute-start | bytes 491528 | tf_op jit(solution)/shard_map/ppermute | solution.py:27
  28.1 1.8 %copy-start.3 = (f32[96,640]{1,0:T(8,128)S(1)}, f32[96,640]{1,0:T(8,128)}, u32[]{:S(2)}) copy-start(f32[96,640]{1,0:T(8,128)} %copy-done.2) | copy-start | bytes 737284

commit v5 on v4

--- a/solution.py
+++ b/solution.py
@@ -40,26 +40,28 @@
 
 def fill_select(select_ref, index, row_count):
     blocks, width = index.shape
-    columns = index.T
-    lane = lax.broadcasted_iota(jnp.int32, (width, row_count), 1)
+    columns = index.T.astype(jnp.int16)
+    lane = lax.broadcasted_iota(jnp.int32, (width, row_count), 1).astype(jnp.int16)
     for block in range(blocks):
         hit = lane == columns[:, block : block + 1]
-        select_ref[block * width : (block + 1) * width, :] = jnp.where(hit, 1.0, 0.0).astype(BF16)
+        select_ref[block * width : (block + 1) * width, :] = jnp.where(hit, BF16(1), BF16(0))
 
 
 def fill_select_t(select_ref, index, row_count):
     blocks, width = index.shape
-    sublane = lax.broadcasted_iota(jnp.int32, (row_count, width), 0)
+    index = index.astype(jnp.int16)
+    sublane = lax.broadcasted_iota(jnp.int32, (row_count, width), 0).astype(jnp.int16)
     for block in range(blocks):
-        hit = sublane == index[block : block + 1, :]
-        select_ref[:, block * width : (block + 1) * width] = jnp.where(hit, 1.0, 0.0).astype(BF16)
+        hit = sublane == jnp.broadcast_to(index[block : block + 1, :], (row_count, width))
+        select_ref[:, block * width : (block + 1) * width] = jnp.where(hit, BF16(1), BF16(0))
 
 
 def cluster_columns(row_count, depth):
     cluster = row_count >> depth
     column = lax.broadcasted_iota(jnp.int32, (1, row_count), 1)
     return [
-        (column >= start) & (column < start + cluster) for start in range(0, row_count, cluster)
+        jnp.where((column >= start) & (column < start + cluster), 1.0, 0.0).astype(BF16)
+        for start in range(0, row_count, cluster)
     ]
 
 
@@ -72,7 +74,7 @@
 
 
 def coef_kernel(dev_bits, ranks_hbm, perm_hbm, v_hbm, sources_hbm, u_hbm,
-                send_ref, keep_ref, near_far_ref, perm, u,
+                send_ref, keep_ref, near_0_ref, near_1_ref, perm, u,
                 select, sources, v, ranks, v_rows, sems):
     copies = [
         pltpu.make_async_copy(source, target, sems.at[at])
@@ -90,7 +92,7 @@
 
     def masked(level, start):
         rows = v[level, pl.ds(pl.multiple_of(start, half), half), :]
-        return jnp.where(iota + start < ranks[level], rows.astype(F32), 0.0).astype(BF16)
+        return rows * jnp.where(iota + start < ranks[level], 1.0, 0.0).astype(BF16)
 
     copies[0].wait()
     fill_select(select, local_positions(perm, row_count), row_count)
@@ -106,10 +108,10 @@
     row = 2 * coarse + rank_cap
     rank = lax.broadcasted_iota(jnp.int32, (rank_cap, 1), 0)
     for level in range(dev_bits, level_count):
-        rows = jnp.where(rank < ranks[level], v[level].astype(F32), 0.0)
+        rows = v[level] * jnp.where(rank < ranks[level], 1.0, 0.0).astype(BF16)
         clusters = cluster_columns(row_count, level - dev_bits + 1)
         for group in range(len(clusters)):
-            v_rows[row : row + rank_cap, :] = jnp.where(clusters[group ^ 1], rows, 0.0).astype(BF16)
+            v_rows[row : row + rank_cap, :] = rows * clusters[group ^ 1]
             row += rank_cap
     v_local = dot(v_rows[...], select[...]).astype(BF16)
     copies[3].wait()
@@ -117,7 +119,9 @@
     split = coarse + rank_cap
     send_ref[...] = coef[:split]
     keep_ref[...] = coef[split : split + coarse]
-    near_far_ref[...] = coef[split + coarse :].astype(BF16)
+    near_half = split + coarse + (coef.shape[0] - split - coarse) // 2
+    near_0_ref[...] = coef[split + coarse : near_half]
+    near_1_ref[...] = coef[near_half:]
     copies[4].wait()
 
 
@@ -133,7 +137,7 @@
     rows.append(u_ref[dev_bits - 1])
     for level in range(dev_bits, level_count):
         for inside in cluster_columns(row_count, level - dev_bits + 1):
-            rows.append(jnp.where(inside, u_ref[level].astype(F32), 0.0).astype(BF16))
+            rows.append(u_ref[level] * inside)
     u_far_ref[...] = dot_t(select_t[...], jnp.concatenate(rows, axis=0)).astype(BF16)
 
 
@@ -154,19 +158,30 @@
     lefts, ordered, near_ref = refs[:leaves], refs[leaves:-1], refs[-1]
     leaf_size = lefts[0].shape[1]
     parts = []
-    for (start, stop), piece in zip(pieces, ordered):
-        at = slice(start % leaf_size, start % leaf_size + stop - start)
-        parts.append(dot(lefts[start // leaf_size][:, at], piece[...]))
+    for leaf in range(leaves):
+        first, last = leaf * leaf_size, (leaf + 1) * leaf_size
+        for (start, stop), piece in zip(pieces, ordered):
+            low, high = max(start, first), min(stop, last)
+            if low < high:
+                columns = slice(low - first, high - first)
+                parts.append(dot(lefts[leaf][:, columns], piece[low - start : high - start, :]))
     near_ref[...] = sum(parts)
 
 
-def far_kernel(block, near_ref, u_far_ref, mine_ref, other_ref, first_ref, near_far_ref, out_ref, far, out, sems):
+def round_kernel(coef_ref, rounded_ref):
+    rounded_ref[...] = coef_ref[...].astype(BF16)
+
+
+def far_kernel(block, near_ref, u_far_ref, mine_ref, other_ref, first_ref, near_0_ref, near_1_ref,
+               out_ref, far, out, sems):
     coarse = mine_ref.shape[0]
     rank_cap = first_ref.shape[0] - coarse
     far[:coarse, :] = mine_ref[...].astype(BF16)
     far[coarse : 2 * coarse, :] = other_ref[...].astype(BF16)
     far[2 * coarse : 2 * coarse + rank_cap, :] = first_ref[coarse:, :].astype(BF16)
-    far[2 * coarse + rank_cap :, :] = near_far_ref[...]
+    near_half = 2 * coarse + rank_cap + near_0_ref.shape[0]
+    far[2 * coarse + rank_cap : near_half, :] = near_0_ref[...]
+    far[near_half:, :] = near_1_ref[...]
     copies = []
     for step in range(near_ref.shape[0] // block):
         at = slice(step * block, (step + 1) * block)
@@ -259,17 +274,18 @@
     def in_hbm(x):
         return pltpu.with_memory_space_constraint(x, pltpu.HBM)
 
-    send, keep, near_far, perm, u_in = pl.pallas_call(
+    send, keep, *near_coef, perm, u_in = pl.pallas_call(
         functools.partial(coef_kernel, dev_bits),
         out_shape=(
             like((coarse + rank_cap, rhs_count), F32),
             like((coarse, rhs_count), F32),
-            like((near_rows, rhs_count), BF16),
+            like((near_rows // 2, rhs_count), F32),
+            like((near_rows // 2, rhs_count), F32),
             like(perm_shape, jnp.int32),
             like(u_factors.shape, BF16),
         ),
         in_specs=[HBM] * 5,
-        out_specs=(VMEM,) * 5,
+        out_specs=(VMEM,) * 6,
         scratch_shapes=[
             pltpu.VMEM((row_count, row_count), BF16),
             pltpu.VMEM(sources.shape, BF16),
@@ -295,8 +311,8 @@
     )(perm, u_in)
 
     leaves = row_count // leaf_size
-    middle = row_count // 2
-    pieces = [(0, middle), (middle, middle + middle // 2), (middle + middle // 2, row_count)]
+    cut = row_count * 3 // 4
+    pieces = [(0, cut), (cut, row_count)]
     ordered, left = [], []
     for start, stop in pieces:
         ordered.append(
@@ -335,13 +351,27 @@
         name="near",
     )(*left, *ordered)
 
+    rounded = []
+    for rows in near_coef:
+        rounded.append(
+            pl.pallas_call(
+                round_kernel,
+                out_shape=like(rows.shape, BF16),
+                in_specs=[VMEM],
+                out_specs=VMEM,
+                compiler_params=params(16),
+                cost_estimate=cost(rows.size, 6 * rows.size),
+                name="round",
+            )(rows)
+        )
+
     mine, other, received = exchange(send, keep, half, dev_bits)
 
     block = row_count // 8
     return pl.pallas_call(
         functools.partial(far_kernel, block),
         out_shape=like((row_count, rhs_count), BF16),
-        in_specs=[VMEM] * 6,
+        in_specs=[VMEM] * 7,
         out_specs=HBM,
         scratch_shapes=[
             pltpu.VMEM((total + near_rows, rhs_count), BF16),
@@ -351,7 +381,7 @@
         compiler_params=params(16),
         cost_estimate=cost(2 * row_count * total * rhs_count, 5 << 20),
         name="far",
-    )(near, u_far, mine, other, received, near_far)
+    )(near, u_far, mine, other, received, *rounded)
 
 
 def solution(mesh):

time: 31.5 us -> 28.4 us (0.902)
  local copies, waits for them, and re-layouts: 2.45 us -> 0.02 us
  waiting for transfers between devices: 5.19 us -> 6.02 us
  Pallas kernels: 10.7 us -> 9.91 us
  other arithmetic: 0.88 us -> 0.11 us
    unnamed x20 -> x4, local copies, waits for them, and re-layouts: 2.44 us -> 0.01 us
    ppermute x7, waiting for transfers between devices: 5.19 us -> 6.02 us  [chip_swap(): return lax.ppermute(x, AXES, pairs)]
    add x2, other arithmetic: 0.79 us -> 0.01 us  [add_unless(): return own + received]
    pallas_call x3 -> x2, Pallas kernels: 2.55 us -> 2.17 us  [per_device(): pl.pallas_call(functools.partial(order_kernel, start, stop), out_shape=li...]
  transfers between devices with their start and end apart: 9 -> 9, of which waited for: 4 -> 5; matrix products, arithmetic and copies ran while one was open for 3% -> 0% of each run, Pallas kernels for 22% -> 22%
where the time goes in v5:
time: 28.4 us; the launch traced here: 28.2 us
  starting transfers between devices  12 us (42%)
  Pallas kernels  9.91 us (35%)
  waiting for transfers between devices  6.02 us (21%)
    ppermute x7, starting transfers between devices, chip_swap(): return lax.ppermute(x, AXES, pairs)  11.4 us
    ppermute x7, waiting for transfers between devices, chip_swap(): return lax.ppermute(x, AXES, pairs)  6.02 us
    pallas_call x1, Pallas kernels, per_device(): pl.pallas_call(functools.partial(coef_kernel, dev_bits), out_shape=(like(...  2.33 us
    pallas_call x2, Pallas kernels, per_device(): pl.pallas_call(functools.partial(order_kernel, start, stop), out_shape=li...  2.17 us
    pallas_call x1, Pallas kernels, per_device(): pl.pallas_call(functools.partial(near_kernel, leaves, pieces), out_shape=...  1.81 us
    pallas_call x2, Pallas kernels, per_device(): pl.pallas_call(functools.partial(leaf_kernel, leaf), out_shape=like((row_...  1.44 us
    pallas_call x1, Pallas kernels, per_device(): pl.pallas_call(functools.partial(far_kernel, block), out_shape=like((row_...  1.36 us
    pallas_call x1, Pallas kernels, per_device(): pl.pallas_call(functools.partial(basis_kernel, dev_bits), out_shape=like(...  0.77 us
  transfers between devices with their start and end apart: 9, of which 5 were waited for; matrix products, arithmetic and copies ran while one was open for 0% of the time, Pallas kernels for 22%

profile of v5, /device:TPU:0, one launch (start us, length us, event | category | flops | bytes accessed | tf_op | source)
XLA Modules:
  0.0 28.2 jit_solution(1670382246420607041)
XLA Ops:
  0.0 2.3 %coef.1 = (f32[96,640]{1,0:T(8,128)S(1)}, f32[64,640]{1,0:T(8,128)S(1)}, f32[32,640]{1,0:T(8,128)S(1)}, f32[32,640]{1,0:T(8,128)S(1)}, s32[8,128]{1,0:T(8,128)S(1)}, /*index=5*/bf16[6,32,1024]{2,1,0:T(8,128)(2,1)S(1)}) custom-call(s32[6]{0:T(128)} %ranks_hbm.1, s32[8,128]{1,0:T(8,128)} %bitcast.1, bf16[6,32,1024]{2,1,0:T(8,128)(2,1)} %v_hbm.1, ...), custom_call_target="tpu_custom_call" | custom-call | flops 545259520 | bytes 2097152 | tf_op jit(solution)/shard_map/coef/pallas_call | solution.py:277
  2.3 0.6 %collective-permute-start = (f32[96,640]{1,0:T(8,128)S(1)}, f32[96,640]{1,0:T(8,128)S(1)}, u32[]{:S(2)}, u32[]{:S(2)}) collective-permute-start(f32[96,640]{1,0:T(8,128)S(1)} %get-tuple-element.17), channel_id=1, source_target_pairs={{0,1},{1,0},{2,3},{3,2},{4,5},{5,4},{6,7},{7,6},{8,9},{9,8},{10,11... | collective-permute-start | bytes 737288 | tf_op jit(solution)/shard_map/ppermute | solution.py:27
  2.9 1.5 %order.2.refs_2_ = bf16[768,640]{1,0:T(8,128)(2,1)S(1)} custom-call(s32[8,128]{1,0:T(8,128)S(1)} %get-tuple-element.14.perm_ref, bf16[1024,640]{1,0:T(8,128)(2,1)S(1)} %copy-done), custom_call_target="tpu_custom_call" | custom-call | flops 1006632960 | bytes 2097152 | tf_op jit(solution)/shard_map/order/pallas_call | solution.py:319
  4.5 2.7 %collective-permute-start.1 = (f32[16,640]{1,0:T(8,128)S(1)}, f32[16,640]{1,0:T(8,128)S(1)}, u32[]{:S(2)}, u32[]{:S(2)}) collective-permute-start(f32[16,640]{1,0:T(8,128)S(1)} %slice.52), channel_id=1, source_target_pairs={{0,5},{1,2},{2,1},{3,6},{4,7},{5,0},{6,3},{7,4},{8,11},{9,12},{10,... | collective-permute-start | bytes 122888 | tf_op jit(solution)/shard_map/ppermute | solution.py:32
  7.1 0.7 %leaf.2.refs_0_ = bf16[1024,512]{1,0:T(8,128)(2,1)S(1)} custom-call(s32[8,128]{1,0:T(8,128)S(1)} %get-tuple-element.14.perm_ref, bf16[1024,512]{1,0:T(8,128)(2,1)S(1)} %copy-done.1), custom_call_target="tpu_custom_call" | custom-call | flops 536870912 | bytes 2097152 | tf_op jit(solution)/shard_map/leaf/pallas_call | solution.py:332
  7.9 0.1 collective-permute-start.5
  8.0 0.8 %collective-permute-done.1 = f32[16,640]{1,0:T(8,128)S(1)} collective-permute-done((f32[16,640]{1,0:T(8,128)S(1)}, f32[16,640]{1,0:T(8,128)S(1)}, u32[]{:S(2)}, u32[]{:S(2)}) %collective-permute-start.1) | collective-permute-done | bytes 40992 | tf_op jit(solution)/shard_map/ppermute | solution.py:32
  8.8 2.0 %collective-permute-start.2 = (f32[16,640]{1,0:T(8,128)S(1)}, f32[16,640]{1,0:T(8,128)S(1)}, u32[]{:S(2)}, u32[]{:S(2)}) collective-permute-start(f32[16,640]{1,0:T(8,128)S(1)} %slice_add_fusion.3), channel_id=1, source_target_pairs={{0,3},{1,4},{2,7},{3,0},{4,1},{5,6},{6,5},{7,2},{8,13},{9,10},{10,... | collective-permute-start | bytes 122888 | tf_op jit(solution)/shard_map/ppermute | solution.py:32
  10.8 0.7 %leaf.3.refs_1_ = bf16[1024,512]{1,0:T(8,128)(2,1)S(1)} custom-call(s32[8,128]{1,0:T(8,128)S(1)} %get-tuple-element.14.perm_ref, bf16[1024,512]{1,0:T(8,128)(2,1)S(1)} %copy-done.1), custom_call_target="tpu_custom_call" | custom-call | flops 536870912 | bytes 2097152 | tf_op jit(solution)/shard_map/leaf/pallas_call | solution.py:332
  11.6 1.3 %collective-permute-done.2 = f32[16,640]{1,0:T(8,128)S(1)} collective-permute-done((f32[16,640]{1,0:T(8,128)S(1)}, f32[16,640]{1,0:T(8,128)S(1)}, u32[]{:S(2)}, u32[]{:S(2)}) %collective-permute-start.2) | collective-permute-done | bytes 40992 | tf_op jit(solution)/shard_map/ppermute | solution.py:32
  12.9 2.3 %collective-permute-start.3 = (f32[16,640]{1,0:T(8,128)S(1)}, f32[16,640]{1,0:T(8,128)S(1)}, u32[]{:S(2)}, u32[]{:S(2)}) collective-permute-start(f32[16,640]{1,0:T(8,128)S(1)} %add.32), channel_id=1, source_target_pairs={{0,17},{1,8},{2,11},{3,18},{4,13},{5,20},{6,23},{7,14},{8,1},{9,24... | collective-permute-start | bytes 122888 | tf_op jit(solution)/shard_map/ppermute | solution.py:32
  15.2 0.0 collective-permute-done.5
  15.2 1.1 %collective-permute-start.6 = (f32[48,640]{1,0:T(8,128)S(1)}, f32[48,640]{1,0:T(8,128)S(1)}, u32[]{:S(2)}, u32[]{:S(2)}) collective-permute-start(f32[48,640]{1,0:T(8,128)S(1)} %pad_maximum_fusion.1), channel_id=1, source_target_pairs={{0,3},{1,4},{2,7},{3,0},{4,1},{5,6},{6,5},{7,2},{8,13},{9,10},{10,... | collective-permute-start | bytes 368648 | tf_op jit(solution)/shard_map/ppermute | solution.py:32
  16.3 0.9 %collective-permute-done.3 = f32[16,640]{1,0:T(8,128)S(1)} collective-permute-done((f32[16,640]{1,0:T(8,128)S(1)}, f32[16,640]{1,0:T(8,128)S(1)}, u32[]{:S(2)}, u32[]{:S(2)}) %collective-permute-start.3) | collective-permute-done | bytes 40992 | tf_op jit(solution)/shard_map/ppermute | solution.py:32
  17.2 1.6 %collective-permute-start.4 = (f32[16,640]{1,0:T(8,128)S(1)}, f32[16,640]{1,0:T(8,128)S(1)}, u32[]{:S(2)}, u32[]{:S(2)}) collective-permute-start(f32[16,640]{1,0:T(8,128)S(1)} %select_add_fusion.2), channel_id=1, source_target_pairs={{0,9},{1,16},{2,19},{3,10},{4,21},{5,12},{6,15},{7,22},{8,25},{9,0... | collective-permute-start | bytes 122888 | tf_op jit(solution)/shard_map/ppermute | solution.py:32
  18.8 0.8 %collective-permute-done.6 = f32[48,640]{1,0:T(8,128)S(1)} collective-permute-done((f32[48,640]{1,0:T(8,128)S(1)}, f32[48,640]{1,0:T(8,128)S(1)}, u32[]{:S(2)}, u32[]{:S(2)}) %collective-permute-start.6) | collective-permute-done | bytes 122912 | tf_op jit(solution)/shard_map/ppermute | solution.py:32
  19.6 1.6 %collective-permute-start.7 = (f32[16,640]{1,0:T(8,128)S(1)}, f32[16,640]{1,0:T(8,128)S(1)}, u32[]{:S(2)}, u32[]{:S(2)}) collective-permute-start(f32[16,640]{1,0:T(8,128)S(1)} %get-tuple-element.26), channel_id=1, source_target_pairs={{0,9},{1,8},{2,11},{3,10},{4,13},{5,12},{6,15},{7,14},{8,1},{9,0},... | collective-permute-start | bytes 122888 | tf_op jit(solution)/shard_map/ppermute | solution.py:32
  21.2 0.0 collective-permute-done.4
  21.2 2.2 %collective-permute-done.7 = f32[16,640]{1,0:T(8,128)S(1)} collective-permute-done((f32[16,640]{1,0:T(8,128)S(1)}, f32[16,640]{1,0:T(8,128)S(1)}, u32[]{:S(2)}, u32[]{:S(2)}) %collective-permute-start.7) | collective-permute-done | bytes 40992 | tf_op jit(solution)/shard_map/ppermute | solution.py:32
  23.5 0.1 collective-permute-start.8
  23.5 0.7 %order.3.refs_3_ = bf16[256,640]{1,0:T(8,128)(2,1)S(1)} custom-call(s32[8,128]{1,0:T(8,128)S(1)} %get-tuple-element.14.perm_ref, bf16[1024,640]{1,0:T(8,128)(2,1)S(1)} %copy-done), custom_call_target="tpu_custom_call" | custom-call | flops 335544320 | bytes 2097152 | tf_op jit(solution)/shard_map/order/pallas_call | solution.py:319
  24.3 0.8 %basis.1.u_far_ref = bf16[1024,224]{1,0:T(8,128)(2,1)S(1)} custom-call(s32[8,128]{1,0:T(8,128)S(1)} %get-tuple-element.14.perm_ref, bf16[6,32,1024]{2,1,0:T(8,128)(2,1)S(1)} %get-tuple-element.15.u_ref), custom_call_target="tpu_custom_call" | custom-call | flops 335544320 | bytes 3145728 | tf_op jit(solution)/shard_map/basis/pallas_call | solution.py:302
  25.0 1.8 %near.1.near_ref = f32[1024,640]{1,0:T(8,128)S(1)} custom-call(bf16[1024,512]{1,0:T(8,128)(2,1)S(1)} %leaf.2.refs_0_, bf16[1024,512]{1,0:T(8,128)(2,1)S(1)} %leaf.3.refs_1_, bf16[768,640]{1,0:T(8,128)(2,1)S(1)} %order.2.refs_2_, bf16[256,640]{1,0:T(8,128)(2,1)S(1)} %order.3.refs_3_), custom_call_target="tpu_custom_call" | custom-call | flops 1342177280 | bytes 6291456 | tf_op jit(solution)/shard_map/near/pallas_call | solution.py:344
  26.9 1.4 %far.1 = bf16[1024,640]{1,0:T(8,128)(2,1)} custom-call(f32[1024,640]{1,0:T(8,128)S(1)} %near.1.near_ref, bf16[1024,224]{1,0:T(8,128)(2,1)S(1)} %basis.1.u_far_ref, f32[64,640]{1,0:T(8,128)S(1)} %pad_maximum_fusion.mine_ref, f32[64,640]{1,0:T(8,128)S(1)} %collective-permute-done.8.other_ref, f32[96,640]{1,0:T(8,128)S(1)} %collective-permute-done.first_ref, ...), custom_call_target="tpu_custom_call" | custom-call | flops 209715200 | bytes 5242880 | tf_op jit(solution)/shard_map/far/pallas_call | solution.py:371
  (19 shorter events, 0.1 us)
Async XLA Ops:
  0.0 2.9 %copy-start = (bf16[1024,640]{1,0:T(8,128)(2,1)S(1)}, bf16[1024,640]{1,0:T(8,128)(2,1)}, u32[]{:S(2)}) copy-start(bf16[1024,640]{1,0:T(8,128)(2,1)} %sources_ref.3) | copy-start | bytes 3932164
  2.3 2.1 %collective-permute-start = (f32[96,640]{1,0:T(8,128)S(1)}, f32[96,640]{1,0:T(8,128)S(1)}, u32[]{:S(2)}, u32[]{:S(2)}) collective-permute-start(f32[96,640]{1,0:T(8,128)S(1)} %get-tuple-element.17), channel_id=1, source_target_pairs={{0,1},{1,0},{2,3},{3,2},{4,5},{5,4},{6,7},{7,6},{8,9},{9,8},{10,11... | collective-permute-start | bytes 737288 | tf_op jit(solution)/shard_map/ppermute | solution.py:27
  2.9 4.2 %copy-start.1 = (bf16[1024,512]{1,0:T(8,128)(2,1)S(1)}, bf16[1024,512]{1,0:T(8,128)(2,1)}, u32[]{:S(2)}) copy-start(bf16[1024,512]{1,0:T(8,128)(2,1)} %block_ref.3) | copy-start | bytes 3145732
  4.5 4.4 %collective-permute-start.1 = (f32[16,640]{1,0:T(8,128)S(1)}, f32[16,640]{1,0:T(8,128)S(1)}, u32[]{:S(2)}, u32[]{:S(2)}) collective-permute-start(f32[16,640]{1,0:T(8,128)S(1)} %slice.52), channel_id=1, source_target_pairs={{0,5},{1,2},{2,1},{3,6},{4,7},{5,0},{6,3},{7,4},{8,11},{9,12},{10,... | collective-permute-start | bytes 122888 | tf_op jit(solution)/shard_map/ppermute | solution.py:32
  7.9 7.3 %collective-permute-start.5 = (f32[48,640]{1,0:T(8,128)S(1)}, f32[48,640]{1,0:T(8,128)S(1)}, u32[]{:S(2)}, u32[]{:S(2)}) collective-permute-start(f32[48,640]{1,0:T(8,128)S(1)} %slice.54), channel_id=1, source_target_pairs={{0,5},{1,2},{2,1},{3,6},{4,7},{5,0},{6,3},{7,4},{8,11},{9,12},{10,... | collective-permute-start | bytes 368648 | tf_op jit(solution)/shard_map/ppermute | solution.py:32
  8.8 4.1 %collective-permute-start.2 = (f32[16,640]{1,0:T(8,128)S(1)}, f32[16,640]{1,0:T(8,128)S(1)}, u32[]{:S(2)}, u32[]{:S(2)}) collective-permute-start(f32[16,640]{1,0:T(8,128)S(1)} %slice_add_fusion.3), channel_id=1, source_target_pairs={{0,3},{1,4},{2,7},{3,0},{4,1},{5,6},{6,5},{7,2},{8,13},{9,10},{10,... | collective-permute-start | bytes 122888 | tf_op jit(solution)/shard_map/ppermute | solution.py:32
  12.9 4.3 %collective-permute-start.3 = (f32[16,640]{1,0:T(8,128)S(1)}, f32[16,640]{1,0:T(8,128)S(1)}, u32[]{:S(2)}, u32[]{:S(2)}) collective-permute-start(f32[16,640]{1,0:T(8,128)S(1)} %add.32), channel_id=1, source_target_pairs={{0,17},{1,8},{2,11},{3,18},{4,13},{5,20},{6,23},{7,14},{8,1},{9,24... | collective-permute-start | bytes 122888 | tf_op jit(solution)/shard_map/ppermute | solution.py:32
  15.2 4.4 %collective-permute-start.6 = (f32[48,640]{1,0:T(8,128)S(1)}, f32[48,640]{1,0:T(8,128)S(1)}, u32[]{:S(2)}, u32[]{:S(2)}) collective-permute-start(f32[48,640]{1,0:T(8,128)S(1)} %pad_maximum_fusion.1), channel_id=1, source_target_pairs={{0,3},{1,4},{2,7},{3,0},{4,1},{5,6},{6,5},{7,2},{8,13},{9,10},{10,... | collective-permute-start | bytes 368648 | tf_op jit(solution)/shard_map/ppermute | solution.py:32
  17.2 4.0 %collective-permute-start.4 = (f32[16,640]{1,0:T(8,128)S(1)}, f32[16,640]{1,0:T(8,128)S(1)}, u32[]{:S(2)}, u32[]{:S(2)}) collective-permute-start(f32[16,640]{1,0:T(8,128)S(1)} %select_add_fusion.2), channel_id=1, source_target_pairs={{0,9},{1,16},{2,19},{3,10},{4,21},{5,12},{6,15},{7,22},{8,25},{9,0... | collective-permute-start | bytes 122888 | tf_op jit(solution)/shard_map/ppermute | solution.py:32
  19.6 3.8 %collective-permute-start.7 = (f32[16,640]{1,0:T(8,128)S(1)}, f32[16,640]{1,0:T(8,128)S(1)}, u32[]{:S(2)}, u32[]{:S(2)}) collective-permute-start(f32[16,640]{1,0:T(8,128)S(1)} %get-tuple-element.26), channel_id=1, source_target_pairs={{0,9},{1,8},{2,11},{3,10},{4,13},{5,12},{6,15},{7,14},{8,1},{9,0},... | collective-permute-start | bytes 122888 | tf_op jit(solution)/shard_map/ppermute | solution.py:32
  23.5 3.4 %collective-permute-start.8 = (f32[64,640]{1,0:T(8,128)S(1)}, f32[64,640]{1,0:T(8,128)S(1)}, u32[]{:S(2)}, u32[]{:S(2)}) collective-permute-start(f32[64,640]{1,0:T(8,128)S(1)} %pad_maximum_fusion.mine_ref), channel_id=1, source_target_pairs={{0,1},{1,0},{2,3},{3,2},{4,5},{5,4},{6,7},{7,6},{8,9},{9,8},{10,11... | collective-permute-start | bytes 491528 | tf_op jit(solution)/shard_map/ppermute | solution.py:27

commit v6 on v5

--- a/solution.py
+++ b/solution.py
@@ -74,7 +74,7 @@
 
 
 def coef_kernel(dev_bits, ranks_hbm, perm_hbm, v_hbm, sources_hbm, u_hbm,
-                send_ref, keep_ref, near_0_ref, near_1_ref, perm, u,
+                send_ref, keep_ref, v_close_ref, perm, u,
                 select, sources, v, ranks, v_rows, sems):
     copies = [
         pltpu.make_async_copy(source, target, sems.at[at])
@@ -91,7 +91,7 @@
     iota = lax.broadcasted_iota(jnp.int32, (half, 1), 0)
 
     def masked(level, start):
-        rows = v[level, pl.ds(pl.multiple_of(start, half), half), :]
+        rows = v[level, pl.ds(start if isinstance(start, int) else pl.multiple_of(start, half), half), :]
         return rows * jnp.where(iota + start < ranks[level], 1.0, 0.0).astype(BF16)
 
     copies[0].wait()
@@ -105,23 +105,15 @@
     for part in range(2):
         at = coarse + part * half
         v_rows[at : at + half, :] = masked(dev_bits - 1, jnp.int32(part * half))
-    row = 2 * coarse + rank_cap
-    rank = lax.broadcasted_iota(jnp.int32, (rank_cap, 1), 0)
+    v_local = dot(v_rows[...], select[...]).astype(BF16)
     for level in range(dev_bits, level_count):
-        rows = v[level] * jnp.where(rank < ranks[level], 1.0, 0.0).astype(BF16)
-        clusters = cluster_columns(row_count, level - dev_bits + 1)
-        for group in range(len(clusters)):
-            v_rows[row : row + rank_cap, :] = rows * clusters[group ^ 1]
-            row += rank_cap
-    v_local = dot(v_rows[...], select[...]).astype(BF16)
+        for part in range(2):
+            rows = slice(part * half, (part + 1) * half)
+            v_close_ref[level - dev_bits, rows, :] = masked(level, part * half)
     copies[3].wait()
     coef = dot(v_local, sources[...])
-    split = coarse + rank_cap
-    send_ref[...] = coef[:split]
-    keep_ref[...] = coef[split : split + coarse]
-    near_half = split + coarse + (coef.shape[0] - split - coarse) // 2
-    near_0_ref[...] = coef[split + coarse : near_half]
-    near_1_ref[...] = coef[near_half:]
+    send_ref[...] = coef[: coarse + rank_cap]
+    keep_ref[...] = coef[coarse + rank_cap :]
     copies[4].wait()
 
 
@@ -147,43 +139,51 @@
     ordered_ref[...] = dot(select[...], sources_ref[...]).astype(BF16)
 
 
-def leaf_kernel(leaf, perm_ref, block_ref, left_ref, select_t):
+def leaf_kernel(leaf, perm_ref, block_ref, v_close_ref, left_ref, select_t):
     row_count, leaf_size = block_ref.shape
-    start, stop = leaf * leaf_size, (leaf + 1) * leaf_size
-    fill_select_t(select_t, local_positions(perm_ref, row_count, start, stop), row_count)
-    left_ref[...] = dot(select_t[...], block_ref[start:stop, :]).astype(BF16)
-
-
-def near_kernel(leaves, pieces, *refs):
-    lefts, ordered, near_ref = refs[:leaves], refs[leaves:-1], refs[-1]
-    leaf_size = lefts[0].shape[1]
-    parts = []
-    for leaf in range(leaves):
-        first, last = leaf * leaf_size, (leaf + 1) * leaf_size
-        for (start, stop), piece in zip(pieces, ordered):
-            low, high = max(start, first), min(stop, last)
+    close_count, rank_cap, _ = v_close_ref.shape
+    at = slice(leaf * leaf_size, (leaf + 1) * leaf_size)
+    fill_select_t(select_t, local_positions(perm_ref, row_count, at.start, at.stop), row_count)
+    left_ref[:row_count, :] = dot(select_t[...], block_ref[at, :]).astype(BF16)
+    row = row_count
+    for level in range(close_count):
+        kept = v_close_ref[level, :, at]
+        cluster = row_count >> level + 1
+        for group in range(row_count // cluster):
+            other = group ^ 1
+            low = max(other * cluster, at.start) - at.start
+            high = min((other + 1) * cluster, at.stop) - at.start
+            if high - low < leaf_size:
+                left_ref[row : row + rank_cap, :] = jnp.zeros((rank_cap, leaf_size), BF16)
             if low < high:
-                columns = slice(low - first, high - first)
-                parts.append(dot(lefts[leaf][:, columns], piece[low - start : high - start, :]))
+                left_ref[row : row + rank_cap, low:high] = kept[:, low:high]
+            row += rank_cap
+
+
+def near_kernel(leaf, pieces, *refs):
+    left_ref, ordered, near_ref = refs[0], refs[1 : 1 + len(pieces)], refs[-1]
+    leaf_size = left_ref.shape[1]
+    first, last = leaf * leaf_size, (leaf + 1) * leaf_size
+    parts = [refs[-2][...]] if len(refs) == len(pieces) + 3 else []
+    for (start, stop), piece in zip(pieces, ordered):
+        low, high = max(start, first), min(stop, last)
+        parts.append(dot(left_ref[:, low - first : high - first], piece[low - start : high - start, :]))
     near_ref[...] = sum(parts)
 
 
-def round_kernel(coef_ref, rounded_ref):
-    rounded_ref[...] = coef_ref[...].astype(BF16)
-
-
-def far_kernel(block, near_ref, u_far_ref, mine_ref, other_ref, first_ref, near_0_ref, near_1_ref,
+def round_kernel(start, coef_ref, rounded_ref):
+    rounded_ref[...] = coef_ref[start : start + rounded_ref.shape[0], :].astype(BF16)
+
+
+def far_kernel(block, near_ref, u_far_ref, mine_ref, other_ref, sibling_0_ref, sibling_1_ref,
                out_ref, far, out, sems):
-    coarse = mine_ref.shape[0]
-    rank_cap = first_ref.shape[0] - coarse
-    far[:coarse, :] = mine_ref[...].astype(BF16)
-    far[coarse : 2 * coarse, :] = other_ref[...].astype(BF16)
-    far[2 * coarse : 2 * coarse + rank_cap, :] = first_ref[coarse:, :].astype(BF16)
-    near_half = 2 * coarse + rank_cap + near_0_ref.shape[0]
-    far[2 * coarse + rank_cap : near_half, :] = near_0_ref[...]
-    far[near_half:, :] = near_1_ref[...]
+    row = 0
+    row_count = out.shape[0]
+    for part in (mine_ref, other_ref, sibling_0_ref, sibling_1_ref, near_ref.at[row_count:, :]):
+        far[row : row + part.shape[0], :] = part[...].astype(BF16)
+        row += part.shape[0]
     copies = []
-    for step in range(near_ref.shape[0] // block):
+    for step in range(row_count // block):
         at = slice(step * block, (step + 1) * block)
         out[at, :] = (near_ref[at, :] + dot(u_far_ref[at, :], far[...])).astype(BF16)
         copy = pltpu.make_async_copy(out.at[at, :], out_ref.at[at, :], sems.at[step])
@@ -241,7 +241,7 @@
     head, rest = running[:half], running[half:]
     far = [None] * top
     straight = list(range(3, top - 1))
-    head_bits = list(zip([2, 1] + straight + [top, top - 1], [1, 2] + straight + [top - 1, top]))
+    head_bits = list(zip([2, 1] + straight + [top, top - 1], [1, 2] + straight + [top, top - 1]))
     rest_bits = [(2, 1), (1, 2)] + [(bit, bit) for bit in range(3, top)]
     arriving = None
     for step in range(top):
@@ -274,24 +274,23 @@
     def in_hbm(x):
         return pltpu.with_memory_space_constraint(x, pltpu.HBM)
 
-    send, keep, *near_coef, perm, u_in = pl.pallas_call(
+    send, keep, v_close, perm, u_in = pl.pallas_call(
         functools.partial(coef_kernel, dev_bits),
         out_shape=(
             like((coarse + rank_cap, rhs_count), F32),
             like((coarse, rhs_count), F32),
-            like((near_rows // 2, rhs_count), F32),
-            like((near_rows // 2, rhs_count), F32),
+            like((level_count - dev_bits, rank_cap, row_count), BF16),
             like(perm_shape, jnp.int32),
             like(u_factors.shape, BF16),
         ),
         in_specs=[HBM] * 5,
-        out_specs=(VMEM,) * 6,
+        out_specs=(VMEM,) * 5,
         scratch_shapes=[
             pltpu.VMEM((row_count, row_count), BF16),
             pltpu.VMEM(sources.shape, BF16),
             pltpu.VMEM(v_factors.shape, BF16),
             pltpu.SMEM((level_count,), jnp.int32),
-            pltpu.VMEM((total + near_rows, row_count), BF16),
+            pltpu.VMEM((total, row_count), BF16),
             pltpu.SemaphoreType.DMA((5,)),
         ],
         compiler_params=params(16),
@@ -331,47 +330,57 @@
         left.append(
             pl.pallas_call(
                 functools.partial(leaf_kernel, leaf),
-                out_shape=like((row_count, leaf_size), BF16),
-                in_specs=[VMEM] * 2,
+                out_shape=like((row_count + near_rows, leaf_size), BF16),
+                in_specs=[VMEM] * 3,
                 out_specs=VMEM,
                 scratch_shapes=[pltpu.VMEM((row_count, leaf_size), BF16)],
                 compiler_params=params(16),
                 cost_estimate=cost(2 * row_count * leaf_size * leaf_size, 2 << 20),
                 name="leaf",
-            )(perm, leaf_blocks)
+            )(perm, leaf_blocks, v_close)
         )
 
-    near = pl.pallas_call(
-        functools.partial(near_kernel, leaves, pieces),
-        out_shape=like((row_count, rhs_count), F32),
-        in_specs=[VMEM] * (leaves + len(pieces)),
-        out_specs=VMEM,
-        compiler_params=params(16),
-        cost_estimate=cost(2 * row_count * row_count * rhs_count, 6 << 20),
-        name="near",
-    )(*left, *ordered)
-
-    rounded = []
-    for rows in near_coef:
-        rounded.append(
+    near = None
+    for leaf in reversed(range(leaves)):
+        inside = [
+            number
+            for number, (start, stop) in enumerate(pieces)
+            if start < (leaf + 1) * leaf_size and stop > leaf * leaf_size
+        ]
+        operands = [left[leaf], *(ordered[number] for number in inside)]
+        operands += [] if near is None else [near]
+        near = pl.pallas_call(
+            functools.partial(near_kernel, leaf, [pieces[number] for number in inside]),
+            out_shape=like((row_count + near_rows, rhs_count), F32),
+            in_specs=[VMEM] * len(operands),
+            out_specs=VMEM,
+            input_output_aliases={} if near is None else {len(operands) - 1: 0},
+            compiler_params=params(16),
+            cost_estimate=cost(2 * row_count * leaf_size * rhs_count, 6 << 20),
+            name="near",
+        )(*operands)
+
+    mine, other, received = exchange(send, keep, half, dev_bits)
+
+    sibling = []
+    for number in range(2):
+        sibling.append(
             pl.pallas_call(
-                round_kernel,
-                out_shape=like(rows.shape, BF16),
+                functools.partial(round_kernel, coarse + number * half),
+                out_shape=like((half, rhs_count), BF16),
                 in_specs=[VMEM],
                 out_specs=VMEM,
                 compiler_params=params(16),
-                cost_estimate=cost(rows.size, 6 * rows.size),
+                cost_estimate=cost(half * rhs_count, 6 * half * rhs_count),
                 name="round",
-            )(rows)
+            )(received)
         )
-
-    mine, other, received = exchange(send, keep, half, dev_bits)
 
     block = row_count // 8
     return pl.pallas_call(
         functools.partial(far_kernel, block),
         out_shape=like((row_count, rhs_count), BF16),
-        in_specs=[VMEM] * 7,
+        in_specs=[VMEM] * 6,
         out_specs=HBM,
         scratch_shapes=[
             pltpu.VMEM((total + near_rows, rhs_count), BF16),
@@ -381,7 +390,7 @@
         compiler_params=params(16),
         cost_estimate=cost(2 * row_count * total * rhs_count, 5 << 20),
         name="far",
-    )(near, u_far, mine, other, received, *rounded)
+    )(near, u_far, mine, other, *sibling)
 
 
 def solution(mesh):

time: 28.4 us -> 29.3 us (1.032)
  waiting for transfers between devices: 6.02 us -> 7.14 us
  starting transfers between devices: 12 us -> 11.7 us
    ppermute x2, waiting for transfers between devices: 0.01 us -> 1.14 us  [core_swap(): return lax.ppermute(x, AXES, [(i, i ^ 1) for i in range(1 << dev_bits)])]
    ppermute x7, starting transfers between devices: 11.4 us -> 10.5 us  [chip_swap(): return lax.ppermute(x, AXES, pairs)]
    ppermute x2, starting transfers between devices: 0.65 us -> 1.21 us  [core_swap(): return lax.ppermute(x, AXES, [(i, i ^ 1) for i in range(1 << dev_bits)])]
    pallas_call x3 -> x4, Pallas kernels: 1.83 us -> 2.12 us  [the longest x2 2.1 us: per_device(): pl.pallas_call(functools.partial(near_kernel, leaf, [pieces[number] for n...]
  transfers between devices with their start and end apart: 9 -> 9, of which waited for: 5 -> 6; matrix products, arithmetic and copies ran while one was open for 0% -> 0% of each run, Pallas kernels for 22% -> 22%
where the time goes in v6:
time: 29.3 us; the launch traced here: 29.1 us
  starting transfers between devices  11.7 us (40%)
  Pallas kernels  10 us (34%)
  waiting for transfers between devices  7.14 us (24%)
    ppermute x7, starting transfers between devices, chip_swap(): return lax.ppermute(x, AXES, pairs)  10.5 us
    ppermute x7, waiting for transfers between devices, chip_swap(): return lax.ppermute(x, AXES, pairs)  6 us
    pallas_call x2, Pallas kernels, per_device(): pl.pallas_call(functools.partial(order_kernel, start, stop), out_shape=li...  2.17 us
    pallas_call x1, Pallas kernels, per_device(): pl.pallas_call(functools.partial(coef_kernel, dev_bits), out_shape=(like(...  2.11 us
    pallas_call x2, Pallas kernels, per_device(): pl.pallas_call(functools.partial(near_kernel, leaf, [pieces[number] for n...  2.1 us
    pallas_call x2, Pallas kernels, per_device(): pl.pallas_call(functools.partial(leaf_kernel, leaf), out_shape=like((row_...  1.45 us
    pallas_call x1, Pallas kernels, per_device(): pl.pallas_call(functools.partial(far_kernel, block), out_shape=like((row_...  1.38 us
    ppermute x2, starting transfers between devices, core_swap(): return lax.ppermute(x, AXES, [(i, i ^ 1) for i in range(1 << dev_bits)])  1.21 us
  transfers between devices with their start and end apart: 9, of which 6 were waited for; matrix products, arithmetic and copies ran while one was open for 0% of the time, Pallas kernels for 22%

profile of v6, /device:TPU:0, one launch (start us, length us, event | category | flops | bytes accessed | tf_op | source)
XLA Modules:
  0.0 29.1 jit_solution(3669423941544615166)
XLA Ops:
  0.0 2.1 %coef.1 = (f32[96,640]{1,0:T(8,128)S(1)}, f32[64,640]{1,0:T(8,128)S(1)}, bf16[1,32,1024]{2,1,0:T(8,128)(2,1)S(1)}, s32[8,128]{1,0:T(8,128)S(1)}, bf16[6,32,1024]{2,1,0:T(8,128)(2,1)S(1)}) custom-call(s32[6]{0:T(128)} %ranks_hbm.1, s32[8,128]{1,0:T(8,128)} %bitcast.1, bf16[6,32,1024]{2,1,0:T(8,128)(2,1)} %v_hbm.1, bf16[1024,640]{1,0:T(8,128)(2,1)} %sources_ref.3, ...), custom_call_target="tpu_custom_call" | custom-call | flops 545259520 | bytes 2097152 | tf_op jit(solution)/shard_map/coef/pallas_call | solution.py:277
  2.1 0.6 %collective-permute-start = (f32[96,640]{1,0:T(8,128)S(1)}, f32[96,640]{1,0:T(8,128)S(1)}, u32[]{:S(2)}, u32[]{:S(2)}) collective-permute-start(f32[96,640]{1,0:T(8,128)S(1)} %get-tuple-element.17), channel_id=1, source_target_pairs={{0,1},{1,0},{2,3},{3,2},{4,5},{5,4},{6,7},{7,6},{8,9},{9,8},{10,11... | collective-permute-start | bytes 737288 | tf_op jit(solution)/shard_map/ppermute | solution.py:27
  2.7 1.1 %collective-permute-done.coef_ref = f32[96,640]{1,0:T(8,128)S(1)} collective-permute-done((f32[96,640]{1,0:T(8,128)S(1)}, f32[96,640]{1,0:T(8,128)S(1)}, u32[]{:S(2)}, u32[]{:S(2)}) %collective-permute-start) | collective-permute-done | bytes 245792 | tf_op jit(solution)/shard_map/ppermute | solution.py:27
  3.9 2.7 %collective-permute-start.1 = (f32[16,640]{1,0:T(8,128)S(1)}, f32[16,640]{1,0:T(8,128)S(1)}, u32[]{:S(2)}, u32[]{:S(2)}) collective-permute-start(f32[16,640]{1,0:T(8,128)S(1)} %slice.52), channel_id=1, source_target_pairs={{0,5},{1,2},{2,1},{3,6},{4,7},{5,0},{6,3},{7,4},{8,11},{9,12},{10,... | collective-permute-start | bytes 122888 | tf_op jit(solution)/shard_map/ppermute | solution.py:32
  6.5 0.1 collective-permute-start.5
  6.6 1.6 %collective-permute-done.1 = f32[16,640]{1,0:T(8,128)S(1)} collective-permute-done((f32[16,640]{1,0:T(8,128)S(1)}, f32[16,640]{1,0:T(8,128)S(1)}, u32[]{:S(2)}, u32[]{:S(2)}) %collective-permute-start.1) | collective-permute-done | bytes 40992 | tf_op jit(solution)/shard_map/ppermute | solution.py:32
  8.2 2.0 %collective-permute-start.2 = (f32[16,640]{1,0:T(8,128)S(1)}, f32[16,640]{1,0:T(8,128)S(1)}, u32[]{:S(2)}, u32[]{:S(2)}) collective-permute-start(f32[16,640]{1,0:T(8,128)S(1)} %slice_add_fusion.3), channel_id=1, source_target_pairs={{0,3},{1,4},{2,7},{3,0},{4,1},{5,6},{6,5},{7,2},{8,13},{9,10},{10,... | collective-permute-start | bytes 122888 | tf_op jit(solution)/shard_map/ppermute | solution.py:32
  10.2 0.7 %collective-permute-done.5 = f32[48,640]{1,0:T(8,128)S(1)} collective-permute-done((f32[48,640]{1,0:T(8,128)S(1)}, f32[48,640]{1,0:T(8,128)S(1)}, u32[]{:S(2)}, u32[]{:S(2)}) %collective-permute-start.5) | collective-permute-done | bytes 122912 | tf_op jit(solution)/shard_map/ppermute | solution.py:32
  11.0 1.5 %collective-permute-start.6 = (f32[48,640]{1,0:T(8,128)S(1)}, f32[48,640]{1,0:T(8,128)S(1)}, u32[]{:S(2)}, u32[]{:S(2)}) collective-permute-start(f32[48,640]{1,0:T(8,128)S(1)} %pad_maximum_fusion.1), channel_id=1, source_target_pairs={{0,3},{1,4},{2,7},{3,0},{4,1},{5,6},{6,5},{7,2},{8,13},{9,10},{10,... | collective-permute-start | bytes 368648 | tf_op jit(solution)/shard_map/ppermute | solution.py:32
  12.5 1.5 %order.2.refs_1_ = bf16[768,640]{1,0:T(8,128)(2,1)S(1)} custom-call(s32[8,128]{1,0:T(8,128)S(1)} %get-tuple-element.13.perm_ref, bf16[1024,640]{1,0:T(8,128)(2,1)S(1)} %copy-done), custom_call_target="tpu_custom_call" | custom-call | flops 1006632960 | bytes 2097152 | tf_op jit(solution)/shard_map/order/pallas_call | solution.py:318
  14.0 2.4 %collective-permute-start.3 = (f32[16,640]{1,0:T(8,128)S(1)}, f32[16,640]{1,0:T(8,128)S(1)}, u32[]{:S(2)}, u32[]{:S(2)}) collective-permute-start(f32[16,640]{1,0:T(8,128)S(1)} %add.29), channel_id=1, source_target_pairs={{0,17},{1,16},{2,19},{3,18},{4,21},{5,20},{6,23},{7,22},{8,25},{9,... | collective-permute-start | bytes 122888 | tf_op jit(solution)/shard_map/ppermute | solution.py:32
  16.4 0.7 %leaf.2.refs_0_ = bf16[1088,512]{1,0:T(8,128)(2,1)S(1)} custom-call(s32[8,128]{1,0:T(8,128)S(1)} %get-tuple-element.13.perm_ref, bf16[1024,512]{1,0:T(8,128)(2,1)S(1)} %copy-done.1, bf16[1,32,1024]{2,1,0:T(8,128)(2,1)S(1)} %get-tuple-element.14.v_close_ref), custom_call_target="tpu_custom_call" | custom-call | flops 536870912 | bytes 2097152 | tf_op jit(solution)/shard_map/leaf/pallas_call | solution.py:331
  17.2 1.4 %collective-permute-done.3 = f32[16,640]{1,0:T(8,128)S(1)} collective-permute-done((f32[16,640]{1,0:T(8,128)S(1)}, f32[16,640]{1,0:T(8,128)S(1)}, u32[]{:S(2)}, u32[]{:S(2)}) %collective-permute-start.3) | collective-permute-done | bytes 40992 | tf_op jit(solution)/shard_map/ppermute | solution.py:32
  18.5 1.4 %collective-permute-start.4 = (f32[16,640]{1,0:T(8,128)S(1)}, f32[16,640]{1,0:T(8,128)S(1)}, u32[]{:S(2)}, u32[]{:S(2)}) collective-permute-start(f32[16,640]{1,0:T(8,128)S(1)} %collective-permute-done.3), channel_id=1, source_target_pairs={{0,9},{1,8},{2,11},{3,10},{4,13},{5,12},{6,15},{7,14},{8,1},{9,0},... | collective-permute-start | bytes 122888 | tf_op jit(solution)/shard_map/ppermute | solution.py:32
  20.0 0.4 %collective-permute-start.7 = (f32[16,640]{1,0:T(8,128)S(1)}, f32[16,640]{1,0:T(8,128)S(1)}, u32[]{:S(2)}, u32[]{:S(2)}) collective-permute-start(f32[16,640]{1,0:T(8,128)S(1)} %get-tuple-element.24), channel_id=1, source_target_pairs={{0,9},{1,8},{2,11},{3,10},{4,13},{5,12},{6,15},{7,14},{8,1},{9,0},... | collective-permute-start | bytes 122888 | tf_op jit(solution)/shard_map/ppermute | solution.py:32
  20.4 0.7 %leaf.3.refs_0_ = bf16[1088,512]{1,0:T(8,128)(2,1)S(1)} custom-call(s32[8,128]{1,0:T(8,128)S(1)} %get-tuple-element.13.perm_ref, bf16[1024,512]{1,0:T(8,128)(2,1)S(1)} %copy-done.1, bf16[1,32,1024]{2,1,0:T(8,128)(2,1)S(1)} %get-tuple-element.14.v_close_ref), custom_call_target="tpu_custom_call" | custom-call | flops 536870912 | bytes 2097152 | tf_op jit(solution)/shard_map/leaf/pallas_call | solution.py:331
  21.1 0.9 %collective-permute-done.4 = f32[16,640]{1,0:T(8,128)S(1)} collective-permute-done((f32[16,640]{1,0:T(8,128)S(1)}, f32[16,640]{1,0:T(8,128)S(1)}, u32[]{:S(2)}, u32[]{:S(2)}) %collective-permute-start.4) | collective-permute-done | bytes 40992 | tf_op jit(solution)/shard_map/ppermute | solution.py:32
  22.0 1.5 %collective-permute-done.7 = f32[16,640]{1,0:T(8,128)S(1)} collective-permute-done((f32[16,640]{1,0:T(8,128)S(1)}, f32[16,640]{1,0:T(8,128)S(1)}, u32[]{:S(2)}, u32[]{:S(2)}) %collective-permute-start.7) | collective-permute-done | bytes 40992 | tf_op jit(solution)/shard_map/ppermute | solution.py:32
  23.5 0.7 %collective-permute-start.8 = (f32[64,640]{1,0:T(8,128)S(1)}, f32[64,640]{1,0:T(8,128)S(1)}, u32[]{:S(2)}, u32[]{:S(2)}) collective-permute-start(f32[64,640]{1,0:T(8,128)S(1)} %pad_maximum_fusion.mine_ref), channel_id=1, source_target_pairs={{0,1},{1,0},{2,3},{3,2},{4,5},{5,4},{6,7},{7,6},{8,9},{9,8},{10,11... | collective-permute-start | bytes 491528 | tf_op jit(solution)/shard_map/ppermute | solution.py:27
  24.1 0.7 %order.3.refs_2_ = bf16[256,640]{1,0:T(8,128)(2,1)S(1)} custom-call(s32[8,128]{1,0:T(8,128)S(1)} %get-tuple-element.13.perm_ref, bf16[1024,640]{1,0:T(8,128)(2,1)S(1)} %copy-done), custom_call_target="tpu_custom_call" | custom-call | flops 335544320 | bytes 2097152 | tf_op jit(solution)/shard_map/order/pallas_call | solution.py:318
  24.8 0.8 %basis.1.u_far_ref = bf16[1024,224]{1,0:T(8,128)(2,1)S(1)} custom-call(s32[8,128]{1,0:T(8,128)S(1)} %get-tuple-element.13.perm_ref, bf16[6,32,1024]{2,1,0:T(8,128)(2,1)S(1)} %get-tuple-element.15.u_ref), custom_call_target="tpu_custom_call" | custom-call | flops 335544320 | bytes 3145728 | tf_op jit(solution)/shard_map/basis/pallas_call | solution.py:301
  25.6 1.0 %near.2.refs_2_ = f32[1088,640]{1,0:T(8,128)S(1)} custom-call(bf16[1088,512]{1,0:T(8,128)(2,1)S(1)} %leaf.3.refs_0_, bf16[768,640]{1,0:T(8,128)(2,1)S(1)} %order.2.refs_1_, bf16[256,640]{1,0:T(8,128)(2,1)S(1)} %order.3.refs_2_), custom_call_target="tpu_custom_call" | custom-call | flops 671088640 | bytes 6291456 | tf_op jit(solution)/shard_map/near/pallas_call | solution.py:352
  26.6 1.1 %near.3.near_ref = f32[1088,640]{1,0:T(8,128)S(1)} custom-call(bf16[1088,512]{1,0:T(8,128)(2,1)S(1)} %leaf.2.refs_0_, bf16[768,640]{1,0:T(8,128)(2,1)S(1)} %order.2.refs_1_, f32[1088,640]{1,0:T(8,128)S(1)} %near.2.refs_2_), custom_call_target="tpu_custom_call", output_to_operand_aliasing={{}: (2, {})} | custom-call | flops 671088640 | bytes 6291456 | tf_op jit(solution)/shard_map/near/pallas_call | solution.py:352
  27.7 1.4 %far.1 = bf16[1024,640]{1,0:T(8,128)(2,1)} custom-call(f32[1088,640]{1,0:T(8,128)S(1)} %near.3.near_ref, bf16[1024,224]{1,0:T(8,128)(2,1)S(1)} %basis.1.u_far_ref, f32[64,640]{1,0:T(8,128)S(1)} %pad_maximum_fusion.mine_ref, f32[64,640]{1,0:T(8,128)S(1)} %collective-permute-done.8.other_ref, bf16[16,640]{1,0:T(8,128)(2,1)S(1)} %round.2.sibling_0_ref, ...), custom_call_target="tpu_custom_call" | custom-call | flops 209715200 | bytes 5242880 | tf_op jit(solution)/shard_map/far/pallas_call | solution.py:380
  (19 shorter events, 0.1 us)
Async XLA Ops:
  0.0 12.5 %copy-start = (bf16[1024,640]{1,0:T(8,128)(2,1)S(1)}, bf16[1024,640]{1,0:T(8,128)(2,1)}, u32[]{:S(2)}) copy-start(bf16[1024,640]{1,0:T(8,128)(2,1)} %sources_ref.3) | copy-start | bytes 3932164
  2.1 1.7 %collective-permute-start = (f32[96,640]{1,0:T(8,128)S(1)}, f32[96,640]{1,0:T(8,128)S(1)}, u32[]{:S(2)}, u32[]{:S(2)}) collective-permute-start(f32[96,640]{1,0:T(8,128)S(1)} %get-tuple-element.17), channel_id=1, source_target_pairs={{0,1},{1,0},{2,3},{3,2},{4,5},{5,4},{6,7},{7,6},{8,9},{9,8},{10,11... | collective-permute-start | bytes 737288 | tf_op jit(solution)/shard_map/ppermute | solution.py:27
  3.9 4.4 %collective-permute-start.1 = (f32[16,640]{1,0:T(8,128)S(1)}, f32[16,640]{1,0:T(8,128)S(1)}, u32[]{:S(2)}, u32[]{:S(2)}) collective-permute-start(f32[16,640]{1,0:T(8,128)S(1)} %slice.52), channel_id=1, source_target_pairs={{0,5},{1,2},{2,1},{3,6},{4,7},{5,0},{6,3},{7,4},{8,11},{9,12},{10,... | collective-permute-start | bytes 122888 | tf_op jit(solution)/shard_map/ppermute | solution.py:32
  6.5 4.4 %collective-permute-start.5 = (f32[48,640]{1,0:T(8,128)S(1)}, f32[48,640]{1,0:T(8,128)S(1)}, u32[]{:S(2)}, u32[]{:S(2)}) collective-permute-start(f32[48,640]{1,0:T(8,128)S(1)} %slice.54), channel_id=1, source_target_pairs={{0,5},{1,2},{2,1},{3,6},{4,7},{5,0},{6,3},{7,4},{8,11},{9,12},{10,... | collective-permute-start | bytes 368648 | tf_op jit(solution)/shard_map/ppermute | solution.py:32
  8.2 5.8 %collective-permute-start.2 = (f32[16,640]{1,0:T(8,128)S(1)}, f32[16,640]{1,0:T(8,128)S(1)}, u32[]{:S(2)}, u32[]{:S(2)}) collective-permute-start(f32[16,640]{1,0:T(8,128)S(1)} %slice_add_fusion.3), channel_id=1, source_target_pairs={{0,3},{1,4},{2,7},{3,0},{4,1},{5,6},{6,5},{7,2},{8,13},{9,10},{10,... | collective-permute-start | bytes 122888 | tf_op jit(solution)/shard_map/ppermute | solution.py:32
  11.0 9.0 %collective-permute-start.6 = (f32[48,640]{1,0:T(8,128)S(1)}, f32[48,640]{1,0:T(8,128)S(1)}, u32[]{:S(2)}, u32[]{:S(2)}) collective-permute-start(f32[48,640]{1,0:T(8,128)S(1)} %pad_maximum_fusion.1), channel_id=1, source_target_pairs={{0,3},{1,4},{2,7},{3,0},{4,1},{5,6},{6,5},{7,2},{8,13},{9,10},{10,... | collective-permute-start | bytes 368648 | tf_op jit(solution)/shard_map/ppermute | solution.py:32
  12.5 3.9 %copy-start.1 = (bf16[1024,512]{1,0:T(8,128)(2,1)S(1)}, bf16[1024,512]{1,0:T(8,128)(2,1)}, u32[]{:S(2)}) copy-start(bf16[1024,512]{1,0:T(8,128)(2,1)} %block_ref.3) | copy-start | bytes 3145732
  14.0 4.5 %collective-permute-start.3 = (f32[16,640]{1,0:T(8,128)S(1)}, f32[16,640]{1,0:T(8,128)S(1)}, u32[]{:S(2)}, u32[]{:S(2)}) collective-permute-start(f32[16,640]{1,0:T(8,128)S(1)} %add.29), channel_id=1, source_target_pairs={{0,17},{1,16},{2,19},{3,18},{4,21},{5,20},{6,23},{7,22},{8,25},{9,... | collective-permute-start | bytes 122888 | tf_op jit(solution)/shard_map/ppermute | solution.py:32
  18.5 3.4 %collective-permute-start.4 = (f32[16,640]{1,0:T(8,128)S(1)}, f32[16,640]{1,0:T(8,128)S(1)}, u32[]{:S(2)}, u32[]{:S(2)}) collective-permute-start(f32[16,640]{1,0:T(8,128)S(1)} %collective-permute-done.3), channel_id=1, source_target_pairs={{0,9},{1,8},{2,11},{3,10},{4,13},{5,12},{6,15},{7,14},{8,1},{9,0},... | collective-permute-start | bytes 122888 | tf_op jit(solution)/shard_map/ppermute | solution.py:32
  20.0 3.5 %collective-permute-start.7 = (f32[16,640]{1,0:T(8,128)S(1)}, f32[16,640]{1,0:T(8,128)S(1)}, u32[]{:S(2)}, u32[]{:S(2)}) collective-permute-start(f32[16,640]{1,0:T(8,128)S(1)} %get-tuple-element.24), channel_id=1, source_target_pairs={{0,9},{1,8},{2,11},{3,10},{4,13},{5,12},{6,15},{7,14},{8,1},{9,0},... | collective-permute-start | bytes 122888 | tf_op jit(solution)/shard_map/ppermute | solution.py:32
  23.5 4.3 %collective-permute-start.8 = (f32[64,640]{1,0:T(8,128)S(1)}, f32[64,640]{1,0:T(8,128)S(1)}, u32[]{:S(2)}, u32[]{:S(2)}) collective-permute-start(f32[64,640]{1,0:T(8,128)S(1)} %pad_maximum_fusion.mine_ref), channel_id=1, source_target_pairs={{0,1},{1,0},{2,3},{3,2},{4,5},{5,4},{6,7},{7,6},{8,9},{9,8},{10,11... | collective-permute-start | bytes 491528 | tf_op jit(solution)/shard_map/ppermute | solution.py:27

commit v7 on v6

--- a/solution.py
+++ b/solution.py
@@ -310,8 +310,7 @@
     )(perm, u_in)
 
     leaves = row_count // leaf_size
-    cut = row_count * 3 // 4
-    pieces = [(0, cut), (cut, row_count)]
+    pieces = [(0, row_count)]
     ordered, left = [], []
     for start, stop in pieces:
         ordered.append(
@@ -376,7 +375,7 @@
             )(received)
         )
 
-    block = row_count // 8
+    block = row_count // 4
     return pl.pallas_call(
         functools.partial(far_kernel, block),
         out_shape=like((row_count, rhs_count), BF16),

time: 29.3 us -> 28.7 us (0.980)
  waiting for transfers between devices: 7.14 us -> 6.48 us
  starting transfers between devices: 11.7 us -> 12.1 us
  Pallas kernels: 10 us -> 9.65 us
    ppermute x7, starting transfers between devices: 10.5 us -> 11.4 us  [chip_swap(): return lax.ppermute(x, AXES, pairs)]
    ppermute x7, waiting for transfers between devices: 6 us -> 5.34 us  [chip_swap(): return lax.ppermute(x, AXES, pairs)]
    ppermute x2, starting transfers between devices: 1.21 us -> 0.74 us  [core_swap(): return lax.ppermute(x, AXES, [(i, i ^ 1) for i in range(1 << dev_bits)])]
    pallas_call x2 -> x1, Pallas kernels: 2.17 us -> 1.9 us  [per_device(): pl.pallas_call(functools.partial(order_kernel, start, stop), out_shape=li...]
  transfers between devices with their start and end apart: 9 -> 9, of which waited for: 6 -> 5; matrix products, arithmetic and copies ran while one was open for 0% -> 0% of each run, Pallas kernels for 22% -> 22%
where the time goes in v7:
time: 28.7 us; the launch traced here: 28.5 us
  starting transfers between devices  12.1 us (42%)
  Pallas kernels  9.65 us (34%)
  waiting for transfers between devices  6.48 us (23%)
    ppermute x7, starting transfers between devices, chip_swap(): return lax.ppermute(x, AXES, pairs)  11.4 us
    ppermute x7, waiting for transfers between devices, chip_swap(): return lax.ppermute(x, AXES, pairs)  5.34 us
    pallas_call x2, Pallas kernels, per_device(): pl.pallas_call(functools.partial(near_kernel, leaf, [pieces[number] for n...  2.11 us
    pallas_call x1, Pallas kernels, per_device(): pl.pallas_call(functools.partial(coef_kernel, dev_bits), out_shape=(like(...  2 us
    pallas_call x1, Pallas kernels, per_device(): pl.pallas_call(functools.partial(order_kernel, start, stop), out_shape=li...  1.9 us
    pallas_call x2, Pallas kernels, per_device(): pl.pallas_call(functools.partial(leaf_kernel, leaf), out_shape=like((row_...  1.45 us
    pallas_call x1, Pallas kernels, per_device(): pl.pallas_call(functools.partial(far_kernel, block), out_shape=like((row_...  1.42 us
    ppermute x2, waiting for transfers between devices, core_swap(): return lax.ppermute(x, AXES, [(i, i ^ 1) for i in range(1 << dev_bits)])  1.14 us
  transfers between devices with their start and end apart: 9, of which 5 were waited for; matrix products, arithmetic and copies ran while one was open for 0% of the time, Pallas kernels for 22%

profile of v7, /device:TPU:0, one launch (start us, length us, event | category | flops | bytes accessed | tf_op | source)
XLA Modules:
  0.0 28.5 jit_solution(11106474457703339393)
XLA Ops:
  0.0 2.0 %coef.1 = (f32[96,640]{1,0:T(8,128)S(1)}, f32[64,640]{1,0:T(8,128)S(1)}, bf16[1,32,1024]{2,1,0:T(8,128)(2,1)S(1)}, s32[8,128]{1,0:T(8,128)S(1)}, bf16[6,32,1024]{2,1,0:T(8,128)(2,1)S(1)}) custom-call(s32[6]{0:T(128)} %ranks_hbm.1, s32[8,128]{1,0:T(8,128)} %bitcast.1, bf16[6,32,1024]{2,1,0:T(8,128)(2,1)} %v_hbm.1, bf16[1024,640]{1,0:T(8,128)(2,1)} %sources_ref.1, ...), custom_call_target="tpu_custom_call" | custom-call | flops 545259520 | bytes 2097152 | tf_op jit(solution)/shard_map/coef/pallas_call | solution.py:277
  2.0 0.0 copy-start.1
  2.0 0.6 %collective-permute-start = (f32[96,640]{1,0:T(8,128)S(1)}, f32[96,640]{1,0:T(8,128)S(1)}, u32[]{:S(2)}, u32[]{:S(2)}) collective-permute-start(f32[96,640]{1,0:T(8,128)S(1)} %get-tuple-element.17), channel_id=1, source_target_pairs={{0,1},{1,0},{2,3},{3,2},{4,5},{5,4},{6,7},{7,6},{8,9},{9,8},{10,11... | collective-permute-start | bytes 737288 | tf_op jit(solution)/shard_map/ppermute | solution.py:27
  2.6 1.1 %collective-permute-done.coef_ref = f32[96,640]{1,0:T(8,128)S(1)} collective-permute-done((f32[96,640]{1,0:T(8,128)S(1)}, f32[96,640]{1,0:T(8,128)S(1)}, u32[]{:S(2)}, u32[]{:S(2)}) %collective-permute-start) | collective-permute-done | bytes 245792 | tf_op jit(solution)/shard_map/ppermute | solution.py:27
  3.8 2.7 %collective-permute-start.1 = (f32[16,640]{1,0:T(8,128)S(1)}, f32[16,640]{1,0:T(8,128)S(1)}, u32[]{:S(2)}, u32[]{:S(2)}) collective-permute-start(f32[16,640]{1,0:T(8,128)S(1)} %slice.52), channel_id=1, source_target_pairs={{0,5},{1,2},{2,1},{3,6},{4,7},{5,0},{6,3},{7,4},{8,11},{9,12},{10,... | collective-permute-start | bytes 122888 | tf_op jit(solution)/shard_map/ppermute | solution.py:32
  6.4 0.1 collective-permute-start.5
  6.5 1.6 %collective-permute-done.1 = f32[16,640]{1,0:T(8,128)S(1)} collective-permute-done((f32[16,640]{1,0:T(8,128)S(1)}, f32[16,640]{1,0:T(8,128)S(1)}, u32[]{:S(2)}, u32[]{:S(2)}) %collective-permute-start.1) | collective-permute-done | bytes 40992 | tf_op jit(solution)/shard_map/ppermute | solution.py:32
  8.1 2.0 %collective-permute-start.2 = (f32[16,640]{1,0:T(8,128)S(1)}, f32[16,640]{1,0:T(8,128)S(1)}, u32[]{:S(2)}, u32[]{:S(2)}) collective-permute-start(f32[16,640]{1,0:T(8,128)S(1)} %slice_add_fusion.3), channel_id=1, source_target_pairs={{0,3},{1,4},{2,7},{3,0},{4,1},{5,6},{6,5},{7,2},{8,13},{9,10},{10,... | collective-permute-start | bytes 122888 | tf_op jit(solution)/shard_map/ppermute | solution.py:32
  10.1 1.7 %collective-permute-done.2 = f32[16,640]{1,0:T(8,128)S(1)} collective-permute-done((f32[16,640]{1,0:T(8,128)S(1)}, f32[16,640]{1,0:T(8,128)S(1)}, u32[]{:S(2)}, u32[]{:S(2)}) %collective-permute-start.2) | collective-permute-done | bytes 40992 | tf_op jit(solution)/shard_map/ppermute | solution.py:32
  11.8 2.5 %collective-permute-start.3 = (f32[16,640]{1,0:T(8,128)S(1)}, f32[16,640]{1,0:T(8,128)S(1)}, u32[]{:S(2)}, u32[]{:S(2)}) collective-permute-start(f32[16,640]{1,0:T(8,128)S(1)} %add.29), channel_id=1, source_target_pairs={{0,17},{1,16},{2,19},{3,18},{4,21},{5,20},{6,23},{7,22},{8,25},{9,... | collective-permute-start | bytes 122888 | tf_op jit(solution)/shard_map/ppermute | solution.py:32
  14.4 1.5 %collective-permute-start.6 = (f32[48,640]{1,0:T(8,128)S(1)}, f32[48,640]{1,0:T(8,128)S(1)}, u32[]{:S(2)}, u32[]{:S(2)}) collective-permute-start(f32[48,640]{1,0:T(8,128)S(1)} %pad_maximum_fusion.1), channel_id=1, source_target_pairs={{0,3},{1,4},{2,7},{3,0},{4,1},{5,6},{6,5},{7,2},{8,13},{9,10},{10,... | collective-permute-start | bytes 368648 | tf_op jit(solution)/shard_map/ppermute | solution.py:32
  16.0 1.9 %order.1.refs_1_ = bf16[1024,640]{1,0:T(8,128)(2,1)S(1)} custom-call(s32[8,128]{1,0:T(8,128)S(1)} %get-tuple-element.13.perm_ref, bf16[1024,640]{1,0:T(8,128)(2,1)S(1)} %copy-done.1), custom_call_target="tpu_custom_call" | custom-call | flops 1342177280 | bytes 2097152 | tf_op jit(solution)/shard_map/order/pallas_call | solution.py:317
  17.9 0.0 collective-permute-done.3
  17.9 1.7 %collective-permute-start.4 = (f32[16,640]{1,0:T(8,128)S(1)}, f32[16,640]{1,0:T(8,128)S(1)}, u32[]{:S(2)}, u32[]{:S(2)}) collective-permute-start(f32[16,640]{1,0:T(8,128)S(1)} %collective-permute-done.3), channel_id=1, source_target_pairs={{0,9},{1,8},{2,11},{3,10},{4,13},{5,12},{6,15},{7,14},{8,1},{9,0},... | collective-permute-start | bytes 122888 | tf_op jit(solution)/shard_map/ppermute | solution.py:32
  19.6 0.8 %collective-permute-start.7 = (f32[16,640]{1,0:T(8,128)S(1)}, f32[16,640]{1,0:T(8,128)S(1)}, u32[]{:S(2)}, u32[]{:S(2)}) collective-permute-start(f32[16,640]{1,0:T(8,128)S(1)} %get-tuple-element.24), channel_id=1, source_target_pairs={{0,9},{1,8},{2,11},{3,10},{4,13},{5,12},{6,15},{7,14},{8,1},{9,0},... | collective-permute-start | bytes 122888 | tf_op jit(solution)/shard_map/ppermute | solution.py:32
  20.4 0.7 %leaf.2.refs_0_ = bf16[1088,512]{1,0:T(8,128)(2,1)S(1)} custom-call(s32[8,128]{1,0:T(8,128)S(1)} %get-tuple-element.13.perm_ref, bf16[1024,512]{1,0:T(8,128)(2,1)S(1)} %copy-done, bf16[1,32,1024]{2,1,0:T(8,128)(2,1)S(1)} %get-tuple-element.14.v_close_ref), custom_call_target="tpu_custom_call" | custom-call | flops 536870912 | bytes 2097152 | tf_op jit(solution)/shard_map/leaf/pallas_call | solution.py:330
  21.2 0.2 collective-permute-done.4
  21.4 1.9 %collective-permute-done.7 = f32[16,640]{1,0:T(8,128)S(1)} collective-permute-done((f32[16,640]{1,0:T(8,128)S(1)}, f32[16,640]{1,0:T(8,128)S(1)}, u32[]{:S(2)}, u32[]{:S(2)}) %collective-permute-start.7) | collective-permute-done | bytes 40992 | tf_op jit(solution)/shard_map/ppermute | solution.py:32
  23.2 0.2 collective-permute-start.8
  23.4 0.7 %leaf.3.refs_0_ = bf16[1088,512]{1,0:T(8,128)(2,1)S(1)} custom-call(s32[8,128]{1,0:T(8,128)S(1)} %get-tuple-element.13.perm_ref, bf16[1024,512]{1,0:T(8,128)(2,1)S(1)} %copy-done, bf16[1,32,1024]{2,1,0:T(8,128)(2,1)S(1)} %get-tuple-element.14.v_close_ref), custom_call_target="tpu_custom_call" | custom-call | flops 536870912 | bytes 2097152 | tf_op jit(solution)/shard_map/leaf/pallas_call | solution.py:330
  24.2 0.8 %basis.1.u_far_ref = bf16[1024,224]{1,0:T(8,128)(2,1)S(1)} custom-call(s32[8,128]{1,0:T(8,128)S(1)} %get-tuple-element.13.perm_ref, bf16[6,32,1024]{2,1,0:T(8,128)(2,1)S(1)} %get-tuple-element.15.u_ref), custom_call_target="tpu_custom_call" | custom-call | flops 335544320 | bytes 3145728 | tf_op jit(solution)/shard_map/basis/pallas_call | solution.py:301
  24.9 1.0 %near.2.refs_2_ = f32[1088,640]{1,0:T(8,128)S(1)} custom-call(bf16[1088,512]{1,0:T(8,128)(2,1)S(1)} %leaf.3.refs_0_, bf16[1024,640]{1,0:T(8,128)(2,1)S(1)} %order.1.refs_1_), custom_call_target="tpu_custom_call" | custom-call | flops 671088640 | bytes 6291456 | tf_op jit(solution)/shard_map/near/pallas_call | solution.py:351
  26.0 1.1 %near.3.near_ref = f32[1088,640]{1,0:T(8,128)S(1)} custom-call(bf16[1088,512]{1,0:T(8,128)(2,1)S(1)} %leaf.2.refs_0_, bf16[1024,640]{1,0:T(8,128)(2,1)S(1)} %order.1.refs_1_, f32[1088,640]{1,0:T(8,128)S(1)} %near.2.refs_2_), custom_call_target="tpu_custom_call", output_to_operand_aliasing={{}: (2, {})} | custom-call | flops 671088640 | bytes 6291456 | tf_op jit(solution)/shard_map/near/pallas_call | solution.py:351
  27.1 1.4 %far.1 = bf16[1024,640]{1,0:T(8,128)(2,1)} custom-call(f32[1088,640]{1,0:T(8,128)S(1)} %near.3.near_ref, bf16[1024,224]{1,0:T(8,128)(2,1)S(1)} %basis.1.u_far_ref, f32[64,640]{1,0:T(8,128)S(1)} %pad_maximum_fusion.mine_ref, f32[64,640]{1,0:T(8,128)S(1)} %collective-permute-done.8.other_ref, bf16[16,640]{1,0:T(8,128)(2,1)S(1)} %round.2.sibling_0_ref, ...), custom_call_target="tpu_custom_call" | custom-call | flops 209715200 | bytes 5242880 | tf_op jit(solution)/shard_map/far/pallas_call | solution.py:379
  (18 shorter events, 0.1 us)
Async XLA Ops:
  2.0 13.9 %copy-start.1 = (bf16[1024,640]{1,0:T(8,128)(2,1)S(1)}, bf16[1024,640]{1,0:T(8,128)(2,1)}, u32[]{:S(2)}) copy-start(bf16[1024,640]{1,0:T(8,128)(2,1)} %sources_ref.1) | copy-start | bytes 3932164
  2.0 1.7 %collective-permute-start = (f32[96,640]{1,0:T(8,128)S(1)}, f32[96,640]{1,0:T(8,128)S(1)}, u32[]{:S(2)}, u32[]{:S(2)}) collective-permute-start(f32[96,640]{1,0:T(8,128)S(1)} %get-tuple-element.17), channel_id=1, source_target_pairs={{0,1},{1,0},{2,3},{3,2},{4,5},{5,4},{6,7},{7,6},{8,9},{9,8},{10,11... | collective-permute-start | bytes 737288 | tf_op jit(solution)/shard_map/ppermute | solution.py:27
  3.8 4.4 %collective-permute-start.1 = (f32[16,640]{1,0:T(8,128)S(1)}, f32[16,640]{1,0:T(8,128)S(1)}, u32[]{:S(2)}, u32[]{:S(2)}) collective-permute-start(f32[16,640]{1,0:T(8,128)S(1)} %slice.52), channel_id=1, source_target_pairs={{0,5},{1,2},{2,1},{3,6},{4,7},{5,0},{6,3},{7,4},{8,11},{9,12},{10,... | collective-permute-start | bytes 122888 | tf_op jit(solution)/shard_map/ppermute | solution.py:32
  6.4 7.9 %collective-permute-start.5 = (f32[48,640]{1,0:T(8,128)S(1)}, f32[48,640]{1,0:T(8,128)S(1)}, u32[]{:S(2)}, u32[]{:S(2)}) collective-permute-start(f32[48,640]{1,0:T(8,128)S(1)} %slice.54), channel_id=1, source_target_pairs={{0,5},{1,2},{2,1},{3,6},{4,7},{5,0},{6,3},{7,4},{8,11},{9,12},{10,... | collective-permute-start | bytes 368648 | tf_op jit(solution)/shard_map/ppermute | solution.py:32
  8.1 3.7 %collective-permute-start.2 = (f32[16,640]{1,0:T(8,128)S(1)}, f32[16,640]{1,0:T(8,128)S(1)}, u32[]{:S(2)}, u32[]{:S(2)}) collective-permute-start(f32[16,640]{1,0:T(8,128)S(1)} %slice_add_fusion.3), channel_id=1, source_target_pairs={{0,3},{1,4},{2,7},{3,0},{4,1},{5,6},{6,5},{7,2},{8,13},{9,10},{10,... | collective-permute-start | bytes 122888 | tf_op jit(solution)/shard_map/ppermute | solution.py:32
  11.8 6.0 %collective-permute-start.3 = (f32[16,640]{1,0:T(8,128)S(1)}, f32[16,640]{1,0:T(8,128)S(1)}, u32[]{:S(2)}, u32[]{:S(2)}) collective-permute-start(f32[16,640]{1,0:T(8,128)S(1)} %add.29), channel_id=1, source_target_pairs={{0,17},{1,16},{2,19},{3,18},{4,21},{5,20},{6,23},{7,22},{8,25},{9,... | collective-permute-start | bytes 122888 | tf_op jit(solution)/shard_map/ppermute | solution.py:32
  14.4 5.1 %collective-permute-start.6 = (f32[48,640]{1,0:T(8,128)S(1)}, f32[48,640]{1,0:T(8,128)S(1)}, u32[]{:S(2)}, u32[]{:S(2)}) collective-permute-start(f32[48,640]{1,0:T(8,128)S(1)} %pad_maximum_fusion.1), channel_id=1, source_target_pairs={{0,3},{1,4},{2,7},{3,0},{4,1},{5,6},{6,5},{7,2},{8,13},{9,10},{10,... | collective-permute-start | bytes 368648 | tf_op jit(solution)/shard_map/ppermute | solution.py:32
  16.0 4.5 %copy-start = (bf16[1024,512]{1,0:T(8,128)(2,1)S(1)}, bf16[1024,512]{1,0:T(8,128)(2,1)}, u32[]{:S(2)}) copy-start(bf16[1024,512]{1,0:T(8,128)(2,1)} %block_ref.3) | copy-start | bytes 3145732
  17.9 3.5 %collective-permute-start.4 = (f32[16,640]{1,0:T(8,128)S(1)}, f32[16,640]{1,0:T(8,128)S(1)}, u32[]{:S(2)}, u32[]{:S(2)}) collective-permute-start(f32[16,640]{1,0:T(8,128)S(1)} %collective-permute-done.3), channel_id=1, source_target_pairs={{0,9},{1,8},{2,11},{3,10},{4,13},{5,12},{6,15},{7,14},{8,1},{9,0},... | collective-permute-start | bytes 122888 | tf_op jit(solution)/shard_map/ppermute | solution.py:32
  19.6 3.6 %collective-permute-start.7 = (f32[16,640]{1,0:T(8,128)S(1)}, f32[16,640]{1,0:T(8,128)S(1)}, u32[]{:S(2)}, u32[]{:S(2)}) collective-permute-start(f32[16,640]{1,0:T(8,128)S(1)} %get-tuple-element.24), channel_id=1, source_target_pairs={{0,9},{1,8},{2,11},{3,10},{4,13},{5,12},{6,15},{7,14},{8,1},{9,0},... | collective-permute-start | bytes 122888 | tf_op jit(solution)/shard_map/ppermute | solution.py:32
  23.2 3.8 %collective-permute-start.8 = (f32[64,640]{1,0:T(8,128)S(1)}, f32[64,640]{1,0:T(8,128)S(1)}, u32[]{:S(2)}, u32[]{:S(2)}) collective-permute-start(f32[64,640]{1,0:T(8,128)S(1)} %pad_maximum_fusion.mine_ref), channel_id=1, source_target_pairs={{0,1},{1,0},{2,3},{3,2},{4,5},{5,4},{6,7},{7,6},{8,9},{9,8},{10,11... | collective-permute-start | bytes 491528 | tf_op jit(solution)/shard_map/ppermute | solution.py:27
